TPU v7x, 512 devices: a whole 4x4x16 slice. The times are simulated.
512 devices in a mesh: seq: 128 (over z_lo, y, x), tp: 4 (over z_hi, core).
Axes of the slice: x: 4, y: 4, z: 16 (z_hi: 2, z_lo: 8; z = z_hi * 8 + z_lo), core: 2. Of those that a mesh axis runs over, the one named last changes fastest.
Arguments:
- inputs: bfloat16 [32768, 5120], P('seq', 'tp'), may hold values from -6 to 6
- gate_input: bfloat16 [32768, 5120], P('seq', 'tp'), may hold values from -6 to 6
- b_source: bfloat16 [32768, 128], P('seq'), may hold values from -6 to 6
- c_source: bfloat16 [32768, 128], P('seq'), may hold values from -6 to 6
- step_raw: float32 [32768, 80], P('seq', 'tp'), may hold values from -4 to 4
- step_bias: float32 [80], P('tp'), may hold values from -3 to 0
- decay_rate: float32 [80], P('tp'), may hold values from 6.1035157e-06 to 0.05
- conv_weight: float32 [4, 256], replicated, may hold values from -3 to 3
- conv_bias: float32 [256], replicated, may hold values from -3 to 3
- norm_gain: float32 [5120], P('tp'), may hold values from 0.5 to 1.5
- doc_lengths: int32 [8], replicated, may hold values from 1 to 16384, 32768 in all
Outputs:
- output: bfloat16 [32768, 5120], P('seq', 'tp')
Inputs may be any that keep to these rules, and one draw needn't show every extreme that they name: doc_lengths sums to 32768; every length is at least 1 and the largest is exactly 16384.
All inputs are finite; a program needn't handle non-finite values.
Results may differ from a plain program's by a relative error of at most 0.0015.
Values may be sent and summed in bfloat16 or wider, within the bound.
No kernel may reach another device: no remote copies, remote signals or barrier semaphores. Data moves between devices by JAX's collectives and lax.ppermute only.
A program may use at most 192 MiB of HBM per device.

v0:
```python
import jax
import jax.numpy as jnp
from jax import lax
from jax.sharding import Mesh
from jax.sharding import PartitionSpec as P

BLOCK = 256
SEQ = ("seq_0", "seq_1", "seq_2")


epsilon = 1e-05


def nothing_yet(array, identity):
    return jax.tree.map(
        lambda a, e: jnp.broadcast_to(jnp.asarray(e, a.dtype), a.shape), array, identity
    )


def carried_in(array, axes, combine, identity, reverse):
    before = start = nothing_yet(array, identity)
    so_far = array
    for axis in reversed(axes):
        size, place = lax.axis_size(axis), lax.axis_index(axis)
        pieces = jax.tree.map(lambda part: lax.all_gather(part, axis), so_far)
        inside, so_far = start, start
        for k in reversed(range(size)) if reverse else range(size):
            passed = k > place if reverse else k < place
            so_far = combine(so_far, jax.tree.map(lambda part: part[k], pieces))
            inside = jax.tree.map(lambda new, old: jnp.where(passed, new, old), so_far, inside)
        before = combine(inside, before)
    return before


def from_behind(value, axis, steps):
    count = lax.axis_size(axis)
    first, last = max(0, -steps), min(count, count - steps)
    return lax.ppermute(value, axis, [(source, source + steps) for source in range(first, last)])


def gathered_total(array, axis):
    parts = lax.all_gather(array, axis)
    return parts.sum(axis=0)


def locate(position, doc_lengths):
    starts = (jnp.cumsum(doc_lengths) - doc_lengths).astype(jnp.int32)
    chosen = jnp.where(starts[None, :] <= position[:, None], starts[None, :], 0)
    return jnp.max(chosen, axis=1).astype(jnp.int32)


def convolve(padded, weight, conv_bias, position, doc_start):
    kernel_taps = weight.shape[0]
    tokens = position.shape[0]
    widened = padded.astype(jnp.float32)
    summed = jnp.broadcast_to(conv_bias[None, :], (tokens, conv_bias.shape[0]))
    for offset in range(kernel_taps):
        backward = kernel_taps - 1 - offset
        inside = (position - backward >= doc_start)[:, None]
        summed = summed + jnp.where(
            inside, weight[offset][None, :] * widened[offset : offset + tokens], 0.0
        )
    return jax.nn.silu(summed).astype(jnp.bfloat16)


def state_terms(pieces):
    block_inputs, b_block, step_size, cumulated, doc_start, position = pieces
    same_doc = doc_start == doc_start[-1]
    weighting = jnp.where(
        same_doc[:, None], jnp.exp(cumulated[-1][None, :] - cumulated) * step_size, 0.0
    )
    weighted = (block_inputs.astype(jnp.float32) * weighting[:, :, None]).astype(jnp.bfloat16)
    end_state = jnp.einsum("qhp,qn->hpn", weighted, b_block, preferred_element_type=jnp.float32)
    end_factor = jnp.where(doc_start[-1] < position[0], jnp.exp(cumulated[-1]), 0.0)
    return (end_state, end_factor)


def diagonal_terms(pieces):
    block_inputs, b_block, c_block, step_size, cumulated, doc_start = pieces
    row_count = doc_start.shape[0]
    products = jnp.dot(c_block, b_block.T, preferred_element_type=jnp.float32)
    order_ids = jnp.arange(row_count)
    causal = (order_ids[None, :] <= order_ids[:, None]) & (doc_start[None, :] == doc_start[:, None])
    decay_gap = cumulated.T[:, :, None] - cumulated.T[:, None, :]
    scores = jnp.where(
        causal[None], products[None] * jnp.exp(decay_gap) * step_size.T[:, None, :], 0.0
    )
    return jnp.einsum(
        "hts,shp->thp",
        scores.astype(jnp.bfloat16),
        block_inputs,
        preferred_element_type=jnp.float32,
    )


def emit_rows(state_in, pieces):
    end_state, end_factor, c_block, out_decay = pieces
    from_state = jnp.einsum(
        "qn,hpn->qhp", c_block, state_in.astype(jnp.bfloat16), preferred_element_type=jnp.float32
    )
    from_state = from_state * out_decay[:, :, None]
    return (end_factor[:, None, None] * state_in + end_state, from_state)


def fold_local(carry_pair, pieces):
    factor, state_part = carry_pair
    end_state, end_factor = pieces
    return ((factor * end_factor, end_factor[:, None, None] * state_part + end_state), None)


def combine(earlier, later):
    return (earlier[0] * later[0], later[0][:, None, None] * earlier[1] + later[1])


def carried_state(device_factor, device_state):
    identity = (jnp.ones_like(device_factor), jnp.zeros_like(device_state))
    factor_in, state_in = carried_in((device_factor, device_state), SEQ, combine, identity, False)
    return state_in


def body(
    inputs,
    gate_input,
    b_source,
    c_source,
    step_raw,
    step_bias,
    decay_rate,
    conv_weight,
    conv_bias,
    norm_gain,
    doc_lengths,
):
    tokens = inputs.shape[0]
    head_count = step_raw.shape[1]
    head_width = inputs.shape[1] // head_count
    state_width = b_source.shape[1]
    keep_rows = conv_weight.shape[0] - 1
    block_count = tokens // BLOCK
    position = lax.axis_index(SEQ) * tokens + jnp.arange(tokens, dtype=jnp.int32)
    doc_start = locate(position, doc_lengths)
    b_before = from_behind(b_source[tokens - keep_rows :], SEQ, 1)
    c_before = from_behind(c_source[tokens - keep_rows :], SEQ, 1)
    b_conv = convolve(
        jnp.concatenate([b_before, b_source], 0),
        conv_weight[:, :state_width],
        conv_bias[:state_width],
        position,
        doc_start,
    )
    c_conv = convolve(
        jnp.concatenate([c_before, c_source], 0),
        conv_weight[:, state_width:],
        conv_bias[state_width:],
        position,
        doc_start,
    )
    step_size = jax.nn.softplus(step_raw + step_bias[None, :])
    log_decay = -step_size * decay_rate[None, :]
    shaped_inputs = inputs.reshape(block_count, BLOCK, head_count, head_width)
    b_blocks = b_conv.reshape(block_count, BLOCK, state_width)
    c_blocks = c_conv.reshape(block_count, BLOCK, state_width)
    step_blocks = step_size.reshape(block_count, BLOCK, head_count)
    cumulated = jnp.cumsum(log_decay.reshape(block_count, BLOCK, head_count), axis=1)
    start_blocks = doc_start.reshape(block_count, BLOCK)
    position_blocks = position.reshape(block_count, BLOCK)
    out_decay = jnp.where(
        (start_blocks < position_blocks[:, :1])[:, :, None], jnp.exp(cumulated), 0.0
    )
    end_states, end_factors = lax.map(
        state_terms,
        (shaped_inputs, b_blocks, step_blocks, cumulated, start_blocks, position_blocks),
    )
    start_pair = (
        jnp.ones((head_count,), jnp.float32),
        jnp.zeros((head_count, head_width, state_width), jnp.float32),
    )
    device_pair, unused = lax.scan(fold_local, start_pair, (end_states, end_factors))
    diag_pieces = (shaped_inputs, b_blocks, c_blocks, step_blocks, cumulated, start_blocks)
    state_in = carried_state(device_pair[0], device_pair[1])
    diagonal = lax.map(diagonal_terms, diag_pieces)
    final_state, from_state = lax.scan(
        emit_rows, state_in, (end_states, end_factors, c_blocks, out_decay)
    )
    mixed = (diagonal + from_state).reshape(tokens, head_count * head_width)
    gated = mixed * jax.nn.silu(gate_input.astype(jnp.float32))
    square_sums = gathered_total(jnp.sum(gated * gated, axis=1), "tp")
    mean_square = square_sums / (head_count * head_width * lax.axis_size("tp"))
    return (gated * lax.rsqrt(mean_square + epsilon)[:, None] * norm_gain[None, :]).astype(
        jnp.bfloat16
    )


def solution(mesh):
    finer = Mesh(mesh.devices.reshape(8, 4, 4, mesh.shape["tp"]), ("seq_0", "seq_1", "seq_2", "tp"))
    in_specs = (
        P(SEQ, "tp"),
        P(SEQ, "tp"),
        P(SEQ, None),
        P(SEQ, None),
        P(SEQ, "tp"),
        P("tp"),
        P("tp"),
        P(),
        P(),
        P("tp"),
        P(),
    )
    out_specs = P(SEQ, "tp")
    return jax.shard_map(body, mesh=finer, in_specs=in_specs, out_specs=out_specs, check_vma=False)
```

profile of v0, /device:TPU:1, one launch (start us, length us, event | category | flops | bytes accessed | tf_op | source)
XLA Modules:
  0.0 272.8 jit_solution(13329174135072824862)
XLA Ops:
  6.5 0.8 slice.203
  7.3 3.9 %collective-permute-start.1 = (bf16[3,128]{1,0:T(4,128)(2,1)S(1)}, bf16[3,128]{1,0:T(4,128)(2,1)S(1)}, u32[]{:S(2)}, u32[]{:S(2)}) collective-permute-start(bf16[3,128]{1,0:T(4,128)(2,1)S(1)} %slice.203), channel_id=1, source_target_pairs={{0,4},{4,8},{8,12},{12,16},{16,20},{20,24},{24,28},{28,32},{32,36}... | collective-permute-start | bytes 2312 | tf_op jit(solution)/shard_map/ppermute | solution.py:38
  11.2 0.8 multiply_bitcast_fusion
  12.1 0.6 reduce-window.20
  12.7 0.2 slice_reduce_fusion
  12.9 0.8 reduce-window.19
  13.7 0.7 bitcast_subtract_fusion
  14.4 0.5 slice.214
  14.9 0.1 select_reduce_fusion
  15.0 0.7 slice.213
  15.7 0.1 copy.33
  15.8 0.7 broadcast_compare_fusion.1
  17.7 0.9 slice_bitcast_fusion.19
  18.6 0.8 fusion.62
  19.4 0.1 broadcast.232
  19.5 0.3 broadcast_select_fusion.1
  19.8 0.9 fusion.55
  20.7 1.3 copy.35
  22.0 0.2 multiply_convert_fusion.3
  22.3 1.2 convolution_add_fusion
  23.5 0.0 all-gather.14.cloned.1.call-update
  23.5 0.0 all-gather.10.cloned.1.call-start
  23.6 0.1 copy.36
  23.6 7.7 %all-gather = f32[4,1,20]{2,1,0:T(1,128)S(1)} all-gather(f32[1,1,20]{2,1,0:T(1,128)S(1)} %copy.36), channel_id=2, replica_groups=mesh['seq_0'=8,'seq_1'=4,'seq_2'=4,'tp'=4] {'seq_2'}, dimensions={0}, use_global_device_ids=true | all-gather | bytes 400 | tf_op jit(solution)/shard_map/all_gather | solution.py:25
  31.4 8.0 %all-gather.3 = f32[4,1,20]{2,1,0:T(1,128)S(1)} all-gather(f32[1,1,20]{2,1,0:T(1,128)S(1)} %get-tuple-element.122), channel_id=1, replica_groups=mesh['seq_0'=8,'seq_1'=4,'seq_2'=4,'tp'=4] {'seq_1'}, dimensions={0}, use_global_device_ids=true | all-gather | bytes 400 | tf_op jit(solution)/shard_map/all_gather | solution.py:25
  39.3 31.2 %all-gather.14.cloned.1.call-done = f32[80,64,128]{2,1,0:T(8,128)} async-done(((f32[20,64,128]{2,1,0:T(8,128)}), f32[80,64,128]{2,1,0:T(8,128)}) %all-gather.14.cloned.1.call-update) | async-done | bytes 2621456 | tf_op jit(solution)/shard_map/all_gather | solution.py:25
  70.5 2.8 %bitcast_add_fusion.4 = f32[1,20,64,128]{3,2,1,0:T(8,128)} fusion(f32[80,64,128]{2,1,0:T(8,128)} %all-gather.14.cloned.1.call-done, f32[20]{0:T(128)S(1)} %get-tuple-element.120, f32[20]{0:T(128)S(1)} %get-tuple-element.125, f32[20]{0:T(128)S(1)} %get-tuple-element.124, f32[20]{0:T(128)S(1)} %get-tuple-element.123), kind=kLoop, calls=%fused_computation.48 | loop fusion | flops 1146880 | bytes 3277120 | tf_op jit(solution)/shard_map/add | solution.py:112
  73.3 0.0 all-gather.10.cloned.1.call-update
  73.3 0.0 all-gather.12.cloned.1.call-start
  73.4 43.0 %all-gather.10.cloned.1.call-done = f32[4,20,64,128]{3,2,1,0:T(8,128)} async-done(((f32[1,20,64,128]{3,2,1,0:T(8,128)}), f32[4,20,64,128]{3,2,1,0:T(8,128)}) %all-gather.10.cloned.1.call-update) | async-done | bytes 2621456 | tf_op jit(solution)/shard_map/all_gather | solution.py:25
  116.4 2.8 %multiply_add_fusion = f32[1,20,64,128]{3,2,1,0:T(8,128)} fusion(f32[4,20,64,128]{3,2,1,0:T(8,128)} %all-gather.10.cloned.1.call-done, f32[20]{0:T(128)S(1)} %get-tuple-element.121, f32[20]{0:T(128)S(1)} %get-tuple-element.118, f32[20]{0:T(128)S(1)} %get-tuple-element.116, f32[20]{0:T(128)S(1)} %get-tuple-element.108), kind=kLoop, calls=%fused_computation.55 | loop fusion | flops 1146880 | bytes 3277120 | tf_op jit(solution)/shard_map/add | solution.py:112
  119.2 0.0 all-gather.12.cloned.1.call-update
  119.2 3.1 %collective-permute-start = (bf16[3,128]{1,0:T(4,128)(2,1)S(1)}, bf16[3,128]{1,0:T(4,128)(2,1)S(1)}, u32[]{:S(2)}, u32[]{:S(2)}) collective-permute-start(bf16[3,128]{1,0:T(4,128)(2,1)S(1)} %slice.193), channel_id=1, source_target_pairs={{0,4},{4,8},{8,12},{12,16},{16,20},{20,24},{24,28},{28,32},{32,36}... | collective-permute-start | bytes 2312 | tf_op jit(solution)/shard_map/ppermute | solution.py:38
  122.3 29.6 %all-gather.4 = f32[8,1,20]{2,1,0:T(1,128)S(1)} all-gather(f32[1,1,20]{2,1,0:T(1,128)S(1)} %get-tuple-element.107), channel_id=1, replica_groups=mesh['seq_0'=8,'seq_1'=4,'seq_2'=4,'tp'=4] {'seq_0'}, dimensions={0}, use_global_device_ids=true | all-gather | bytes 720 | tf_op jit(solution)/shard_map/all_gather | solution.py:25
  151.9 0.1 copy.37
  152.0 0.1 fusion.33
  152.1 0.2 multiply_reduce_fusion.1
  152.4 0.2 multiply_convert_fusion.4
  152.6 0.2 fusion.63
  152.8 2.5 fusion.7
  155.4 85.7 %all-gather.12.cloned.1.call-done = f32[8,20,64,128]{3,2,1,0:T(8,128)} async-done(((f32[1,20,64,128]{3,2,1,0:T(8,128)}), f32[8,20,64,128]{3,2,1,0:T(8,128)}) %all-gather.12.cloned.1.call-update) | async-done | bytes 5242896 | tf_op jit(solution)/shard_map/all_gather | solution.py:25
  241.0 5.9 %fusion.8 = f32[256,20,64]{0,2,1:T(8,128)S(1)} fusion(f32[256,20,64]{0,2,1:T(8,128)} %fusion.7, f32[256,20]{0,1:T(8,128)S(1)} %get-tuple-element.135, f32[8,20,64,128]{3,2,1,0:T(8,128)} %all-gather.12.cloned.1.call-done, f32[4,20,64,128]{3,2,1,0:T(8,128)} %all-gather.10.cloned.1.call-done, f32[80,64,128]{2,1,0:T(8,128)} %all-gather.14.cloned.1.call-done, ...), kind=kOutput, calls=%fused_computation.12 | convolution fusion | flops 92733440 | bytes 13194672 | tf_op jit(solution)/shard_map/while/body/eval_jaxpr/qn,hpn->qhp/dot_general | solution.py:98
  246.9 0.0 copy-start
  246.9 0.4 copy.38
  247.3 0.7 copy-done
  248.0 0.5 multiply_reduce_fusion
  248.5 16.4 %all-gather.5 = f32[4,1,256]{2,1,0:T(1,128)S(1)} all-gather(f32[1,1,256]{2,1,0:T(1,128)S(1)} %bitcast.233), channel_id=4, replica_groups=mesh['seq_0'=8,'seq_1'=4,'seq_2'=4,'tp'=4] {'tp'}, dimensions={0}, use_global_device_ids=true | all-gather | bytes 5120 | tf_op jit(solution)/shard_map/all_gather | solution.py:42
  265.0 1.3 multiply_convert_fusion
  (28 shorter events, 0.3 us)
Async XLA Ops:
  6.5 15.5 %copy-start.1 = (bf16[256,128]{1,0:T(8,128)(2,1)S(1)}, bf16[256,128]{1,0:T(8,128)(2,1)}, u32[]{:S(2)}) copy-start(bf16[256,128]{1,0:T(8,128)(2,1)} %param.13) | copy-start | bytes 196612
  6.5 64.0 %all-gather.14.cloned.1.call-start = ((), (), s32[]{:S(2)}) async-start(), calls=%async_computation.2 | async-start | bytes 3276800 | tf_op jit(solution)/shard_map/all_gather | solution.py:25
  7.3 14.7 %collective-permute-start.1 = (bf16[3,128]{1,0:T(4,128)(2,1)S(1)}, bf16[3,128]{1,0:T(4,128)(2,1)S(1)}, u32[]{:S(2)}, u32[]{:S(2)}) collective-permute-start(bf16[3,128]{1,0:T(4,128)(2,1)S(1)} %slice.203), channel_id=1, source_target_pairs={{0,4},{4,8},{8,12},{12,16},{16,20},{20,24},{24,28},{28,32},{32,36}... | collective-permute-start | bytes 2312 | tf_op jit(solution)/shard_map/ppermute | solution.py:38
  23.5 92.9 %all-gather.10.cloned.1.call-start = ((), (), s32[]{:S(2)}) async-start(), calls=%async_computation | async-start | bytes 3276800 | tf_op jit(solution)/shard_map/all_gather | solution.py:25
  73.3 167.7 %all-gather.12.cloned.1.call-start = ((), (), s32[]{:S(2)}) async-start(), calls=%async_computation.1 | async-start | bytes 5898240 | tf_op jit(solution)/shard_map/all_gather | solution.py:25
  116.4 2.8 %copy-start.2 = (bf16[256,128]{1,0:T(8,128)(2,1)S(1)}, bf16[256,128]{1,0:T(8,128)(2,1)}, u32[]{:S(2)}) copy-start(bf16[256,128]{1,0:T(8,128)(2,1)} %param.14) | copy-start | bytes 196612
  119.2 33.1 %collective-permute-start = (bf16[3,128]{1,0:T(4,128)(2,1)S(1)}, bf16[3,128]{1,0:T(4,128)(2,1)S(1)}, u32[]{:S(2)}, u32[]{:S(2)}) collective-permute-start(bf16[3,128]{1,0:T(4,128)(2,1)S(1)} %slice.193), channel_id=1, source_target_pairs={{0,4},{4,8},{8,12},{12,16},{16,20},{20,24},{24,28},{28,32},{32,36}... | collective-permute-start | bytes 2312 | tf_op jit(solution)/shard_map/ppermute | solution.py:38
  246.9 1.1 copy-start
  248.0 17.0 %copy-start.3 = (f32[1280]{0:T(1024)S(1)}, f32[1280]{0:T(1024)}, u32[]{:S(2)}) copy-start(f32[1280]{0:T(1024)} %param.20) | copy-start | bytes 15364
Sparse Core Ops, SparseCore 0:
  23.6 46.8 all-gather.13
  73.4 42.9 all-gather.9
  119.3 121.6 all-gather.11
where the time goes:
time: 273 us
  waiting for transfers between devices  160 us (59%)
  blocking collectives  61.7 us (23%)
  between operations  14.6 us (5%)
  other arithmetic  13.2 us (5%)
  matrix products  9.79 us (4%)
  starting transfers between devices  7.11 us (3%)
  local copies, waits for them, and re-layouts  6.55 us (2%)
    all_gather x3, waiting for transfers between devices, carried_in(): pieces = jax.tree.map(lambda part: lax.all_gather(part, axis), so_far)  160 us
    all_gather x3, blocking collectives, carried_in(): pieces = jax.tree.map(lambda part: lax.all_gather(part, axis), so_far)  45.3 us
    all_gather x1, blocking collectives, gathered_total(): parts = lax.all_gather(array, axis)  16.4 us
    ppermute x2, starting transfers between devices, from_behind(): lax.ppermute(value, axis, [(source, source + steps) for source in range(f...  7.02 us
    dot_general x1, matrix products, emit_rows(): jnp.einsum('qn,hpn->qhp', c_block, state_in.astype(jnp.bfloat16), preferr...  5.9 us
    add x2, other arithmetic, combine(): later[0][:, None, None] * earlier[1] + later[1]  5.57 us
  transfers between devices with their start and end apart: 5, of which 3 were waited for; matrix products, arithmetic and copies ran while one was open for 5% of the time, Pallas kernels for 0%

commit v1 on v0

v1 whole, which is shorter than its diff:
```python
import functools

import jax
import jax.numpy as jnp
from jax import lax
from jax.experimental import pallas as pl
from jax.experimental.pallas import tpu as pltpu
from jax.sharding import Mesh
from jax.sharding import PartitionSpec as P

SEQ = ("za", "zb", "y", "x")
GROUP = ("zb", "y", "x")
OUTER = "za"
LANES = 128
epsilon = 1e-05
HIGHEST = lax.Precision.HIGHEST
VMEM = pl.BlockSpec(memory_space=pltpu.VMEM)
SMEM = pl.BlockSpec(memory_space=pltpu.SMEM)


def call(kernel, outs, *args, scalars=0, scratch=(), flops=1_000_000):
    multiple = isinstance(outs, (list, tuple))
    return pl.pallas_call(
        kernel,
        out_shape=list(outs) if multiple else outs,
        in_specs=[SMEM] * scalars + [VMEM] * (len(args) - scalars),
        out_specs=[VMEM] * len(outs) if multiple else VMEM,
        scratch_shapes=list(scratch),
        compiler_params=pltpu.CompilerParams(vmem_limit_bytes=24 * 1024 * 1024),
        cost_estimate=pl.CostEstimate(flops=flops, bytes_accessed=1_000_000, transcendentals=0),
    )(*args)


def out(shape, dtype=jnp.float32):
    return jax.ShapeDtypeStruct(shape, dtype)


def latest_start(position, doc_ref):
    start, chosen = jnp.int32(0), jnp.zeros_like(position)
    for i in range(doc_ref.shape[0]):
        chosen = jnp.maximum(chosen, jnp.where(start <= position, start, 0))
        start = start + doc_ref[i]
    return chosen


def tile_of_heads(columns, tile, width):
    per, rows = LANES // width, columns.shape[0]
    lane = lax.broadcasted_iota(jnp.int32, (rows, LANES), 1)
    spread = jnp.broadcast_to(columns[:, tile * per : tile * per + 1], (rows, LANES))
    for k in range(1, per):
        h = tile * per + k
        spread = jnp.where(
            lane < k * width, spread, jnp.broadcast_to(columns[:, h : h + 1], (rows, LANES))
        )
    return spread


def convolve(source_ref, halo, weight, bias, base, doc_ref, padded_ref):
    tokens = source_ref.shape[0]
    padded_ref[0:8, :] = halo.astype(jnp.float32)
    padded_ref[8:, :] = source_ref[...].astype(jnp.float32)
    position = base + lax.broadcasted_iota(jnp.int32, source_ref.shape, 0)
    doc_start = latest_start(position, doc_ref)
    summed = jnp.broadcast_to(bias, source_ref.shape)
    taps = weight.shape[0]
    for k in range(taps):
        back = taps - 1 - k
        term = weight[k : k + 1, :] * padded_ref[8 - back : 8 - back + tokens, :]
        summed = summed + jnp.where(position - back >= doc_start, term, 0.0)
    return (summed * jax.nn.sigmoid(summed)).astype(jnp.bfloat16)


def prepare_kernel(
    base_ref, doc_ref, x_ref, raw_ref, bias_ref, rate_ref, weighted_ref, cum_ref, step_ref, factor_ref
):
    base = base_ref[0]
    tokens, heads = raw_ref.shape
    width = x_ref.shape[1] // heads
    step = jax.nn.softplus(raw_ref[...] + bias_ref[...])
    log_decay = -step * rate_ref[...]
    rows = lax.broadcasted_iota(jnp.int32, (tokens, tokens), 0)
    cols = lax.broadcasted_iota(jnp.int32, (tokens, tokens), 1)
    cum = jnp.dot(
        jnp.where(cols <= rows, 1.0, 0.0), log_decay, precision=HIGHEST,
        preferred_element_type=jnp.float32,
    )
    cum_ref[...] = jnp.zeros_like(cum_ref)
    step_ref[...] = jnp.zeros_like(step_ref)
    factor_ref[...] = jnp.zeros_like(factor_ref)
    cum_ref[:, 0:heads] = cum
    step_ref[:, 0:heads] = step
    end_start = latest_start(base + tokens - 1, doc_ref)
    last = cum[tokens - 1 : tokens, :]
    position = base + lax.broadcasted_iota(jnp.int32, (tokens, heads), 0)
    weighting = jnp.where(position >= end_start, jnp.exp(last - cum) * step, 0.0)
    factor_ref[:, 0:heads] = jnp.where(end_start < base, jnp.exp(last), 0.0)
    for j in range(x_ref.shape[1] // LANES):
        tile = slice(j * LANES, (j + 1) * LANES)
        weighted_ref[:, tile] = (
            x_ref[:, tile].astype(jnp.float32) * tile_of_heads(weighting, j, width)
        ).astype(jnp.bfloat16)


def states_kernel(
    base_ref, doc_ref, b_ref, halo_ref, weight_ref, bias_ref, weighted_ref, factor_ref,
    pieces_ref, b_conv_ref, padded_ref,
):
    state, features = b_ref.shape[1], weighted_ref.shape[1]
    members, rows, _ = pieces_ref.shape
    b_conv = convolve(
        b_ref, halo_ref[:, 0:state], weight_ref[:, 0:state], bias_ref[:, 0:state],
        base_ref[0], doc_ref, padded_ref,
    )
    b_conv_ref[...] = b_conv
    b_rows = b_conv.astype(jnp.float32).T.astype(jnp.bfloat16)
    for j in range(features // 256):
        tile = slice(j * 256, (j + 1) * 256)
        end_state = jnp.dot(b_rows, weighted_ref[:, tile], preferred_element_type=jnp.float32)
        for m in range(members):
            pieces_ref[m, :, tile] = end_state[m * rows : (m + 1) * rows, :]
    spread = jnp.broadcast_to(factor_ref[...], (rows, LANES))
    for m in range(members):
        pieces_ref[m, :, features:] = spread


def prefix_kernel(heads, pieces_ref, before_ref, factors_ref, totals_ref, single_ref, wide_ref):
    members, rows, padded = pieces_ref.shape
    features = padded - LANES
    width = features // heads
    for m in range(members):
        single_ref[m : m + 1, :] = pieces_ref[m, 0:1, features:]
    single = single_ref[...]
    for j in range(features // LANES):
        wide_ref[:, j * LANES : (j + 1) * LANES] = tile_of_heads(single, j, width)
    product = jnp.ones((1, LANES), jnp.float32)
    for m in range(members):
        factors_ref[m : m + 1, :] = product
        product = product * single_ref[m : m + 1, :]
    total = jnp.zeros((rows, features), jnp.float32)
    for m in range(members):
        before_ref[m] = total
        total = wide_ref[m : m + 1, :] * total + pieces_ref[m, :, 0:features]
    for d in range(totals_ref.shape[0]):
        totals_ref[d, :, 0:features] = total
        totals_ref[d, :, features:] = jnp.broadcast_to(product, (rows, LANES))


def states_in_kernel(heads, place_ref, totals_ref, before_ref, factors_ref, state_ref, wide_ref):
    members, rows, features = before_ref.shape
    width = features // heads
    place = place_ref[0]
    entering = jnp.zeros((rows, features), jnp.float32)
    for g in range(totals_ref.shape[0] - 1):
        factor = jnp.concatenate(
            [
                tile_of_heads(totals_ref[g, 0:1, features:], j, width)
                for j in range(features // LANES)
            ],
            axis=1,
        )
        passed = factor * entering + totals_ref[g, :, 0:features]
        entering = jnp.where(g < place, passed, entering)
    factors = factors_ref[...]
    for j in range(features // LANES):
        wide_ref[:, j * LANES : (j + 1) * LANES] = tile_of_heads(factors, j, width)
    for m in range(members):
        state_ref[m] = (wide_ref[m : m + 1, :] * entering + before_ref[m]).astype(jnp.bfloat16)


def diagonal_kernel(
    base_ref, doc_ref, c_ref, halo_ref, weight_ref, bias_ref, b_conv_ref, cum_ref, step_ref,
    x_ref, gate_ref, c_conv_ref, gated_ref, scale_ref, padded_ref, products_ref,
):
    base = base_ref[0]
    tokens, state = c_ref.shape
    features = x_ref.shape[1]
    half = tokens // 2
    c_conv = convolve(
        c_ref, halo_ref[:, state:], weight_ref[:, state:], bias_ref[:, state:], base, doc_ref,
        padded_ref,
    )
    c_conv_ref[...] = c_conv
    products = lax.dot_general(
        c_conv, b_conv_ref[...], (((1,), (1,)), ((), ())), preferred_element_type=jnp.float32
    )
    row = lax.broadcasted_iota(jnp.int32, (tokens, tokens), 0)
    col = lax.broadcasted_iota(jnp.int32, (tokens, tokens), 1)
    doc_start = latest_start(base + row, doc_ref)
    products_ref[...] = jnp.where((col <= row) & (base + col >= doc_start), products, 0.0)
    cum, cum_rows, step_rows = cum_ref[...], cum_ref[...].T, step_ref[...].T
    width = features // HEADS_OF(features)
    position = base + lax.broadcasted_iota(jnp.int32, (tokens, LANES), 0)
    carried = jnp.where(doc_start[:, 0:LANES] < base, jnp.exp(cum), 0.0)
    lane = lax.broadcasted_iota(jnp.int32, (tokens, LANES), 1)
    del position
    per = LANES // width
    for j in range(features // LANES):
        tile = slice(j * LANES, (j + 1) * LANES)
        diagonal = None
        for k in range(per):
            h = j * per + k
            column = jnp.broadcast_to(cum[:, h : h + 1], (tokens, LANES))
            cum_row, step_row = cum_rows[h : h + 1, :], step_rows[h : h + 1, :]
            upper = (
                products_ref[0:half, 0:half] * jnp.exp(column[0:half] - cum_row[:, 0:half])
            ) * step_row[:, 0:half]
            lower_left = (
                products_ref[half:, 0:half] * jnp.exp(column[half:] - cum_row[:, 0:half])
            ) * step_row[:, 0:half]
            lower_right = (
                products_ref[half:, half:] * jnp.exp(column[half:] - cum_row[:, half:])
            ) * step_row[:, half:]
            lower = jnp.concatenate([lower_left, lower_right], axis=1).astype(jnp.bfloat16)
            part = jnp.concatenate(
                [
                    jnp.dot(upper.astype(jnp.bfloat16), x_ref[0:half, tile],
                            preferred_element_type=jnp.float32),
                    jnp.dot(lower, x_ref[:, tile], preferred_element_type=jnp.float32),
                ],
                axis=0,
            )
            diagonal = part if diagonal is None else jnp.where(lane < k * width, diagonal, part)
        gate = gate_ref[:, tile].astype(jnp.float32)
        gate = gate * jax.nn.sigmoid(gate)
        gated_ref[:, tile] = diagonal * gate
        scale_ref[:, tile] = tile_of_heads(carried, j, width) * gate


def HEADS_OF(features):
    return features // 64


def gate_kernel(state_ref, c_conv_ref, diagonal_ref, scale_ref, gated_ref, squares_ref, rows_ref):
    members, rows, features = state_ref.shape
    for m in range(members):
        rows_ref[m * rows : (m + 1) * rows, :] = state_ref[m].astype(jnp.float32)
    c_conv = c_conv_ref[...]
    squares = jnp.zeros((c_conv.shape[0], LANES), jnp.float32)
    for j in range(features // LANES):
        tile = slice(j * LANES, (j + 1) * LANES)
        carried = jnp.dot(
            c_conv, rows_ref[:, tile].astype(jnp.bfloat16), preferred_element_type=jnp.float32
        )
        gated = diagonal_ref[:, tile] + scale_ref[:, tile] * carried
        gated_ref[:, tile] = gated
        squares = squares + gated * gated
    squares_ref[...] = lax.dot_general(
        jnp.ones((8, LANES), jnp.float32), squares, (((1,), (1,)), ((), ())),
        precision=HIGHEST, preferred_element_type=jnp.float32,
    )[0:1]


def normalize_kernel(features_all, squares_ref, gated_ref, gain_ref, out_ref):
    count = squares_ref.shape[0]
    total = squares_ref[0]
    for k in range(1, count):
        total = total + squares_ref[k]
    first = lax.broadcasted_iota(jnp.int32, (8, total.shape[1]), 0) == 0
    column = lax.dot_general(
        jnp.where(first, jnp.broadcast_to(total, first.shape), 0.0),
        jnp.ones((8, LANES), jnp.float32), (((0,), (0,)), ((), ())),
        precision=HIGHEST, preferred_element_type=jnp.float32,
    )
    scale = lax.rsqrt(column / features_all + epsilon)
    for j in range(gated_ref.shape[1] // LANES):
        tile = slice(j * LANES, (j + 1) * LANES)
        out_ref[:, tile] = (gated_ref[:, tile] * scale * gain_ref[:, tile]).astype(jnp.bfloat16)


def body(
    inputs, gate_input, b_source, c_source, step_raw, step_bias, decay_rate, conv_weight,
    conv_bias, norm_gain, doc_lengths,
):
    tokens, features = inputs.shape
    heads = step_raw.shape[1]
    state = b_source.shape[1]
    members = 1
    for axis in GROUP:
        members *= lax.axis_size(axis)
    outer = lax.axis_size(OUTER)
    rows = state // members
    shards = members * outer
    base = (lax.axis_index(SEQ) * tokens).astype(jnp.int32).reshape(1)
    place = lax.axis_index(OUTER).astype(jnp.int32).reshape(1)

    tails = jnp.concatenate([b_source[tokens - 8 :], c_source[tokens - 8 :]], axis=1)
    halo = lax.ppermute(tails, SEQ, [(i, i + 1) for i in range(shards - 1)])

    weighted, cum, step, factor = call(
        prepare_kernel,
        [out((tokens, features), jnp.bfloat16), out((tokens, LANES)), out((tokens, LANES)), out((1, LANES))],
        base, doc_lengths, inputs, step_raw, step_bias[None, :], decay_rate[None, :], scalars=2,
    )
    pieces, b_conv = call(
        states_kernel,
        [out((members, rows, features + LANES)), out((tokens, state), jnp.bfloat16)],
        base, doc_lengths, b_source, halo, conv_weight, conv_bias[None, :], weighted, factor,
        scalars=2, scratch=[pltpu.VMEM((tokens + 8, state), jnp.float32)],
    )
    pieces = lax.all_to_all(pieces, GROUP, 0, 0)
    c_conv, diagonal, scale = call(
        diagonal_kernel,
        [out((tokens, state), jnp.bfloat16), out((tokens, features)), out((tokens, features))],
        base, doc_lengths, c_source, halo, conv_weight, conv_bias[None, :], b_conv, cum, step,
        inputs, gate_input, scalars=2,
        scratch=[
            pltpu.VMEM((tokens + 8, state), jnp.float32),
            pltpu.VMEM((tokens, tokens), jnp.float32),
        ],
    )
    before, factors, totals = call(
        functools.partial(prefix_kernel, heads),
        [out((members, rows, features)), out((members, LANES)), out((outer, rows, features + LANES))],
        pieces,
        scratch=[pltpu.VMEM((members, LANES), jnp.float32), pltpu.VMEM((members, features), jnp.float32)],
    )
    totals = lax.all_to_all(totals, OUTER, 0, 0)
    states_in = call(
        functools.partial(states_in_kernel, heads),
        out((members, rows, features), jnp.bfloat16),
        place, totals, before, factors, scalars=1,
        scratch=[pltpu.VMEM((members, features), jnp.float32)],
    )
    states_in = lax.all_to_all(states_in, GROUP, 0, 0)
    gated, squares = call(
        gate_kernel,
        [out((tokens, features)), out((1, tokens))],
        states_in, c_conv, diagonal, scale,
        scratch=[pltpu.VMEM((state, features), jnp.float32)],
    )
    squares = lax.all_gather(squares, "tp")
    return call(
        functools.partial(normalize_kernel, features * lax.axis_size("tp")),
        out((tokens, features), jnp.bfloat16),
        squares, gated, norm_gain[None, :],
    )


def solution(mesh):
    finer = Mesh(
        mesh.devices.reshape(4, 2, 4, 4, mesh.shape["tp"]), ("za", "zb", "y", "x", "tp")
    )
    in_specs = (
        P(SEQ, "tp"), P(SEQ, "tp"), P(SEQ, None), P(SEQ, None), P(SEQ, "tp"), P("tp"), P("tp"),
        P(), P(), P("tp"), P(),
    )
    return jax.shard_map(
        body, mesh=finer, in_specs=in_specs, out_specs=P(SEQ, "tp"), check_vma=False
    )
```

time: 273 us -> 91.7 us (0.34)
  waiting for transfers between devices: 160 us -> 4.52 us
  between operations: 14.6 us -> 0.2 us
  other arithmetic: 13.2 us -> 0.01 us
  matrix products: 9.79 us -> 0 us
  Pallas kernels: 0 us -> 8.82 us
  blocking collectives: 61.7 us -> 56.9 us
  starting transfers between devices: 7.11 us -> 10.8 us
  local copies, waits for them, and re-layouts: 6.55 us -> 9.87 us
    all_gather x3 -> x0, waiting for transfers between devices: 160 us -> none  [carried_in(): pieces = jax.tree.map(lambda part: lax.all_gather(part, axis), so_far)]
    all_gather x4 -> x1, blocking collectives: 61.7 us -> 17.4 us  [body(): squares = lax.all_gather(squares, 'tp')]
    all_to_all x0 -> x2, blocking collectives: none -> 39.5 us  [the longest x1 19.8 us: body(): totals = lax.all_to_all(totals, OUTER, 0, 0)]
    dot_general x4 -> x0, matrix products: 9.79 us -> none  [the longest x1 5.9 us: emit_rows(): jnp.einsum('qn,hpn->qhp', c_block, state_in.astype(jnp.bfloat16), preferr...]
    pallas_call x0 -> x7, Pallas kernels: none -> 8.82 us  [call(): pl.pallas_call(kernel, out_shape=list(outs) if multiple else outs, in_spe...]
    all_to_all x0 -> x1, starting transfers between devices: none -> 6.9 us  [body(): states_in = lax.all_to_all(states_in, GROUP, 0, 0)]
    unnamed x9 -> x33, local copies, waits for them, and re-layouts: 2.01 us -> 8.51 us
    add x3 -> x0, other arithmetic: 5.57 us -> none  [the longest x2 5.57 us: combine(): later[0][:, None, None] * earlier[1] + later[1]]
  transfers between devices with their start and end apart: 5 -> 2, of which waited for: 3 -> 1; matrix products, arithmetic and copies ran while one was open for 5% -> 1% of each run, Pallas kernels for 0% -> 5%
where the time goes in v1:
time: 91.7 us; the launch traced here: 91.2 us
  blocking collectives  56.9 us (62%)
  starting transfers between devices  10.8 us (12%)
  local copies, waits for them, and re-layouts  9.87 us (11%)
  Pallas kernels  8.82 us (10%)
  waiting for transfers between devices  4.52 us (5%)
    all_to_all x1, blocking collectives, body(): totals = lax.all_to_all(totals, OUTER, 0, 0)  19.8 us
    all_to_all x1, blocking collectives, body(): pieces = lax.all_to_all(pieces, GROUP, 0, 0)  19.7 us
    all_gather x1, blocking collectives, body(): squares = lax.all_gather(squares, 'tp')  17.4 us
    pallas_call x7, Pallas kernels, call(): pl.pallas_call(kernel, out_shape=list(outs) if multiple else outs, in_spe...  8.82 us
    unnamed x33, local copies, waits for them, and re-layouts  8.51 us
    all_to_all x1, starting transfers between devices, body(): states_in = lax.all_to_all(states_in, GROUP, 0, 0)  6.9 us
    all_to_all x1, waiting for transfers between devices, body(): states_in = lax.all_to_all(states_in, GROUP, 0, 0)  4.51 us
    ppermute x1, starting transfers between devices, body(): halo = lax.ppermute(tails, SEQ, [(i, i + 1) for i in range(shards - 1)])  3.93 us
  transfers between devices with their start and end apart: 2, of which 1 were waited for; matrix products, arithmetic and copies ran while one was open for 1% of the time, Pallas kernels for 5%

profile of v1, /device:TPU:1, one launch (start us, length us, event | category | flops | bytes accessed | tf_op | source)
XLA Modules:
  0.0 91.2 jit_solution(8721899636084278885)
XLA Ops:
  0.0 0.7 slice.6
  0.7 0.7 slice.7
  1.4 3.9 %collective-permute-start = (bf16[8,256]{1,0:T(8,128)(2,1)S(1)}, bf16[8,256]{1,0:T(8,128)(2,1)S(1)}, u32[]{:S(2)}, u32[]{:S(2)}) collective-permute-start(bf16[8,256]{1,0:T(8,128)(2,1)S(1)} %pad_maximum_fusion), channel_id=1, source_target_pairs={{0,4},{4,8},{8,12},{12,16},{16,20},{20,24},{24,28},{28,32},{32,36}... | collective-permute-start | bytes 12296 | tf_op jit(solution)/shard_map/ppermute | solution.py:287
  5.3 0.8 copy.13.raw_ref
  6.2 0.0 copy-start
  6.2 1.1 %copy-done = bf16[256,1280]{1,0:T(8,128)(2,1)S(1)} copy-done((bf16[256,1280]{1,0:T(8,128)(2,1)S(1)}, bf16[256,1280]{1,0:T(8,128)(2,1)}, u32[]{:S(2)}) %copy-start) | copy-done | bytes 655384
  7.3 0.0 copy-start.9
  7.3 0.7 copy-done.9
  7.9 0.0 copy-start.13
  7.9 0.7 copy-done.13
  8.6 0.0 copy-start.14
  8.6 0.7 copy-done.14
  9.2 1.8 %shard_map.109 = (bf16[256,1280]{1,0:T(8,128)(2,1)S(1)}, f32[256,128]{1,0:T(8,128)S(1)}, f32[256,128]{1,0:T(8,128)S(1)}, f32[1,128]{1,0:T(1,128)S(1)}) custom-call(s32[1]{0:T(128)} %bitcast.1.base_ref, s32[8]{0:T(128)S(1)} %copy-done.9, bf16[256,1280]{1,0:T(8,128)(2,1)S(1)} %copy-done, f32[256,20]{1,0:T(8,128)S(1)} %copy.13.raw_ref, f32[1,20]{1,0:T(1,128)S(1)} %bitcast.9, ...), custom_call_target="tpu_custom_call" | custom-call | flops 1000000 | bytes 1000000 | tf_op jit(solution)/shard_map/pallas_call | solution.py:23
  11.0 0.0 collective-permute-done.halo_ref
  11.0 0.0 copy-start.5
  11.0 0.8 copy-done.5
  11.9 0.0 copy-start.7
  11.9 0.7 copy-done.7
  12.6 0.7 copy-done.11
  13.2 1.0 %shard_map.110 = (f32[32,4,1408]{2,1,0:T(4,128)S(1)}, bf16[256,128]{1,0:T(8,128)(2,1)S(1)}) custom-call(s32[1]{0:T(128)} %bitcast.1.base_ref, s32[8]{0:T(128)S(1)} %copy-done.9, bf16[256,128]{1,0:T(8,128)(2,1)S(1)} %copy-done.5, bf16[8,256]{1,0:T(8,128)(2,1)S(1)} %collective-permute-done.halo_ref, f32[4,256]{1,0:T(4,128)S(1)} %copy-done.7, ...), custom_call_target="tpu_custom_call" | custom-call | flops 1000000 | bytes 1000000 | tf_op jit(solution)/shard_map/pallas_call | solution.py:23
  14.3 19.7 %all_to_all.15.pieces_ref = f32[32,4,1408]{2,1,0:T(4,128)S(1)} all-to-all(f32[32,4,1408]{2,1,0:T(4,128)S(1)} %get-tuple-element.21), channel_id=1, replica_groups=mesh['za'=4,'zb'=2,'y'=4,'x'=4,'tp'=4] {'zb','y','x'}, dimensions={0} | all-to-all | bytes 1441792 | tf_op jit(solution)/shard_map/all_to_all | solution.py:300
  34.0 0.0 copy-start.15
  34.0 0.0 copy-start.1
  34.0 0.0 copy-start.4
  34.0 0.0 copy-start.6
  34.0 0.0 copy-start.8
  34.0 0.0 copy-start.10
  34.0 0.0 copy-start.12
  34.1 0.3 shard_map.111
  34.4 19.8 %all_to_all.16.totals_ref = f32[4,4,1408]{2,1,0:T(4,128)S(1)} all-to-all(f32[4,4,1408]{2,1,0:T(4,128)S(1)} %get-tuple-element.22), channel_id=1, replica_groups=mesh['za'=4,'zb'=2,'y'=4,'x'=4,'tp'=4] {'za'}, dimensions={0} | all-to-all | bytes 180224 | tf_op jit(solution)/shard_map/all_to_all | solution.py:317
  54.2 1.2 %shard_map.112 = bf16[32,4,1280]{2,1,0:T(4,128)(2,1)} custom-call(s32[1]{0:T(128)} %bitcast.place_ref, f32[4,4,1408]{2,1,0:T(4,128)S(1)} %all_to_all.16.totals_ref, f32[32,4,1280]{2,1,0:T(4,128)S(1)} %get-tuple-element.23.before_ref, f32[32,128]{1,0:T(8,128)S(1)} %get-tuple-element.24.factors_ref), custom_call_target="tpu_custom_call" | custom-call | flops 1000000 | bytes 1000000 | tf_op jit(solution)/shard_map/pallas_call | solution.py:23
  55.4 6.9 %all-to-all-start.2 = ((bf16[32,4,1280]{2,1,0:T(4,128)(2,1)}), bf16[32,4,1280]{2,1,0:T(4,128)(2,1)S(1)}, u32[]{:S(2)}, u32[]{:S(2)}) async-start(bf16[32,4,1280]{2,1,0:T(4,128)(2,1)} %shard_map.112), calls=%async_computation.2 | async-start | bytes 655360 | tf_op jit(solution)/shard_map/all_to_all | solution.py:324
  62.3 0.0 copy-done.15
  62.3 0.0 copy-done.1
  62.3 0.0 copy-done.4
  62.3 0.0 copy-done.6
  62.3 0.0 copy-done.8
  62.3 0.0 copy-done.10
  62.3 0.0 copy-done.12
  62.4 2.5 %shard_map.113 = (bf16[256,128]{1,0:T(8,128)(2,1)S(1)}, f32[256,1280]{1,0:T(8,128)S(1)}, f32[256,1280]{1,0:T(8,128)S(1)}) custom-call(s32[1]{0:T(128)} %bitcast.1.base_ref, s32[8]{0:T(128)S(1)} %copy-done.10, bf16[256,128]{1,0:T(8,128)(2,1)S(1)} %copy-done.6, bf16[8,256]{1,0:T(8,128)(2,1)S(1)} %collective-permute-done.halo_ref, f32[4,256]{1,0:T(4,128)S(1)} %copy-done.8, ...), custom_call_target="tpu_custom_call" | custom-call | flops 1000000 | bytes 1000000 | tf_op jit(solution)/shard_map/pallas_call | solution.py:23
  64.9 0.0 copy-start.2
  64.9 1.1 %copy-done.2 = f32[256,1280]{1,0:T(8,128)} copy-done((f32[256,1280]{1,0:T(8,128)}, f32[256,1280]{1,0:T(8,128)S(1)}, u32[]{:S(2)}) %copy-start.2) | copy-done | bytes 1310744
  65.9 4.5 %all-to-all-done.2.state_ref = bf16[32,4,1280]{2,1,0:T(4,128)(2,1)S(1)} async-done(((bf16[32,4,1280]{2,1,0:T(4,128)(2,1)}), bf16[32,4,1280]{2,1,0:T(4,128)(2,1)S(1)}, u32[]{:S(2)}, u32[]{:S(2)}) %all-to-all-start.2) | async-done | bytes 327712 | tf_op jit(solution)/shard_map/all_to_all | solution.py:324
  70.4 0.0 copy-start.3
  70.4 1.3 %copy-done.3 = f32[256,1280]{1,0:T(8,128)S(1)} copy-done((f32[256,1280]{1,0:T(8,128)S(1)}, f32[256,1280]{1,0:T(8,128)}, u32[]{:S(2)}) %copy-start.3) | copy-done | bytes 1310744
  71.8 0.7 shard_map.114
  72.4 17.4 %all-gather.1.squares_ref = f32[4,1,256]{2,1,0:T(1,128)S(1)} all-gather(f32[1,1,256]{2,1,0:T(1,128)S(1)} %bitcast.8), channel_id=2, replica_groups=mesh['za'=4,'zb'=2,'y'=4,'x'=4,'tp'=4] {'tp'}, dimensions={0}, use_global_device_ids=true | all-gather | bytes 5120 | tf_op jit(solution)/shard_map/all_gather | solution.py:331
  89.9 1.3 %shard_map.115 = bf16[256,1280]{1,0:T(8,128)(2,1)} custom-call(f32[4,1,256]{2,1,0:T(1,128)S(1)} %all-gather.1.squares_ref, f32[256,1280]{1,0:T(8,128)S(1)} %get-tuple-element.32.gated_ref, f32[1,1280]{1,0:T(1,128)S(1)} %broadcast_in_dim.16.gain_ref), custom_call_target="tpu_custom_call" | custom-call | flops 1000000 | bytes 1000000 | tf_op jit(solution)/shard_map/pallas_call | solution.py:23
  (3 shorter events, 0.0 us)
Async XLA Ops:
  1.4 9.7 %collective-permute-start = (bf16[8,256]{1,0:T(8,128)(2,1)S(1)}, bf16[8,256]{1,0:T(8,128)(2,1)S(1)}, u32[]{:S(2)}, u32[]{:S(2)}) collective-permute-start(bf16[8,256]{1,0:T(8,128)(2,1)S(1)} %pad_maximum_fusion), channel_id=1, source_target_pairs={{0,4},{4,8},{8,12},{12,16},{16,20},{20,24},{24,28},{28,32},{32,36}... | collective-permute-start | bytes 12296 | tf_op jit(solution)/shard_map/ppermute | solution.py:287
  6.2 1.1 %copy-start = (bf16[256,1280]{1,0:T(8,128)(2,1)S(1)}, bf16[256,1280]{1,0:T(8,128)(2,1)}, u32[]{:S(2)}) copy-start(bf16[256,1280]{1,0:T(8,128)(2,1)} %x_ref.3) | copy-start | bytes 1966084
  7.3 0.7 copy-start.9
  7.9 0.7 copy-start.13
  8.6 0.7 copy-start.14
  11.0 0.8 copy-start.5
  11.9 0.7 copy-start.7
  12.6 0.7 copy-start.11
  34.0 28.3 %copy-start.15 = (f32[1280]{0:T(1024)S(1)}, f32[1280]{0:T(1024)}, u32[]{:S(2)}) copy-start(f32[1280]{0:T(1024)} %param.20) | copy-start | bytes 15364
  34.0 28.3 %copy-start.1 = (bf16[256,1280]{1,0:T(8,128)(2,1)S(1)}, bf16[256,1280]{1,0:T(8,128)(2,1)}, u32[]{:S(2)}) copy-start(bf16[256,1280]{1,0:T(8,128)(2,1)} %x_ref.3) | copy-start | bytes 1966084
  34.0 28.3 %copy-start.4 = (bf16[256,1280]{1,0:T(8,128)(2,1)S(1)}, bf16[256,1280]{1,0:T(8,128)(2,1)}, u32[]{:S(2)}) copy-start(bf16[256,1280]{1,0:T(8,128)(2,1)} %gate_ref.1) | copy-start | bytes 1966084
  34.0 28.3 %copy-start.6 = (bf16[256,128]{1,0:T(8,128)(2,1)S(1)}, bf16[256,128]{1,0:T(8,128)(2,1)}, u32[]{:S(2)}) copy-start(bf16[256,128]{1,0:T(8,128)(2,1)} %c_ref.1) | copy-start | bytes 196612
  34.0 28.3 %copy-start.8 = (f32[4,256]{1,0:T(4,128)S(1)}, f32[4,256]{1,0:T(4,128)}, u32[]{:S(2)}) copy-start(f32[4,256]{1,0:T(4,128)} %weight_ref.3) | copy-start | bytes 12292
  34.0 28.3 %copy-start.10 = (s32[8]{0:T(128)S(1)}, s32[8]{0:T(128)}, u32[]{:S(2)}) copy-start(s32[8]{0:T(128)} %doc_ref.5) | copy-start | bytes 100
  34.0 28.3 %copy-start.12 = (f32[256]{0:T(256)S(1)}, f32[256]{0:T(256)}, u32[]{:S(2)}) copy-start(f32[256]{0:T(256)} %param.19) | copy-start | bytes 3076
  55.4 15.1 %all-to-all-start.2 = ((bf16[32,4,1280]{2,1,0:T(4,128)(2,1)}), bf16[32,4,1280]{2,1,0:T(4,128)(2,1)S(1)}, u32[]{:S(2)}, u32[]{:S(2)}) async-start(bf16[32,4,1280]{2,1,0:T(4,128)(2,1)} %shard_map.112), calls=%async_computation.2 | async-start | bytes 655360 | tf_op jit(solution)/shard_map/all_to_all | solution.py:324
  64.9 1.1 %copy-start.2 = (f32[256,1280]{1,0:T(8,128)}, f32[256,1280]{1,0:T(8,128)S(1)}, u32[]{:S(2)}) copy-start(f32[256,1280]{1,0:T(8,128)S(1)} %get-tuple-element.30.scale_ref) | copy-start | bytes 3932164
  70.4 1.3 %copy-start.3 = (f32[256,1280]{1,0:T(8,128)S(1)}, f32[256,1280]{1,0:T(8,128)}, u32[]{:S(2)}) copy-start(f32[256,1280]{1,0:T(8,128)} %copy-done.2) | copy-start | bytes 3932164

commit v2 on v1

v2 whole, which is shorter than its diff:
```python
import functools

import jax
import jax.numpy as jnp
from jax import lax
from jax.experimental import pallas as pl
from jax.experimental.pallas import tpu as pltpu
from jax.sharding import Mesh
from jax.sharding import PartitionSpec as P

SEQ = ("za", "zb", "y", "x")
GROUP = ("zb", "y", "x")
OUTER = "za"
LANES = 128
epsilon = 1e-05
HIGHEST = lax.Precision.HIGHEST
VMEM = pl.BlockSpec(memory_space=pltpu.VMEM)
HBM = pl.BlockSpec(memory_space=pltpu.HBM)


def call(kernel, outs, *args, hbm=0, after=(), scratch=(), flops=1_000_000):
    if after:
        inner, skip = kernel, len(after)
        kernel = lambda *refs: inner(*refs[:len(args)], *refs[len(args) + skip:])
    multiple = isinstance(outs, (list, tuple))
    return pl.pallas_call(
        kernel,
        out_shape=list(outs) if multiple else outs,
        in_specs=[HBM] * hbm + [VMEM] * (len(args) - hbm) + [VMEM] * len(after),
        out_specs=[VMEM] * len(outs) if multiple else VMEM,
        scratch_shapes=list(scratch),
        compiler_params=pltpu.CompilerParams(vmem_limit_bytes=24 * 1024 * 1024),
        cost_estimate=pl.CostEstimate(flops=flops, bytes_accessed=1_000_000, transcendentals=0),
    )(*(pltpu.with_memory_space_constraint(a, pltpu.HBM) for a in args[:hbm]), *args[hbm:], *after)


def out(shape, dtype=jnp.float32):
    return pltpu.VMEM(shape, dtype)


def tile_of_heads(columns, tile, width, first=0):
    per, rows = LANES // width, columns.shape[0]
    lane = lax.broadcasted_iota(jnp.int32, (rows, LANES), 1)
    h = first + tile * per
    spread = jnp.broadcast_to(columns[:, h : h + 1], (rows, LANES))
    for k in range(1, per):
        other = jnp.broadcast_to(columns[:, h + k : h + k + 1], (rows, LANES))
        spread = jnp.where(lane < k * width, spread, other)
    return spread


def load_kernel(b_ref, c_ref, *refs):
    count = (len(refs) - 2) // 2
    sources, tails_ref, targets, sems = refs[:count], refs[count], refs[count + 1 : -1], refs[-1]
    tokens, state = b_ref.shape
    copies = [
        pltpu.make_async_copy(
            r.at[pl.ds(tokens - 8, 8), :], tails_ref.at[:, pl.ds(k * state, state)], sems.at[k]
        )
        for k, r in enumerate((b_ref, c_ref))
    ]
    for k, (source, target) in enumerate(zip(sources, targets)):
        copies.append(pltpu.make_async_copy(source, target, sems.at[k + 2]))
    for copy in copies:
        copy.start()
    for copy in copies:
        copy.wait()


def convolve(padded_ref, weight, bias, relative, start):
    tokens = relative.shape[0]
    taps = weight.shape[0]
    summed = jnp.broadcast_to(bias, (tokens, bias.shape[1]))
    for k in range(taps):
        back = taps - 1 - k
        term = weight[k : k + 1, :] * padded_ref[8 - back : 8 - back + tokens, :]
        summed = summed + jnp.where(relative - back >= start, term, 0.0)
    return (summed * jax.nn.sigmoid(summed)).astype(jnp.bfloat16)


def sequence_index():
    index = 0
    for axis in SEQ:
        index = index * lax.axis_size(axis) + lax.axis_index(axis)
    return index


def to_column(row):
    n = row.shape[1]
    same = lax.broadcasted_iota(jnp.int32, (n, n), 0) == lax.broadcasted_iota(jnp.int32, (n, n), 1)
    return jnp.sum(jnp.where(same, jnp.broadcast_to(row, (n, n)), 0.0), axis=1, keepdims=True)


WEIGHTS_AT = 32


def prepare_kernel(
    x_ref, raw_ref, bias_ref, rate_ref, docs_ref, b_ref, c_ref, taps_ref, taps_bias_ref,
    weighted_ref, cum_rows_ref, step_rows_ref, columns_ref, factor_ref, start_ref, b_conv_ref,
    c_conv_ref, stack_ref, padded_ref,
):
    heads, tokens = raw_ref.shape
    state = b_ref.shape[1]
    width = x_ref.shape[1] // heads
    base = sequence_index() * tokens
    relative = lax.broadcasted_iota(jnp.int32, (tokens, LANES), 0)
    start = jnp.zeros((1, 1), jnp.int32) - base
    last_position = jnp.full((1, 1), tokens - 1, jnp.int32)
    chosen = jnp.broadcast_to(start, relative.shape)
    end_start = start
    for i in range(1, docs_ref.shape[1]):
        start = start + docs_ref[0:1, i - 1 : i]
        chosen = jnp.where(start <= relative, start, chosen)
        end_start = jnp.where(start <= last_position, start, end_start)
    start_ref[...] = chosen

    step = jax.nn.softplus(raw_ref[...] + to_column(bias_ref[...]))
    log_decay = -step * to_column(rate_ref[...])
    rows = lax.broadcasted_iota(jnp.int32, (tokens, tokens), 0)
    cols = lax.broadcasted_iota(jnp.int32, (tokens, tokens), 1)
    cum = jnp.dot(
        log_decay, jnp.where(rows <= cols, 1.0, 0.0), precision=HIGHEST,
        preferred_element_type=jnp.float32,
    )
    cum_rows_ref[...] = cum
    step_rows_ref[...] = step
    position = lax.broadcasted_iota(jnp.int32, (heads, tokens), 1)
    weighting = jnp.where(
        position >= end_start, jnp.exp(cum[:, tokens - 1 : tokens] - cum) * step, 0.0
    )
    stack_ref[...] = jnp.zeros_like(stack_ref)
    stack_ref[0:heads, :] = cum
    stack_ref[WEIGHTS_AT : WEIGHTS_AT + heads, :] = weighting
    columns = stack_ref[...].T
    columns_ref[...] = columns
    factor_ref[...] = jnp.where(end_start < 0, jnp.exp(columns[tokens - 1 : tokens, :]), 0.0)
    for j in range(x_ref.shape[1] // LANES):
        tile = slice(j * LANES, (j + 1) * LANES)
        weighted_ref[:, tile] = (
            x_ref[:, tile].astype(jnp.float32) * tile_of_heads(columns, j, width, WEIGHTS_AT)
        ).astype(jnp.bfloat16)
    padded_ref[0:8, :] = jnp.zeros((8, state), jnp.float32)
    for k, (source_ref, target_ref) in enumerate(((b_ref, b_conv_ref), (c_ref, c_conv_ref))):
        side = slice(k * state, (k + 1) * state)
        padded_ref[8:, :] = source_ref[...].astype(jnp.float32)
        result = convolve(padded_ref, taps_ref[:, side], taps_bias_ref[:, side], relative, chosen)
        target_ref[...] = result.astype(target_ref.dtype)


def first_rows(source_ref, halo, weight, bias, start_ref, padded_ref):
    padded_ref[0:8, :] = halo.astype(jnp.float32)
    padded_ref[8:, :] = source_ref[0:8, :].astype(jnp.float32)
    relative = lax.broadcasted_iota(jnp.int32, (8, LANES), 0)
    return convolve(padded_ref, weight, bias, relative, start_ref[0:8, :])


def states_kernel(
    b_ref, halo_ref, taps_ref, taps_bias_ref, start_ref, b_early_ref, weighted_ref, factor_ref,
    pieces_ref, b_conv_ref, padded_ref,
):
    state, features = b_ref.shape[1], weighted_ref.shape[1]
    members, rows, _ = pieces_ref.shape
    first = first_rows(
        b_ref, halo_ref[:, 0:state], taps_ref[:, 0:state], taps_bias_ref[:, 0:state], start_ref,
        padded_ref,
    )
    b_conv = jnp.concatenate([first.astype(jnp.float32), b_early_ref[8:, :]], axis=0)
    b_conv_ref[...] = b_conv.astype(jnp.bfloat16)
    b_rows = b_conv.T.astype(jnp.bfloat16)
    for j in range(features // 256):
        tile = slice(j * 256, (j + 1) * 256)
        end_state = jnp.dot(b_rows, weighted_ref[:, tile], preferred_element_type=jnp.float32)
        for m in range(members):
            pieces_ref[m, :, tile] = end_state[m * rows : (m + 1) * rows, :]
    spread = jnp.broadcast_to(factor_ref[...], (rows, LANES))
    for m in range(members):
        pieces_ref[m, :, features:] = spread


def prefix_kernel(heads, pieces_ref, before_ref, factors_ref, total_ref, single_ref, wide_ref):
    members, rows, padded = pieces_ref.shape
    features = padded - LANES
    width = features // heads
    for m in range(members):
        single_ref[m : m + 1, :] = pieces_ref[m, 0:1, features:]
    single = single_ref[...]
    for j in range(features // LANES):
        wide_ref[:, j * LANES : (j + 1) * LANES] = tile_of_heads(single, j, width)
    product = jnp.ones((1, LANES), jnp.float32)
    for m in range(members):
        factors_ref[m : m + 1, :] = product
        product = product * single_ref[m : m + 1, :]
    total = jnp.zeros((rows, features), jnp.float32)
    for m in range(members):
        before_ref[m] = total
        total = wide_ref[m : m + 1, :] * total + pieces_ref[m, :, 0:features]
    total_ref[:, 0:features] = total
    total_ref[:, features:] = jnp.broadcast_to(product, (rows, LANES))


def wide_factor(pair_ref, features, width):
    factor = pair_ref[0:1, features:]
    return jnp.concatenate(
        [tile_of_heads(factor, j, width) for j in range(features // LANES)], axis=1
    )


def join_kernel(heads, own_ref, behind_ref, joined_ref):
    features = own_ref.shape[1] - LANES
    factor = wide_factor(own_ref, features, features // heads)
    joined_ref[:, 0:features] = factor * behind_ref[:, 0:features] + own_ref[:, 0:features]
    joined_ref[:, features:] = own_ref[:, features:] * behind_ref[:, features:]


def states_in_kernel(heads, near_ref, far_ref, before_ref, factors_ref, state_ref, wide_ref):
    members, rows, features = before_ref.shape
    width = features // heads
    factor = wide_factor(near_ref, features, width)
    entering = factor * far_ref[:, 0:features] + near_ref[:, 0:features]
    factors = factors_ref[...]
    for j in range(features // LANES):
        wide_ref[:, j * LANES : (j + 1) * LANES] = tile_of_heads(factors, j, width)
    for m in range(members):
        state_ref[m] = (wide_ref[m : m + 1, :] * entering + before_ref[m]).astype(jnp.bfloat16)


def diagonal_kernel(
    first_head, c_ref, halo_ref, taps_ref, taps_bias_ref, start_ref, c_early_ref, b_conv_ref,
    columns_ref, cum_rows_ref, step_rows_ref, x_ref, gate_ref, c_conv_ref, gated_ref, scale_ref,
    padded_ref, products_ref,
):
    tokens, state = c_ref.shape
    features, heads = x_ref.shape[1], cum_rows_ref.shape[0]
    width, half = features // heads, tokens // 2
    first = first_rows(
        c_ref, halo_ref[:, state:], taps_ref[:, state:], taps_bias_ref[:, state:], start_ref,
        padded_ref,
    )
    c_conv = jnp.concatenate(
        [first.astype(jnp.float32), c_early_ref[8:, :]], axis=0
    ).astype(jnp.bfloat16)
    c_conv_ref[...] = c_conv
    products = lax.dot_general(
        c_conv, b_conv_ref[...], (((1,), (1,)), ((), ())), preferred_element_type=jnp.float32
    )
    row = lax.broadcasted_iota(jnp.int32, (tokens, tokens), 0)
    col = lax.broadcasted_iota(jnp.int32, (tokens, tokens), 1)
    start = start_ref[...]
    starts = jnp.concatenate([start] * (tokens // LANES), axis=1)
    products_ref[...] = jnp.where((col <= row) & (col >= starts), products, 0.0)
    columns = columns_ref[...]
    carried = jnp.where(start < 0, jnp.exp(columns), 0.0)
    lane = lax.broadcasted_iota(jnp.int32, (tokens, LANES), 1)
    per = LANES // width
    for i in range(gated_ref.shape[1] // LANES):
        j = first_head // per + i
        tile = slice(j * LANES, (j + 1) * LANES)
        here = slice(i * LANES, (i + 1) * LANES)
        diagonal = None
        for k in range(per):
            h = j * per + k
            column = jnp.broadcast_to(columns[:, h : h + 1], (tokens, LANES))
            cum_row, step_row = cum_rows_ref[h : h + 1, :], step_rows_ref[h : h + 1, :]
            upper = (
                products_ref[0:half, 0:half] * jnp.exp(column[0:half] - cum_row[:, 0:half])
            ) * step_row[:, 0:half]
            lower_left = (
                products_ref[half:, 0:half] * jnp.exp(column[half:] - cum_row[:, 0:half])
            ) * step_row[:, 0:half]
            lower_right = (
                products_ref[half:, half:] * jnp.exp(column[half:] - cum_row[:, half:])
            ) * step_row[:, half:]
            lower = jnp.concatenate([lower_left, lower_right], axis=1).astype(jnp.bfloat16)
            part = jnp.concatenate(
                [
                    jnp.dot(upper.astype(jnp.bfloat16), x_ref[0:half, tile],
                            preferred_element_type=jnp.float32),
                    jnp.dot(lower, x_ref[:, tile], preferred_element_type=jnp.float32),
                ],
                axis=0,
            )
            diagonal = part if diagonal is None else jnp.where(lane < k * width, diagonal, part)
        gate = gate_ref[:, tile].astype(jnp.float32)
        gate = gate * jax.nn.sigmoid(gate)
        gated_ref[:, here] = diagonal * gate
        scale_ref[:, here] = tile_of_heads(carried, j, width) * gate


def gate_kernel(
    state_ref, c_conv_ref, diagonal_a_ref, scale_a_ref, diagonal_b_ref, scale_b_ref, gated_ref,
    squares_ref, rows_ref,
):
    members, rows, features = state_ref.shape
    for m in range(members):
        rows_ref[m * rows : (m + 1) * rows, :] = state_ref[m].astype(jnp.float32)
    c_conv = c_conv_ref[...]
    squares = jnp.zeros((c_conv.shape[0], LANES), jnp.float32)
    parts = diagonal_a_ref.shape[1] // LANES
    for j in range(features // LANES):
        tile = slice(j * LANES, (j + 1) * LANES)
        diagonal_ref, scale_ref = (
            (diagonal_a_ref, scale_a_ref) if j < parts else (diagonal_b_ref, scale_b_ref)
        )
        here = slice((j % parts) * LANES, (j % parts + 1) * LANES)
        carried = jnp.dot(
            c_conv, rows_ref[:, tile].astype(jnp.bfloat16), preferred_element_type=jnp.float32
        )
        gated = diagonal_ref[:, here] + scale_ref[:, here] * carried
        gated_ref[:, tile] = gated
        squares = squares + gated * gated
    squares_ref[...] = lax.dot_general(
        jnp.ones((8, LANES), jnp.float32), squares, (((1,), (1,)), ((), ())),
        precision=HIGHEST, preferred_element_type=jnp.float32,
    )[0:1]


def normalize_kernel(features_all, squares_ref, gated_ref, gain_ref, out_ref):
    count = squares_ref.shape[0]
    total = squares_ref[0]
    for k in range(1, count):
        total = total + squares_ref[k]
    first = lax.broadcasted_iota(jnp.int32, (8, total.shape[1]), 0) == 0
    column = lax.dot_general(
        jnp.where(first, jnp.broadcast_to(total, first.shape), 0.0),
        jnp.ones((8, LANES), jnp.float32), (((0,), (0,)), ((), ())),
        precision=HIGHEST, preferred_element_type=jnp.float32,
    )
    scale = lax.rsqrt(column / features_all + epsilon)
    for j in range(gated_ref.shape[1] // LANES):
        tile = slice(j * LANES, (j + 1) * LANES)
        out_ref[:, tile] = (gated_ref[:, tile] * scale * gain_ref[:, tile]).astype(jnp.bfloat16)


def body(
    inputs, gate_input, b_source, c_source, step_raw, step_bias, decay_rate, conv_weight,
    conv_bias, norm_gain, doc_lengths,
):
    tokens, features = inputs.shape
    heads = step_raw.shape[1]
    state = b_source.shape[1]
    members = 1
    for axis in GROUP:
        members *= lax.axis_size(axis)
    outer = lax.axis_size(OUTER)
    rows = state // members
    shards = members * outer
    ahead = lambda n, k: [(i, i + k) for i in range(n - k)]

    bf16 = jnp.bfloat16
    operands = [
        inputs, step_raw.T, step_bias[None, :], decay_rate[None, :], doc_lengths[None, :],
        b_source, c_source, conv_weight, conv_bias[None, :], norm_gain[None, :],
    ]
    tails, *loaded = call(
        load_kernel,
        [out((8, 2 * state), bf16)] + [out(o.shape, o.dtype) for o in operands],
        b_source, c_source, *operands,
        hbm=2 + len(operands),
        scratch=[pltpu.SemaphoreType.DMA((2 + len(operands),))],
    )
    x, raw, bias, rate, docs, b, c, taps, taps_bias, gain = loaded
    halo = lax.ppermute(tails, SEQ, ahead(shards, 1))
    weighted, cum_rows, step_rows, columns, factor, start, b_early, c_early = call(
        prepare_kernel,
        [
            out((tokens, features), bf16), out((heads, tokens)), out((heads, tokens)),
            out((tokens, LANES)), out((1, LANES)), out((tokens, LANES), jnp.int32),
            out((tokens, state)), out((tokens, state)),
        ],
        x, raw, bias, rate, docs, b, c, taps, taps_bias,
        scratch=[
            pltpu.VMEM((LANES, tokens), jnp.float32),
            pltpu.VMEM((tokens + 8, state), jnp.float32),
        ],
    )
    pieces, b_conv = call(
        states_kernel,
        [out((members, rows, features + LANES)), out((tokens, state), bf16)],
        b, halo, taps, taps_bias, start, b_early, weighted, factor,
        scratch=[pltpu.VMEM((16, state), jnp.float32)],
    )
    pieces = lax.all_to_all(pieces, GROUP, 0, 0)
    before, factors, total = call(
        functools.partial(prefix_kernel, heads),
        [out((members, rows, features)), out((members, LANES)), out((rows, features + LANES))],
        pieces,
        scratch=[
            pltpu.VMEM((members, LANES), jnp.float32),
            pltpu.VMEM((members, features), jnp.float32),
        ],
    )

    def diagonal_part(first_head):
        return call(
            functools.partial(diagonal_kernel, first_head),
            [out((tokens, state), bf16), out((tokens, features // 2)), out((tokens, features // 2))],
            c, halo, taps, taps_bias, start, c_early, b_conv, columns, cum_rows, step_rows, x,
            gate_input, flops=20_000_000_000,
            scratch=[
                pltpu.VMEM((16, state), jnp.float32),
                pltpu.VMEM((tokens, tokens), jnp.float32),
            ],
        )

    near = lax.ppermute(total, OUTER, ahead(outer, 1))
    c_conv, diagonal_a, scale_a = diagonal_part(0)
    joined = call(functools.partial(join_kernel, heads), out(total.shape), total, near, after=(c_conv,))
    far = lax.ppermute(joined, OUTER, ahead(outer, 2))
    _, diagonal_b, scale_b = diagonal_part(heads // 2)
    states_in = call(
        functools.partial(states_in_kernel, heads),
        out((members, rows, features), bf16),
        near, far, before, factors, after=(diagonal_b, scale_b),
        scratch=[pltpu.VMEM((members, features), jnp.float32)],
    )
    states_in = lax.all_to_all(states_in, GROUP, 0, 0)
    gated, squares = call(
        gate_kernel,
        [out((tokens, features)), out((1, tokens))],
        states_in, c_conv, diagonal_a, scale_a, diagonal_b, scale_b,
        scratch=[pltpu.VMEM((state, features), jnp.float32)],
    )
    squares = lax.all_gather(squares, "tp")
    return call(
        functools.partial(normalize_kernel, features * lax.axis_size("tp")),
        jax.ShapeDtypeStruct((tokens, features), bf16),
        squares, gated, gain,
    )


def solution(mesh):
    finer = Mesh(
        mesh.devices.reshape(4, 2, 4, 4, mesh.shape["tp"]), ("za", "zb", "y", "x", "tp")
    )
    in_specs = (
        P(SEQ, "tp"), P(SEQ, "tp"), P(SEQ, None), P(SEQ, None), P(SEQ, "tp"), P("tp"), P("tp"),
        P(), P(), P("tp"), P(),
    )
    return jax.shard_map(
        body, mesh=finer, in_specs=in_specs, out_specs=P(SEQ, "tp"), check_vma=False
    )
```

time: 91.7 us -> 80.5 us (0.88)
  local copies, waits for them, and re-layouts: 9.87 us -> 1.3 us
  starting transfers between devices: 10.8 us -> 18.5 us
  blocking collectives: 56.9 us -> 51.8 us
  waiting for transfers between devices: 4.52 us -> 0.01 us
    ppermute x1 -> x3, starting transfers between devices: 3.93 us -> 18.5 us  [the longest x1 9.74 us: body(): far = lax.ppermute(joined, OUTER, ahead(outer, 2))]
    unnamed x33 -> x2, local copies, waits for them, and re-layouts: 8.51 us -> 0.01 us
    all_to_all x1 -> x0, starting transfers between devices: 6.9 us -> none  [body(): states_in = lax.all_to_all(states_in, GROUP, 0, 0)]
    all_to_all x1, blocking collectives: 19.8 us -> 13.7 us  [body(): states_in = lax.all_to_all(states_in, GROUP, 0, 0)]
    all_to_all x1 -> x0, waiting for transfers between devices: 4.51 us -> none  [body(): states_in = lax.all_to_all(states_in, GROUP, 0, 0)]
    slice x2 -> x0, local copies, waits for them, and re-layouts: 1.36 us -> none  [the longest x1 0.68 us: body(): b_source[tokens - 8:]]
    broadcast_in_dim x1, local copies, waits for them, and re-layouts: 0.01 us -> 1.29 us  [body(): norm_gain[None, :]]
    all_to_all x1, blocking collectives: 19.7 us -> 20.8 us  [body(): pieces = lax.all_to_all(pieces, GROUP, 0, 0)]
  transfers between devices with their start and end apart: 2 -> 3, of which waited for: 1 -> 0; matrix products, arithmetic and copies ran while one was open for 1% -> 0% of each run, Pallas kernels for 5% -> 5%
where the time goes in v2:
time: 80.5 us; the launch traced here: 80.2 us
  blocking collectives  51.8 us (64%)
  starting transfers between devices  18.5 us (23%)
  Pallas kernels  8.44 us (10%)
  local copies, waits for them, and re-layouts  1.3 us (2%)
    all_to_all x1, blocking collectives, body(): pieces = lax.all_to_all(pieces, GROUP, 0, 0)  20.8 us
    all_gather x1, blocking collectives, body(): squares = lax.all_gather(squares, 'tp')  17.3 us
    all_to_all x1, blocking collectives, body(): states_in = lax.all_to_all(states_in, GROUP, 0, 0)  13.7 us
    ppermute x1, starting transfers between devices, body(): far = lax.ppermute(joined, OUTER, ahead(outer, 2))  9.74 us
    pallas_call x10, Pallas kernels, call(): pl.pallas_call(kernel, out_shape=list(outs) if multiple else outs, in_spe...  8.44 us
    ppermute x1, starting transfers between devices, body(): near = lax.ppermute(total, OUTER, ahead(outer, 1))  4.81 us
    ppermute x1, starting transfers between devices, body(): halo = lax.ppermute(tails, SEQ, ahead(shards, 1))  3.94 us
  transfers between devices with their start and end apart: 3, of which 0 were waited for; matrix products, arithmetic and copies ran while one was open for 0% of the time, Pallas kernels for 5%

profile of v2, /device:TPU:1, one launch (start us, length us, event | category | flops | bytes accessed | tf_op | source)
XLA Modules:
  0.0 80.2 jit_solution(5476427152385938706)
XLA Ops:
  0.0 1.3 %broadcast_in_dim.19.refs_9_ = f32[1,1280]{1,0:T(1,128)} reshape(f32[1280]{0:T(1024)} %param.20) | data formatting | bytes 10240 | tf_op jit(solution)/shard_map/broadcast_in_dim | solution.py:352
  1.3 1.3 %shard_map.109 = (bf16[8,256]{1,0:T(8,128)(2,1)S(1)}, bf16[256,1280]{1,0:T(8,128)(2,1)S(1)}, f32[20,256]{1,0:T(8,128)S(1)}, f32[1,20]{1,0:T(1,128)S(1)}, f32[1,2...) custom-call(bf16[256,128]{1,0:T(8,128)(2,1)} %refs_5_.1, ...), custom_call_target="tpu_custom_call" | custom-call | flops 1000000 | bytes 1000000 | tf_op jit(solution)/shard_map/pallas_call | solution.py:26
  2.6 3.9 %collective-permute-start = (bf16[8,256]{1,0:T(8,128)(2,1)S(1)}, bf16[8,256]{1,0:T(8,128)(2,1)S(1)}, u32[]{:S(2)}, u32[]{:S(2)}) collective-permute-start(bf16[8,256]{1,0:T(8,128)(2,1)S(1)} %get-tuple-element.37), channel_id=1, source_target_pairs={{0,4},{4,8},{8,12},{12,16},{16,20},{20,24},{24,28},{28,32},{32,36}... | collective-permute-start | bytes 12296 | tf_op jit(solution)/shard_map/ppermute | solution.py:362
  6.5 1.7 %shard_map.110 = (bf16[256,1280]{1,0:T(8,128)(2,1)S(1)}, f32[20,256]{1,0:T(8,128)S(1)}, f32[20,256]{1,0:T(8,128)S(1)}, f32[256,128]{1,0:T(8,128)S(1)}, f32[1,128...) custom-call(bf16[256,1280]{1,0:T(8,128)(2,1)S(1)} %get-tuple-element.40.x_ref, ...), custom_call_target="tpu_custom_call" | custom-call | flops 1000000 | bytes 1000000 | tf_op jit(solution)/shard_map/pallas_call | solution.py:26
  8.2 0.0 collective-permute-done.halo_ref
  8.2 0.3 shard_map.111
  8.6 0.0 copy-start
  8.6 20.8 %all_to_all.10.pieces_ref = f32[32,4,1408]{2,1,0:T(4,128)S(1)} all-to-all(f32[32,4,1408]{2,1,0:T(4,128)S(1)} %get-tuple-element.50), channel_id=1, replica_groups=mesh['za'=4,'zb'=2,'y'=4,'x'=4,'tp'=4] {'zb','y','x'}, dimensions={0} | all-to-all | bytes 1441792 | tf_op jit(solution)/shard_map/all_to_all | solution.py:382
  29.4 0.3 shard_map.112
  29.7 4.8 %collective-permute-start.1 = (f32[4,1408]{1,0:T(4,128)S(1)}, f32[4,1408]{1,0:T(4,128)S(1)}, u32[]{:S(2)}, u32[]{:S(2)}) collective-permute-start(f32[4,1408]{1,0:T(4,128)S(1)} %get-tuple-element.51.refs_0_), channel_id=1, source_target_pairs={{0,128},{128,256},{256,384},{1,129},{129,257},{257,385},{2,130},{1... | collective-permute-start | bytes 67592 | tf_op jit(solution)/shard_map/ppermute | solution.py:405
  34.6 0.0 copy-done
  34.6 0.9 %shard_map.113 = (bf16[256,128]{1,0:T(8,128)(2,1)S(1)}, f32[256,640]{1,0:T(8,128)S(1)}, f32[256,640]{1,0:T(8,128)S(1)}) custom-call(bf16[256,128]{1,0:T(8,128)(2,1)S(1)} %get-tuple-element.45.c_ref, bf16[8,256]{1,0:T(8,128)(2,1)S(1)} %collective-permute-done.halo_ref, f32[4,256]{1,0:T(4,128)S(1)} %get-tuple-element.38.taps_ref, ...), custom_call_target="tpu_custom_call" | custom-call | flops 20000000000 | bytes 1000000 | tf_op jit(solution)/shard_map/pallas_call | solution.py:26
  35.5 0.0 collective-permute-done.1.refs_1_.refs_0_
  35.5 0.1 shard_map.114
  35.6 9.7 %collective-permute-start.2 = (f32[4,1408]{1,0:T(4,128)S(1)}, f32[4,1408]{1,0:T(4,128)S(1)}, u32[]{:S(2)}, u32[]{:S(2)}) collective-permute-start(f32[4,1408]{1,0:T(4,128)S(1)} %shard_map.114), channel_id=1, source_target_pairs={{0,256},{128,384},{1,257},{129,385},{2,258},{130,386},{3,259},{131... | collective-permute-start | bytes 67592 | tf_op jit(solution)/shard_map/ppermute | solution.py:408
  45.4 1.4 %shard_map.115 = (bf16[256,128]{1,0:T(8,128)(2,1)}, f32[256,640]{1,0:T(8,128)S(1)}, f32[256,640]{1,0:T(8,128)S(1)}) custom-call(bf16[256,128]{1,0:T(8,128)(2,1)S(1)} %get-tuple-element.45.c_ref, bf16[8,256]{1,0:T(8,128)(2,1)S(1)} %collective-permute-done.halo_ref, f32[4,256]{1,0:T(4,128)S(1)} %get-tuple-element.38.taps_ref, ...), custom_call_target="tpu_custom_call" | custom-call | flops 20000000000 | bytes 1000000 | tf_op jit(solution)/shard_map/pallas_call | solution.py:26
  46.8 0.0 collective-permute-done.2.refs_1_
  46.8 0.4 shard_map.116
  47.2 13.7 %all_to_all.11.state_ref = bf16[32,4,1280]{2,1,0:T(4,128)(2,1)S(1)} all-to-all(bf16[32,4,1280]{2,1,0:T(4,128)(2,1)S(1)} %shard_map.116), channel_id=1, replica_groups=mesh['za'=4,'zb'=2,'y'=4,'x'=4,'tp'=4] {'zb','y','x'}, dimensions={0} | all-to-all | bytes 655360 | tf_op jit(solution)/shard_map/all_to_all | solution.py:416
  60.9 0.7 shard_map.117
  61.6 17.3 %all-gather.1.squares_ref = f32[4,1,256]{2,1,0:T(1,128)S(1)} all-gather(f32[1,1,256]{2,1,0:T(1,128)S(1)} %bitcast.6), channel_id=2, replica_groups=mesh['za'=4,'zb'=2,'y'=4,'x'=4,'tp'=4] {'tp'}, dimensions={0}, use_global_device_ids=true | all-gather | bytes 5120 | tf_op jit(solution)/shard_map/all_gather | solution.py:423
  78.9 1.3 %shard_map.118 = bf16[256,1280]{1,0:T(8,128)(2,1)} custom-call(f32[4,1,256]{2,1,0:T(1,128)S(1)} %all-gather.1.squares_ref, f32[256,1280]{1,0:T(8,128)S(1)} %get-tuple-element.65.gated_ref, f32[1,1280]{1,0:T(1,128)S(1)} %get-tuple-element.66.gain_ref), custom_call_target="tpu_custom_call" | custom-call | flops 1000000 | bytes 1000000 | tf_op jit(solution)/shard_map/pallas_call | solution.py:26
Async XLA Ops:
  2.6 5.7 %collective-permute-start = (bf16[8,256]{1,0:T(8,128)(2,1)S(1)}, bf16[8,256]{1,0:T(8,128)(2,1)S(1)}, u32[]{:S(2)}, u32[]{:S(2)}) collective-permute-start(bf16[8,256]{1,0:T(8,128)(2,1)S(1)} %get-tuple-element.37), channel_id=1, source_target_pairs={{0,4},{4,8},{8,12},{12,16},{16,20},{20,24},{24,28},{28,32},{32,36}... | collective-permute-start | bytes 12296 | tf_op jit(solution)/shard_map/ppermute | solution.py:362
  8.6 26.0 %copy-start = (bf16[256,1280]{1,0:T(8,128)(2,1)S(1)}, bf16[256,1280]{1,0:T(8,128)(2,1)}, u32[]{:S(2)}) copy-start(bf16[256,1280]{1,0:T(8,128)(2,1)} %gate_ref.3) | copy-start | bytes 1966084
  29.7 5.8 %collective-permute-start.1 = (f32[4,1408]{1,0:T(4,128)S(1)}, f32[4,1408]{1,0:T(4,128)S(1)}, u32[]{:S(2)}, u32[]{:S(2)}) collective-permute-start(f32[4,1408]{1,0:T(4,128)S(1)} %get-tuple-element.51.refs_0_), channel_id=1, source_target_pairs={{0,128},{128,256},{256,384},{1,129},{129,257},{257,385},{2,130},{1... | collective-permute-start | bytes 67592 | tf_op jit(solution)/shard_map/ppermute | solution.py:405
  35.6 11.1 %collective-permute-start.2 = (f32[4,1408]{1,0:T(4,128)S(1)}, f32[4,1408]{1,0:T(4,128)S(1)}, u32[]{:S(2)}, u32[]{:S(2)}) collective-permute-start(f32[4,1408]{1,0:T(4,128)S(1)} %shard_map.114), channel_id=1, source_target_pairs={{0,256},{128,384},{1,257},{129,385},{2,258},{130,386},{3,259},{131... | collective-permute-start | bytes 67592 | tf_op jit(solution)/shard_map/ppermute | solution.py:408

commit v3 on v2

--- a/solution.py
+++ b/solution.py
@@ -49,9 +49,7 @@
     return spread
 
 
-def load_kernel(b_ref, c_ref, *refs):
-    count = (len(refs) - 2) // 2
-    sources, tails_ref, targets, sems = refs[:count], refs[count], refs[count + 1 : -1], refs[-1]
+def tails_kernel(b_ref, c_ref, tails_ref, sems):
     tokens, state = b_ref.shape
     copies = [
         pltpu.make_async_copy(
@@ -59,8 +57,6 @@
         )
         for k, r in enumerate((b_ref, c_ref))
     ]
-    for k, (source, target) in enumerate(zip(sources, targets)):
-        copies.append(pltpu.make_async_copy(source, target, sems.at[k + 2]))
     for copy in copies:
         copy.start()
     for copy in copies:
@@ -94,11 +90,23 @@
 WEIGHTS_AT = 32
 
 
-def prepare_kernel(
-    x_ref, raw_ref, bias_ref, rate_ref, docs_ref, b_ref, c_ref, taps_ref, taps_bias_ref,
-    weighted_ref, cum_rows_ref, step_rows_ref, columns_ref, factor_ref, start_ref, b_conv_ref,
-    c_conv_ref, stack_ref, padded_ref,
-):
+def prepare_kernel(*refs):
+    count, early = 10, 4
+    sources, kept, results = refs[:count], refs[count : 2 * count - early], refs[2 * count - early :]
+    (
+        weighted_ref, cum_rows_ref, step_rows_ref, columns_ref, factor_ref, start_ref, b_conv_ref,
+        c_conv_ref, stack_ref, padded_ref, sems, docs_ref, raw_ref, bias_ref, rate_ref,
+    ) = results
+    targets = (docs_ref, raw_ref, bias_ref, rate_ref, *kept)
+    x_ref, b_ref, c_ref, taps_ref, taps_bias_ref, _ = kept
+    copies = [
+        pltpu.make_async_copy(source, target, sems.at[k])
+        for k, (source, target) in enumerate(zip(sources, targets))
+    ]
+    for copy in copies:
+        copy.start()
+    for copy in copies[:early]:
+        copy.wait()
     heads, tokens = raw_ref.shape
     state = b_ref.shape[1]
     width = x_ref.shape[1] // heads
@@ -134,6 +142,8 @@
     columns = stack_ref[...].T
     columns_ref[...] = columns
     factor_ref[...] = jnp.where(end_start < 0, jnp.exp(columns[tokens - 1 : tokens, :]), 0.0)
+    for copy in copies[early:]:
+        copy.wait()
     for j in range(x_ref.shape[1] // LANES):
         tile = slice(j * LANES, (j + 1) * LANES)
         weighted_ref[:, tile] = (
@@ -212,11 +222,12 @@
     joined_ref[:, features:] = own_ref[:, features:] * behind_ref[:, features:]
 
 
-def states_in_kernel(heads, near_ref, far_ref, before_ref, factors_ref, state_ref, wide_ref):
+def states_in_kernel(heads, near_ref, far_a_ref, far_b_ref, before_ref, factors_ref, state_ref, wide_ref):
     members, rows, features = before_ref.shape
     width = features // heads
     factor = wide_factor(near_ref, features, width)
-    entering = factor * far_ref[:, 0:features] + near_ref[:, 0:features]
+    far = far_a_ref[:, 0:features] + far_b_ref[:, 0:features]
+    entering = factor * far + near_ref[:, 0:features]
     factors = factors_ref[...]
     for j in range(features // LANES):
         wide_ref[:, j * LANES : (j + 1) * LANES] = tile_of_heads(factors, j, width)
@@ -224,14 +235,11 @@
         state_ref[m] = (wide_ref[m : m + 1, :] * entering + before_ref[m]).astype(jnp.bfloat16)
 
 
-def diagonal_kernel(
-    first_head, c_ref, halo_ref, taps_ref, taps_bias_ref, start_ref, c_early_ref, b_conv_ref,
-    columns_ref, cum_rows_ref, step_rows_ref, x_ref, gate_ref, c_conv_ref, gated_ref, scale_ref,
-    padded_ref, products_ref,
+def products_of(
+    c_ref, halo_ref, taps_ref, taps_bias_ref, start_ref, c_early_ref, b_conv_ref, c_conv_ref,
+    products_ref, padded_ref,
 ):
     tokens, state = c_ref.shape
-    features, heads = x_ref.shape[1], cum_rows_ref.shape[0]
-    width, half = features // heads, tokens // 2
     first = first_rows(
         c_ref, halo_ref[:, state:], taps_ref[:, state:], taps_bias_ref[:, state:], start_ref,
         padded_ref,
@@ -245,11 +253,18 @@
     )
     row = lax.broadcasted_iota(jnp.int32, (tokens, tokens), 0)
     col = lax.broadcasted_iota(jnp.int32, (tokens, tokens), 1)
-    start = start_ref[...]
-    starts = jnp.concatenate([start] * (tokens // LANES), axis=1)
+    starts = jnp.concatenate([start_ref[...]] * (tokens // LANES), axis=1)
     products_ref[...] = jnp.where((col <= row) & (col >= starts), products, 0.0)
+
+
+def diagonal_of(
+    first_head, start_ref, columns_ref, cum_rows_ref, step_rows_ref, x_ref, gate_ref, products_ref,
+    gated_ref, scale_ref,
+):
+    tokens, features = x_ref.shape
+    width, half = features // cum_rows_ref.shape[0], tokens // 2
     columns = columns_ref[...]
-    carried = jnp.where(start < 0, jnp.exp(columns), 0.0)
+    carried = jnp.where(start_ref[...] < 0, jnp.exp(columns), 0.0)
     lane = lax.broadcasted_iota(jnp.int32, (tokens, LANES), 1)
     per = LANES // width
     for i in range(gated_ref.shape[1] // LANES):
@@ -286,6 +301,16 @@
         scale_ref[:, here] = tile_of_heads(carried, j, width) * gate
 
 
+def early_diagonal_kernel(*refs):
+    (*sources, columns_ref, cum_rows_ref, step_rows_ref, x_ref, gate_ref) = refs[:12]
+    c_conv_ref, products_ref, gated_ref, scale_ref, padded_ref = refs[12:]
+    products_of(*sources, c_conv_ref, products_ref, padded_ref)
+    diagonal_of(
+        0, sources[4], columns_ref, cum_rows_ref, step_rows_ref, x_ref, gate_ref, products_ref,
+        gated_ref, scale_ref,
+    )
+
+
 def gate_kernel(
     state_ref, c_conv_ref, diagonal_a_ref, scale_a_ref, diagonal_b_ref, scale_b_ref, gated_ref,
     squares_ref, rows_ref,
@@ -328,7 +353,8 @@
     scale = lax.rsqrt(column / features_all + epsilon)
     for j in range(gated_ref.shape[1] // LANES):
         tile = slice(j * LANES, (j + 1) * LANES)
-        out_ref[:, tile] = (gated_ref[:, tile] * scale * gain_ref[:, tile]).astype(jnp.bfloat16)
+        gain = gain_ref[j : j + 1, :]
+        out_ref[:, tile] = (gated_ref[:, tile] * scale * gain).astype(jnp.bfloat16)
 
 
 def body(
@@ -347,32 +373,35 @@
     ahead = lambda n, k: [(i, i + k) for i in range(n - k)]
 
     bf16 = jnp.bfloat16
+    tails = call(
+        tails_kernel, out((8, 2 * state), bf16), b_source, c_source,
+        hbm=2, scratch=[pltpu.SemaphoreType.DMA((2,))],
+    )
+    halo = lax.ppermute(tails, SEQ, ahead(shards, 1))
     operands = [
-        inputs, step_raw.T, step_bias[None, :], decay_rate[None, :], doc_lengths[None, :],
-        b_source, c_source, conv_weight, conv_bias[None, :], norm_gain[None, :],
+        doc_lengths[None, :], step_raw.T, step_bias[None, :], decay_rate[None, :], inputs,
+        b_source, c_source, conv_weight, conv_bias[None, :],
+        norm_gain.reshape(features // LANES, LANES),
     ]
-    tails, *loaded = call(
-        load_kernel,
-        [out((8, 2 * state), bf16)] + [out(o.shape, o.dtype) for o in operands],
-        b_source, c_source, *operands,
-        hbm=2 + len(operands),
-        scratch=[pltpu.SemaphoreType.DMA((2 + len(operands),))],
-    )
-    x, raw, bias, rate, docs, b, c, taps, taps_bias, gain = loaded
-    halo = lax.ppermute(tails, SEQ, ahead(shards, 1))
-    weighted, cum_rows, step_rows, columns, factor, start, b_early, c_early = call(
+    results = call(
         prepare_kernel,
-        [
+        [out(o.shape, o.dtype) for o in operands[4:]]
+        + [
             out((tokens, features), bf16), out((heads, tokens)), out((heads, tokens)),
             out((tokens, LANES)), out((1, LANES)), out((tokens, LANES), jnp.int32),
             out((tokens, state)), out((tokens, state)),
         ],
-        x, raw, bias, rate, docs, b, c, taps, taps_bias,
+        *operands,
+        hbm=len(operands), after=(tails,),
         scratch=[
             pltpu.VMEM((LANES, tokens), jnp.float32),
             pltpu.VMEM((tokens + 8, state), jnp.float32),
+            pltpu.SemaphoreType.DMA((len(operands),)),
+            *(pltpu.VMEM(o.shape, o.dtype) for o in operands[:4]),
         ],
     )
+    x, b, c, taps, taps_bias, gain = results[0:6]
+    weighted, cum_rows, step_rows, columns, factor, start, b_early, c_early = results[6:]
     pieces, b_conv = call(
         states_kernel,
         [out((members, rows, features + LANES)), out((tokens, state), bf16)],
@@ -390,27 +419,27 @@
         ],
     )
 
-    def diagonal_part(first_head):
-        return call(
-            functools.partial(diagonal_kernel, first_head),
-            [out((tokens, state), bf16), out((tokens, features // 2)), out((tokens, features // 2))],
-            c, halo, taps, taps_bias, start, c_early, b_conv, columns, cum_rows, step_rows, x,
-            gate_input, flops=20_000_000_000,
-            scratch=[
-                pltpu.VMEM((16, state), jnp.float32),
-                pltpu.VMEM((tokens, tokens), jnp.float32),
-            ],
-        )
-
     near = lax.ppermute(total, OUTER, ahead(outer, 1))
-    c_conv, diagonal_a, scale_a = diagonal_part(0)
+    part = out((tokens, features // 2))
+    c_conv, products, diagonal_a, scale_a = call(
+        early_diagonal_kernel,
+        [out((tokens, state), bf16), out((tokens, tokens)), part, part],
+        c, halo, taps, taps_bias, start, c_early, b_conv, columns, cum_rows, step_rows, x,
+        gate_input,
+        scratch=[pltpu.VMEM((16, state), jnp.float32)],
+    )
     joined = call(functools.partial(join_kernel, heads), out(total.shape), total, near, after=(c_conv,))
-    far = lax.ppermute(joined, OUTER, ahead(outer, 2))
-    _, diagonal_b, scale_b = diagonal_part(heads // 2)
+    far_a = lax.ppermute(joined, OUTER, [(1, 3)])
+    far_b = lax.ppermute(near, OUTER, [(1, 2)])
+    diagonal_b, scale_b = call(
+        functools.partial(diagonal_of, heads // 2), [part, part],
+        start, columns, cum_rows, step_rows, x, gate_input, products,
+        flops=20_000_000_000,
+    )
     states_in = call(
         functools.partial(states_in_kernel, heads),
         out((members, rows, features), bf16),
-        near, far, before, factors, after=(diagonal_b, scale_b),
+        near, far_a, far_b, before, factors, after=(diagonal_b, scale_b),
         scratch=[pltpu.VMEM((members, features), jnp.float32)],
     )
     states_in = lax.all_to_all(states_in, GROUP, 0, 0)

time: 80.5 us -> 79.3 us (0.985)
  the two profiles are of different devices: /device:TPU:1 before, /device:TPU:65 now
where the time goes in v3:
time: 79.3 us; the launch traced here: 79 us
  blocking collectives  51.1 us (64%)
  starting transfers between devices  16.6 us (21%)
  Pallas kernels  8.18 us (10%)
  waiting for transfers between devices  3.06 us (4%)
    all_to_all x1, blocking collectives, body(): pieces = lax.all_to_all(pieces, GROUP, 0, 0)  18.2 us
    all_gather x1, blocking collectives, body(): squares = lax.all_gather(squares, 'tp')  17.8 us
    all_to_all x1, blocking collectives, body(): states_in = lax.all_to_all(states_in, GROUP, 0, 0)  15 us
    pallas_call x10, Pallas kernels, call(): pl.pallas_call(kernel, out_shape=list(outs) if multiple else outs, in_spe...  8.18 us
    ppermute x1, starting transfers between devices, body(): far_a = lax.ppermute(joined, OUTER, [(1, 3)])  7.14 us
    ppermute x1, starting transfers between devices, body(): near = lax.ppermute(total, OUTER, ahead(outer, 1))  5.06 us
    ppermute x1, starting transfers between devices, body(): halo = lax.ppermute(tails, SEQ, ahead(shards, 1))  3.12 us
    ppermute x1, waiting for transfers between devices, body(): halo = lax.ppermute(tails, SEQ, ahead(shards, 1))  3.05 us
  transfers between devices with their start and end apart: 4, of which 1 were waited for; matrix products, arithmetic and copies ran while one was open for 0% of the time, Pallas kernels for 5%

profile of v3, /device:TPU:65, one launch (start us, length us, event | category | flops | bytes accessed | tf_op | source)
XLA Modules:
  0.0 79.0 jit_solution(15587865307436872064)
XLA Ops:
  0.0 0.7 shard_map.109.refs_10_
  0.7 3.1 %collective-permute-start = (bf16[8,256]{1,0:T(8,128)(2,1)S(1)}, bf16[8,256]{1,0:T(8,128)(2,1)S(1)}, u32[]{:S(2)}, u32[]{:S(2)}) collective-permute-start(bf16[8,256]{1,0:T(8,128)(2,1)S(1)} %shard_map.109.refs_10_), channel_id=1, source_target_pairs={{0,4},{4,8},{8,12},{12,16},{16,20},{20,24},{24,28},{28,32},{32,36}... | collective-permute-start | bytes 12296 | tf_op jit(solution)/shard_map/ppermute | solution.py:380
  3.8 2.4 %shard_map.110 = (bf16[256,1280]{1,0:T(8,128)(2,1)S(1)}, bf16[256,128]{1,0:T(8,128)(2,1)S(1)}, bf16[256,128]{1,0:T(8,128)(2,1)S(1)}, f32[4,256]{1,0:T(4,128)S(1)...) custom-call(s32[1,8]{1,0:T(1,128)} %bitcast.11, ...), custom_call_target="tpu_custom_call" | custom-call | flops 1000000 | bytes 1000000 | tf_op jit(solution)/shard_map/pallas_call | solution.py:26
  6.2 3.1 %collective-permute-done.halo_ref.refs_1_ = bf16[8,256]{1,0:T(8,128)(2,1)S(1)} collective-permute-done((bf16[8,256]{1,0:T(8,128)(2,1)S(1)}, bf16[8,256]{1,0:T(8,128)(2,1)S(1)}, u32[]{:S(2)}, u32[]{:S(2)}) %collective-permute-start) | collective-permute-done | bytes 4128 | tf_op jit(solution)/shard_map/ppermute | solution.py:380
  9.3 0.3 shard_map.111
  9.6 0.0 copy-start
  9.6 18.2 %all_to_all.10.pieces_ref = f32[32,4,1408]{2,1,0:T(4,128)S(1)} all-to-all(f32[32,4,1408]{2,1,0:T(4,128)S(1)} %get-tuple-element.39), channel_id=1, replica_groups=mesh['za'=4,'zb'=2,'y'=4,'x'=4,'tp'=4] {'zb','y','x'}, dimensions={0} | all-to-all | bytes 1441792 | tf_op jit(solution)/shard_map/all_to_all | solution.py:411
  27.9 0.3 shard_map.112
  28.2 5.1 %collective-permute-start.1 = (f32[4,1408]{1,0:T(4,128)S(1)}, f32[4,1408]{1,0:T(4,128)S(1)}, u32[]{:S(2)}, u32[]{:S(2)}) collective-permute-start(f32[4,1408]{1,0:T(4,128)S(1)} %get-tuple-element.40.refs_0_), channel_id=1, source_target_pairs={{0,128},{128,256},{256,384},{1,129},{129,257},{257,385},{2,130},{1... | collective-permute-start | bytes 67592 | tf_op jit(solution)/shard_map/ppermute | solution.py:422
  33.3 0.0 copy-done
  33.3 1.0 %shard_map.113 = (bf16[256,128]{1,0:T(8,128)(2,1)S(1)}, f32[256,256]{1,0:T(8,128)S(1)}, f32[256,640]{1,0:T(8,128)S(1)}, f32[256,640]{1,0:T(8,128)S(1)}) custom-call(bf16[256,128]{1,0:T(8,128)(2,1)S(1)} %get-tuple-element.41.refs_0_, bf16[8,256]{1,0:T(8,128)(2,1)S(1)} %collective-permute-done.halo_ref.refs_1_, ...), custom_call_target="tpu_custom_call" | custom-call | flops 1000000 | bytes 1000000 | tf_op jit(solution)/shard_map/pallas_call | solution.py:26
  34.3 0.0 collective-permute-done.1.refs_1_.refs_0_
  34.3 0.1 shard_map.114
  34.4 7.1 %collective-permute-start.2 = (f32[4,1408]{1,0:T(4,128)S(1)}, f32[4,1408]{1,0:T(4,128)S(1)}, u32[]{:S(2)}, u32[]{:S(2)}) collective-permute-start(f32[4,1408]{1,0:T(4,128)S(1)} %shard_map.114), channel_id=1, source_target_pairs={{128,384},{129,385},{130,386},{131,387},{132,388},{133,389},{134,3... | collective-permute-start | bytes 67592 | tf_op jit(solution)/shard_map/ppermute | solution.py:432
  41.5 1.3 %collective-permute-start.3 = (f32[4,1408]{1,0:T(4,128)S(1)}, f32[4,1408]{1,0:T(4,128)S(1)}, u32[]{:S(2)}, u32[]{:S(2)}) collective-permute-start(f32[4,1408]{1,0:T(4,128)S(1)} %collective-permute-done.1.refs_1_.refs_0_), channel_id=1, source_target_pairs={{128,256},{129,257},{130,258},{131,259},{132,260},{133,261},{134,2... | collective-permute-start | bytes 67592 | tf_op jit(solution)/shard_map/ppermute | solution.py:433
  42.8 1.0 %shard_map.115 = (f32[256,640]{1,0:T(8,128)S(1)}, f32[256,640]{1,0:T(8,128)S(1)}) custom-call(s32[256,128]{1,0:T(8,128)S(1)} %get-tuple-element.35.start_ref.refs_4_, f32[256,128]{1,0:T(8,128)S(1)} %get-tuple-element.44.refs_7_.columns_ref, f32[20,256]{1,0:T(8,128)S(1)} %get-tuple-element.45.refs_8_.cum_rows_ref, ...), custom_call_target="tpu_custom_call" | custom-call | flops 20000000000 | bytes 1000000 | tf_op jit(solution)/shard_map/pallas_call | solution.py:26
  43.8 0.0 collective-permute-done.2.refs_1_
  43.8 0.0 collective-permute-done.3.refs_2_
  43.8 0.4 shard_map.116
  44.2 15.0 %all_to_all.11.state_ref = bf16[32,4,1280]{2,1,0:T(4,128)(2,1)S(1)} all-to-all(bf16[32,4,1280]{2,1,0:T(4,128)(2,1)S(1)} %shard_map.116), channel_id=1, replica_groups=mesh['za'=4,'zb'=2,'y'=4,'x'=4,'tp'=4] {'zb','y','x'}, dimensions={0} | all-to-all | bytes 655360 | tf_op jit(solution)/shard_map/all_to_all | solution.py:445
  59.3 0.7 shard_map.117
  60.0 17.8 %all-gather.1.squares_ref = f32[4,1,256]{2,1,0:T(1,128)S(1)} all-gather(f32[1,1,256]{2,1,0:T(1,128)S(1)} %bitcast.7), channel_id=2, replica_groups=mesh['za'=4,'zb'=2,'y'=4,'x'=4,'tp'=4] {'tp'}, dimensions={0}, use_global_device_ids=true | all-gather | bytes 5120 | tf_op jit(solution)/shard_map/all_gather | solution.py:452
  77.7 1.3 %shard_map.118 = bf16[256,1280]{1,0:T(8,128)(2,1)} custom-call(f32[4,1,256]{2,1,0:T(1,128)S(1)} %all-gather.1.squares_ref, f32[256,1280]{1,0:T(8,128)S(1)} %get-tuple-element.57.gated_ref, f32[10,128]{1,0:T(8,128)S(1)} %get-tuple-element.58.gain_ref), custom_call_target="tpu_custom_call" | custom-call | flops 1000000 | bytes 1000000 | tf_op jit(solution)/shard_map/pallas_call | solution.py:26
Async XLA Ops:
  0.7 8.6 %collective-permute-start = (bf16[8,256]{1,0:T(8,128)(2,1)S(1)}, bf16[8,256]{1,0:T(8,128)(2,1)S(1)}, u32[]{:S(2)}, u32[]{:S(2)}) collective-permute-start(bf16[8,256]{1,0:T(8,128)(2,1)S(1)} %shard_map.109.refs_10_), channel_id=1, source_target_pairs={{0,4},{4,8},{8,12},{12,16},{16,20},{20,24},{24,28},{28,32},{32,36}... | collective-permute-start | bytes 12296 | tf_op jit(solution)/shard_map/ppermute | solution.py:380
  9.6 23.7 %copy-start = (bf16[256,1280]{1,0:T(8,128)(2,1)S(1)}, bf16[256,1280]{1,0:T(8,128)(2,1)}, u32[]{:S(2)}) copy-start(bf16[256,1280]{1,0:T(8,128)(2,1)} %gate_ref.1) | copy-start | bytes 1966084
  28.2 6.1 %collective-permute-start.1 = (f32[4,1408]{1,0:T(4,128)S(1)}, f32[4,1408]{1,0:T(4,128)S(1)}, u32[]{:S(2)}, u32[]{:S(2)}) collective-permute-start(f32[4,1408]{1,0:T(4,128)S(1)} %get-tuple-element.40.refs_0_), channel_id=1, source_target_pairs={{0,128},{128,256},{256,384},{1,129},{129,257},{257,385},{2,130},{1... | collective-permute-start | bytes 67592 | tf_op jit(solution)/shard_map/ppermute | solution.py:422
  34.4 9.4 %collective-permute-start.2 = (f32[4,1408]{1,0:T(4,128)S(1)}, f32[4,1408]{1,0:T(4,128)S(1)}, u32[]{:S(2)}, u32[]{:S(2)}) collective-permute-start(f32[4,1408]{1,0:T(4,128)S(1)} %shard_map.114), channel_id=1, source_target_pairs={{128,384},{129,385},{130,386},{131,387},{132,388},{133,389},{134,3... | collective-permute-start | bytes 67592 | tf_op jit(solution)/shard_map/ppermute | solution.py:432
  41.5 2.3 %collective-permute-start.3 = (f32[4,1408]{1,0:T(4,128)S(1)}, f32[4,1408]{1,0:T(4,128)S(1)}, u32[]{:S(2)}, u32[]{:S(2)}) collective-permute-start(f32[4,1408]{1,0:T(4,128)S(1)} %collective-permute-done.1.refs_1_.refs_0_), channel_id=1, source_target_pairs={{128,256},{129,257},{130,258},{131,259},{132,260},{133,261},{134,2... | collective-permute-start | bytes 67592 | tf_op jit(solution)/shard_map/ppermute | solution.py:433

commit v4 on v3

--- a/solution.py
+++ b/solution.py
@@ -222,12 +222,15 @@
     joined_ref[:, features:] = own_ref[:, features:] * behind_ref[:, features:]
 
 
-def states_in_kernel(heads, near_ref, far_a_ref, far_b_ref, before_ref, factors_ref, state_ref, wide_ref):
+def states_in_kernel(
+    heads, first_ref, second_ref, far_a_ref, far_b_ref, before_ref, factors_ref, state_ref, wide_ref
+):
     members, rows, features = before_ref.shape
     width = features // heads
-    factor = wide_factor(near_ref, features, width)
+    factor = wide_factor(second_ref, features, width)
     far = far_a_ref[:, 0:features] + far_b_ref[:, 0:features]
-    entering = factor * far + near_ref[:, 0:features]
+    near = first_ref[:, 0:features] + second_ref[:, 0:features]
+    entering = factor * far + near
     factors = factors_ref[...]
     for j in range(features // LANES):
         wide_ref[:, j * LANES : (j + 1) * LANES] = tile_of_heads(factors, j, width)
@@ -258,8 +261,8 @@
 
 
 def diagonal_of(
-    first_head, start_ref, columns_ref, cum_rows_ref, step_rows_ref, x_ref, gate_ref, products_ref,
-    gated_ref, scale_ref,
+    start_ref, columns_ref, cum_rows_ref, step_rows_ref, x_ref, gate_ref, products_ref, gated_ref,
+    scale_ref,
 ):
     tokens, features = x_ref.shape
     width, half = features // cum_rows_ref.shape[0], tokens // 2
@@ -267,10 +270,8 @@
     carried = jnp.where(start_ref[...] < 0, jnp.exp(columns), 0.0)
     lane = lax.broadcasted_iota(jnp.int32, (tokens, LANES), 1)
     per = LANES // width
-    for i in range(gated_ref.shape[1] // LANES):
-        j = first_head // per + i
+    for j in range(features // LANES):
         tile = slice(j * LANES, (j + 1) * LANES)
-        here = slice(i * LANES, (i + 1) * LANES)
         diagonal = None
         for k in range(per):
             h = j * per + k
@@ -297,40 +298,34 @@
             diagonal = part if diagonal is None else jnp.where(lane < k * width, diagonal, part)
         gate = gate_ref[:, tile].astype(jnp.float32)
         gate = gate * jax.nn.sigmoid(gate)
-        gated_ref[:, here] = diagonal * gate
-        scale_ref[:, here] = tile_of_heads(carried, j, width) * gate
-
-
-def early_diagonal_kernel(*refs):
+        gated_ref[:, tile] = diagonal * gate
+        scale_ref[:, tile] = tile_of_heads(carried, j, width) * gate
+
+
+def diagonal_kernel(*refs):
     (*sources, columns_ref, cum_rows_ref, step_rows_ref, x_ref, gate_ref) = refs[:12]
-    c_conv_ref, products_ref, gated_ref, scale_ref, padded_ref = refs[12:]
+    c_conv_ref, gated_ref, scale_ref, products_ref, padded_ref = refs[12:]
     products_of(*sources, c_conv_ref, products_ref, padded_ref)
     diagonal_of(
-        0, sources[4], columns_ref, cum_rows_ref, step_rows_ref, x_ref, gate_ref, products_ref,
+        sources[4], columns_ref, cum_rows_ref, step_rows_ref, x_ref, gate_ref, products_ref,
         gated_ref, scale_ref,
     )
 
 
 def gate_kernel(
-    state_ref, c_conv_ref, diagonal_a_ref, scale_a_ref, diagonal_b_ref, scale_b_ref, gated_ref,
-    squares_ref, rows_ref,
+    state_ref, c_conv_ref, diagonal_ref, scale_ref, gated_ref, squares_ref, rows_ref
 ):
     members, rows, features = state_ref.shape
     for m in range(members):
         rows_ref[m * rows : (m + 1) * rows, :] = state_ref[m].astype(jnp.float32)
     c_conv = c_conv_ref[...]
     squares = jnp.zeros((c_conv.shape[0], LANES), jnp.float32)
-    parts = diagonal_a_ref.shape[1] // LANES
     for j in range(features // LANES):
         tile = slice(j * LANES, (j + 1) * LANES)
-        diagonal_ref, scale_ref = (
-            (diagonal_a_ref, scale_a_ref) if j < parts else (diagonal_b_ref, scale_b_ref)
-        )
-        here = slice((j % parts) * LANES, (j % parts + 1) * LANES)
         carried = jnp.dot(
             c_conv, rows_ref[:, tile].astype(jnp.bfloat16), preferred_element_type=jnp.float32
         )
-        gated = diagonal_ref[:, here] + scale_ref[:, here] * carried
+        gated = diagonal_ref[:, tile] + scale_ref[:, tile] * carried
         gated_ref[:, tile] = gated
         squares = squares + gated * gated
     squares_ref[...] = lax.dot_general(
@@ -419,34 +414,32 @@
         ],
     )
 
-    near = lax.ppermute(total, OUTER, ahead(outer, 1))
-    part = out((tokens, features // 2))
-    c_conv, products, diagonal_a, scale_a = call(
-        early_diagonal_kernel,
-        [out((tokens, state), bf16), out((tokens, tokens)), part, part],
+    first = lax.ppermute(total, OUTER, [(0, 1)])
+    second = lax.ppermute(total, OUTER, [(1, 2), (2, 3)])
+    joined = call(functools.partial(join_kernel, heads), out(total.shape), total, first)
+    far_a = lax.ppermute(joined, OUTER, [(1, 3)])
+    far_b = lax.ppermute(first, OUTER, [(1, 2)])
+    c_conv, diagonal, scale = call(
+        diagonal_kernel,
+        [out((tokens, state), bf16), out((tokens, features)), out((tokens, features))],
         c, halo, taps, taps_bias, start, c_early, b_conv, columns, cum_rows, step_rows, x,
-        gate_input,
-        scratch=[pltpu.VMEM((16, state), jnp.float32)],
-    )
-    joined = call(functools.partial(join_kernel, heads), out(total.shape), total, near, after=(c_conv,))
-    far_a = lax.ppermute(joined, OUTER, [(1, 3)])
-    far_b = lax.ppermute(near, OUTER, [(1, 2)])
-    diagonal_b, scale_b = call(
-        functools.partial(diagonal_of, heads // 2), [part, part],
-        start, columns, cum_rows, step_rows, x, gate_input, products,
-        flops=20_000_000_000,
+        gate_input, after=(joined,), flops=20_000_000_000,
+        scratch=[
+            pltpu.VMEM((tokens, tokens), jnp.float32),
+            pltpu.VMEM((16, state), jnp.float32),
+        ],
     )
     states_in = call(
         functools.partial(states_in_kernel, heads),
         out((members, rows, features), bf16),
-        near, far_a, far_b, before, factors, after=(diagonal_b, scale_b),
+        first, second, far_a, far_b, before, factors, after=(diagonal, scale),
         scratch=[pltpu.VMEM((members, features), jnp.float32)],
     )
     states_in = lax.all_to_all(states_in, GROUP, 0, 0)
     gated, squares = call(
         gate_kernel,
         [out((tokens, features)), out((1, tokens))],
-        states_in, c_conv, diagonal_a, scale_a, diagonal_b, scale_b,
+        states_in, c_conv, diagonal, scale,
         scratch=[pltpu.VMEM((state, features), jnp.float32)],
     )
     squares = lax.all_gather(squares, "tp")

time: 79.3 us -> 75.5 us (0.952)
  starting transfers between devices: 16.6 us -> 14 us
  blocking collectives: 51.1 us -> 50 us
    ppermute x1, starting transfers between devices: 7.14 us -> 3.96 us  [body(): far_a = lax.ppermute(joined, OUTER, [(1, 3)])]
    all_gather x1, blocking collectives: 17.8 us -> 16.6 us  [body(): squares = lax.all_gather(squares, 'tp')]
    ppermute x2 -> x3, starting transfers between devices: 6.35 us -> 6.94 us  [the longest x1 4.09 us: body(): second = lax.ppermute(total, OUTER, [(1, 2), (2, 3)])]
    pallas_call x10 -> x9, Pallas kernels: 8.18 us -> 7.91 us  [call(): pl.pallas_call(kernel, out_shape=list(outs) if multiple else outs, in_spe...]
  transfers between devices with their start and end apart: 4 -> 5, of which waited for: 1 -> 2; matrix products, arithmetic and copies ran while one was open for 0% -> 0% of each run, Pallas kernels for 5% -> 6%
where the time goes in v4:
time: 75.5 us; the launch traced here: 75.2 us
  blocking collectives  50 us (66%)
  starting transfers between devices  14 us (19%)
  Pallas kernels  7.91 us (10%)
  waiting for transfers between devices  3.12 us (4%)
    all_to_all x1, blocking collectives, body(): pieces = lax.all_to_all(pieces, GROUP, 0, 0)  18.6 us
    all_gather x1, blocking collectives, body(): squares = lax.all_gather(squares, 'tp')  16.6 us
    all_to_all x1, blocking collectives, body(): states_in = lax.all_to_all(states_in, GROUP, 0, 0)  14.9 us
    pallas_call x9, Pallas kernels, call(): pl.pallas_call(kernel, out_shape=list(outs) if multiple else outs, in_spe...  7.91 us
    ppermute x1, starting transfers between devices, body(): second = lax.ppermute(total, OUTER, [(1, 2), (2, 3)])  4.09 us
    ppermute x1, starting transfers between devices, body(): far_a = lax.ppermute(joined, OUTER, [(1, 3)])  3.96 us
    ppermute x1, starting transfers between devices, body(): halo = lax.ppermute(tails, SEQ, ahead(shards, 1))  3.12 us
    ppermute x1, waiting for transfers between devices, body(): halo = lax.ppermute(tails, SEQ, ahead(shards, 1))  3.06 us
  transfers between devices with their start and end apart: 5, of which 2 were waited for; matrix products, arithmetic and copies ran while one was open for 0% of the time, Pallas kernels for 6%

profile of v4, /device:TPU:65, one launch (start us, length us, event | category | flops | bytes accessed | tf_op | source)
XLA Modules:
  0.0 75.2 jit_solution(17937495507646406085)
XLA Ops:
  0.0 0.7 shard_map.109.refs_10_
  0.7 3.1 %collective-permute-start = (bf16[8,256]{1,0:T(8,128)(2,1)S(1)}, bf16[8,256]{1,0:T(8,128)(2,1)S(1)}, u32[]{:S(2)}, u32[]{:S(2)}) collective-permute-start(bf16[8,256]{1,0:T(8,128)(2,1)S(1)} %shard_map.109.refs_10_), channel_id=1, source_target_pairs={{0,4},{4,8},{8,12},{12,16},{16,20},{20,24},{24,28},{28,32},{32,36}... | collective-permute-start | bytes 12296 | tf_op jit(solution)/shard_map/ppermute | solution.py:375
  3.8 2.4 %shard_map.110 = (bf16[256,1280]{1,0:T(8,128)(2,1)S(1)}, bf16[256,128]{1,0:T(8,128)(2,1)S(1)}, bf16[256,128]{1,0:T(8,128)(2,1)S(1)}, f32[4,256]{1,0:T(4,128)S(1)...) custom-call(s32[1,8]{1,0:T(1,128)} %bitcast.11, ...), custom_call_target="tpu_custom_call" | custom-call | flops 1000000 | bytes 1000000 | tf_op jit(solution)/shard_map/pallas_call | solution.py:26
  6.2 3.1 %collective-permute-done.halo_ref.refs_1_ = bf16[8,256]{1,0:T(8,128)(2,1)S(1)} collective-permute-done((bf16[8,256]{1,0:T(8,128)(2,1)S(1)}, bf16[8,256]{1,0:T(8,128)(2,1)S(1)}, u32[]{:S(2)}, u32[]{:S(2)}) %collective-permute-start) | collective-permute-done | bytes 4128 | tf_op jit(solution)/shard_map/ppermute | solution.py:375
  9.3 0.3 shard_map.111
  9.6 0.0 copy-start
  9.6 18.6 %all_to_all.10.pieces_ref = f32[32,4,1408]{2,1,0:T(4,128)S(1)} all-to-all(f32[32,4,1408]{2,1,0:T(4,128)S(1)} %get-tuple-element.36), channel_id=1, replica_groups=mesh['za'=4,'zb'=2,'y'=4,'x'=4,'tp'=4] {'zb','y','x'}, dimensions={0} | all-to-all | bytes 1441792 | tf_op jit(solution)/shard_map/all_to_all | solution.py:406
  28.2 0.3 shard_map.112
  28.5 1.3 %collective-permute-start.1 = (f32[4,1408]{1,0:T(4,128)S(1)}, f32[4,1408]{1,0:T(4,128)S(1)}, u32[]{:S(2)}, u32[]{:S(2)}) collective-permute-start(f32[4,1408]{1,0:T(4,128)S(1)} %get-tuple-element.37.own_ref), channel_id=1, source_target_pairs={{0,128},{1,129},{2,130},{3,131},{4,132},{5,133},{6,134},{7,135},{8... | collective-permute-start | bytes 67592 | tf_op jit(solution)/shard_map/ppermute | solution.py:417
  29.8 4.1 %collective-permute-start.2 = (f32[4,1408]{1,0:T(4,128)S(1)}, f32[4,1408]{1,0:T(4,128)S(1)}, u32[]{:S(2)}, u32[]{:S(2)}) collective-permute-start(f32[4,1408]{1,0:T(4,128)S(1)} %get-tuple-element.37.own_ref), channel_id=1, source_target_pairs={{128,256},{256,384},{129,257},{257,385},{130,258},{258,386},{131,2... | collective-permute-start | bytes 67592 | tf_op jit(solution)/shard_map/ppermute | solution.py:418
  33.9 0.1 collective-permute-done.1.behind_ref.refs_0_
  34.0 0.1 shard_map.113.refs_12_
  34.1 4.0 %collective-permute-start.3 = (f32[4,1408]{1,0:T(4,128)S(1)}, f32[4,1408]{1,0:T(4,128)S(1)}, u32[]{:S(2)}, u32[]{:S(2)}) collective-permute-start(f32[4,1408]{1,0:T(4,128)S(1)} %shard_map.113.refs_12_), channel_id=1, source_target_pairs={{128,384},{129,385},{130,386},{131,387},{132,388},{133,389},{134,3... | collective-permute-start | bytes 67592 | tf_op jit(solution)/shard_map/ppermute | solution.py:420
  38.1 1.6 %collective-permute-start.4 = (f32[4,1408]{1,0:T(4,128)S(1)}, f32[4,1408]{1,0:T(4,128)S(1)}, u32[]{:S(2)}, u32[]{:S(2)}) collective-permute-start(f32[4,1408]{1,0:T(4,128)S(1)} %collective-permute-done.1.behind_ref.refs_0_), channel_id=1, source_target_pairs={{128,256},{129,257},{130,258},{131,259},{132,260},{133,261},{134,2... | collective-permute-start | bytes 67592 | tf_op jit(solution)/shard_map/ppermute | solution.py:421
  39.6 0.0 copy-done
  39.7 1.7 %shard_map.114 = (bf16[256,128]{1,0:T(8,128)(2,1)S(1)}, f32[256,1280]{1,0:T(8,128)S(1)}, f32[256,1280]{1,0:T(8,128)S(1)}) custom-call(bf16[256,128]{1,0:T(8,128)(2,1)S(1)} %get-tuple-element.40.refs_0_, bf16[8,256]{1,0:T(8,128)(2,1)S(1)} %collective-permute-done.halo_ref.refs_1_, f32[4,256]{1,0:T(4,128)S(1)} %get-tuple-element.30.taps_ref.refs_2_, ...), custom_call_target="tpu_custom_call" | custom-call | flops 20000000000 | bytes 1000000 | tf_op jit(solution)/shard_map/pallas_call | solution.py:26
  41.3 0.0 collective-permute-done.2.refs_1_
  41.3 0.0 collective-permute-done.3.refs_2_
  41.3 0.0 collective-permute-done.4.refs_3_
  41.4 0.4 shard_map.115
  41.8 14.9 %all_to_all.11.state_ref = bf16[32,4,1280]{2,1,0:T(4,128)(2,1)S(1)} all-to-all(bf16[32,4,1280]{2,1,0:T(4,128)(2,1)S(1)} %shard_map.115), channel_id=1, replica_groups=mesh['za'=4,'zb'=2,'y'=4,'x'=4,'tp'=4] {'zb','y','x'}, dimensions={0} | all-to-all | bytes 655360 | tf_op jit(solution)/shard_map/all_to_all | solution.py:438
  56.6 0.7 shard_map.116
  57.3 16.6 %all-gather.1.squares_ref = f32[4,1,256]{2,1,0:T(1,128)S(1)} all-gather(f32[1,1,256]{2,1,0:T(1,128)S(1)} %bitcast.7), channel_id=2, replica_groups=mesh['za'=4,'zb'=2,'y'=4,'x'=4,'tp'=4] {'tp'}, dimensions={0}, use_global_device_ids=true | all-gather | bytes 5120 | tf_op jit(solution)/shard_map/all_gather | solution.py:445
  73.9 1.3 %shard_map.117 = bf16[256,1280]{1,0:T(8,128)(2,1)} custom-call(f32[4,1,256]{2,1,0:T(1,128)S(1)} %all-gather.1.squares_ref, f32[256,1280]{1,0:T(8,128)S(1)} %get-tuple-element.51.gated_ref, f32[10,128]{1,0:T(8,128)S(1)} %get-tuple-element.52.gain_ref), custom_call_target="tpu_custom_call" | custom-call | flops 1000000 | bytes 1000000 | tf_op jit(solution)/shard_map/pallas_call | solution.py:26
Async XLA Ops:
  0.7 8.6 %collective-permute-start = (bf16[8,256]{1,0:T(8,128)(2,1)S(1)}, bf16[8,256]{1,0:T(8,128)(2,1)S(1)}, u32[]{:S(2)}, u32[]{:S(2)}) collective-permute-start(bf16[8,256]{1,0:T(8,128)(2,1)S(1)} %shard_map.109.refs_10_), channel_id=1, source_target_pairs={{0,4},{4,8},{8,12},{12,16},{16,20},{20,24},{24,28},{28,32},{32,36}... | collective-permute-start | bytes 12296 | tf_op jit(solution)/shard_map/ppermute | solution.py:375
  9.6 30.0 %copy-start = (bf16[256,1280]{1,0:T(8,128)(2,1)S(1)}, bf16[256,1280]{1,0:T(8,128)(2,1)}, u32[]{:S(2)}) copy-start(bf16[256,1280]{1,0:T(8,128)(2,1)} %refs_11_.1) | copy-start | bytes 1966084
  28.5 5.4 %collective-permute-start.1 = (f32[4,1408]{1,0:T(4,128)S(1)}, f32[4,1408]{1,0:T(4,128)S(1)}, u32[]{:S(2)}, u32[]{:S(2)}) collective-permute-start(f32[4,1408]{1,0:T(4,128)S(1)} %get-tuple-element.37.own_ref), channel_id=1, source_target_pairs={{0,128},{1,129},{2,130},{3,131},{4,132},{5,133},{6,134},{7,135},{8... | collective-permute-start | bytes 67592 | tf_op jit(solution)/shard_map/ppermute | solution.py:417
  29.8 11.5 %collective-permute-start.2 = (f32[4,1408]{1,0:T(4,128)S(1)}, f32[4,1408]{1,0:T(4,128)S(1)}, u32[]{:S(2)}, u32[]{:S(2)}) collective-permute-start(f32[4,1408]{1,0:T(4,128)S(1)} %get-tuple-element.37.own_ref), channel_id=1, source_target_pairs={{128,256},{256,384},{129,257},{257,385},{130,258},{258,386},{131,2... | collective-permute-start | bytes 67592 | tf_op jit(solution)/shard_map/ppermute | solution.py:418
  34.1 7.2 %collective-permute-start.3 = (f32[4,1408]{1,0:T(4,128)S(1)}, f32[4,1408]{1,0:T(4,128)S(1)}, u32[]{:S(2)}, u32[]{:S(2)}) collective-permute-start(f32[4,1408]{1,0:T(4,128)S(1)} %shard_map.113.refs_12_), channel_id=1, source_target_pairs={{128,384},{129,385},{130,386},{131,387},{132,388},{133,389},{134,3... | collective-permute-start | bytes 67592 | tf_op jit(solution)/shard_map/ppermute | solution.py:420
  38.1 3.3 %collective-permute-start.4 = (f32[4,1408]{1,0:T(4,128)S(1)}, f32[4,1408]{1,0:T(4,128)S(1)}, u32[]{:S(2)}, u32[]{:S(2)}) collective-permute-start(f32[4,1408]{1,0:T(4,128)S(1)} %collective-permute-done.1.behind_ref.refs_0_), channel_id=1, source_target_pairs={{128,256},{129,257},{130,258},{131,259},{132,260},{133,261},{134,2... | collective-permute-start | bytes 67592 | tf_op jit(solution)/shard_map/ppermute | solution.py:421

commit v5 on v4

--- a/solution.py
+++ b/solution.py
@@ -18,7 +18,9 @@
 HBM = pl.BlockSpec(memory_space=pltpu.HBM)
 
 
-def call(kernel, outs, *args, hbm=0, after=(), scratch=(), flops=1_000_000):
+def call(
+    kernel, outs, *args, hbm=0, after=(), scratch=(), flops=1_000_000, aliases=None, to_hbm=False
+):
     if after:
         inner, skip = kernel, len(after)
         kernel = lambda *refs: inner(*refs[:len(args)], *refs[len(args) + skip:])
@@ -27,7 +29,8 @@
         kernel,
         out_shape=list(outs) if multiple else outs,
         in_specs=[HBM] * hbm + [VMEM] * (len(args) - hbm) + [VMEM] * len(after),
-        out_specs=[VMEM] * len(outs) if multiple else VMEM,
+        out_specs=[VMEM] * len(outs) if multiple else HBM if to_hbm else VMEM,
+        input_output_aliases=aliases or {},
         scratch_shapes=list(scratch),
         compiler_params=pltpu.CompilerParams(vmem_limit_bytes=24 * 1024 * 1024),
         cost_estimate=pl.CostEstimate(flops=flops, bytes_accessed=1_000_000, transcendentals=0),
@@ -49,7 +52,9 @@
     return spread
 
 
-def tails_kernel(b_ref, c_ref, tails_ref, sems):
+def tails_kernel(b_ref, c_ref, *refs):
+    count = (len(refs) - 2) // 2
+    sources, tails_ref, targets, sems = refs[:count], refs[count], refs[count + 1 : -1], refs[-1]
     tokens, state = b_ref.shape
     copies = [
         pltpu.make_async_copy(
@@ -57,6 +62,8 @@
         )
         for k, r in enumerate((b_ref, c_ref))
     ]
+    for k, (source, target) in enumerate(zip(sources, targets)):
+        copies.append(pltpu.make_async_copy(source, target, sems.at[k + 2]))
     for copy in copies:
         copy.start()
     for copy in copies:
@@ -91,22 +98,20 @@
 
 
 def prepare_kernel(*refs):
-    count, early = 10, 4
-    sources, kept, results = refs[:count], refs[count : 2 * count - early], refs[2 * count - early :]
+    count = 6
+    sources, (docs_ref, raw_ref, bias_ref, rate_ref, _) = refs[:count], refs[count : count + 5]
+    targets = refs[count + 5 : 2 * count + 5]
     (
         weighted_ref, cum_rows_ref, step_rows_ref, columns_ref, factor_ref, start_ref, b_conv_ref,
-        c_conv_ref, stack_ref, padded_ref, sems, docs_ref, raw_ref, bias_ref, rate_ref,
-    ) = results
-    targets = (docs_ref, raw_ref, bias_ref, rate_ref, *kept)
-    x_ref, b_ref, c_ref, taps_ref, taps_bias_ref, _ = kept
+        c_conv_ref, stack_ref, padded_ref, sems,
+    ) = refs[2 * count + 5 :]
+    x_ref, b_ref, c_ref, taps_ref, taps_bias_ref, _ = targets
     copies = [
         pltpu.make_async_copy(source, target, sems.at[k])
         for k, (source, target) in enumerate(zip(sources, targets))
     ]
     for copy in copies:
         copy.start()
-    for copy in copies[:early]:
-        copy.wait()
     heads, tokens = raw_ref.shape
     state = b_ref.shape[1]
     width = x_ref.shape[1] // heads
@@ -142,7 +147,7 @@
     columns = stack_ref[...].T
     columns_ref[...] = columns
     factor_ref[...] = jnp.where(end_start < 0, jnp.exp(columns[tokens - 1 : tokens, :]), 0.0)
-    for copy in copies[early:]:
+    for copy in copies:
         copy.wait()
     for j in range(x_ref.shape[1] // LANES):
         tile = slice(j * LANES, (j + 1) * LANES)
@@ -187,7 +192,9 @@
         pieces_ref[m, :, features:] = spread
 
 
-def prefix_kernel(heads, pieces_ref, before_ref, factors_ref, total_ref, single_ref, wide_ref):
+def prefix_kernel(
+    heads, pieces_ref, before_ref, factors_ref, total_a_ref, total_b_ref, single_ref, wide_ref
+):
     members, rows, padded = pieces_ref.shape
     features = padded - LANES
     width = features // heads
@@ -204,8 +211,9 @@
     for m in range(members):
         before_ref[m] = total
         total = wide_ref[m : m + 1, :] * total + pieces_ref[m, :, 0:features]
-    total_ref[:, 0:features] = total
-    total_ref[:, features:] = jnp.broadcast_to(product, (rows, LANES))
+    for total_ref in (total_a_ref, total_b_ref):
+        total_ref[:, 0:features] = total
+        total_ref[:, features:] = jnp.broadcast_to(product, (rows, LANES))
 
 
 def wide_factor(pair_ref, features, width):
@@ -302,14 +310,18 @@
         scale_ref[:, tile] = tile_of_heads(carried, j, width) * gate
 
 
-def diagonal_kernel(*refs):
+def diagonal_kernel(groups, *refs):
     (*sources, columns_ref, cum_rows_ref, step_rows_ref, x_ref, gate_ref) = refs[:12]
-    c_conv_ref, gated_ref, scale_ref, products_ref, padded_ref = refs[12:]
-    products_of(*sources, c_conv_ref, products_ref, padded_ref)
-    diagonal_of(
-        sources[4], columns_ref, cum_rows_ref, step_rows_ref, x_ref, gate_ref, products_ref,
-        gated_ref, scale_ref,
-    )
+    _, c_conv_ref, gated_ref, scale_ref, products_ref, padded_ref = refs[-6:]
+    place = lax.axis_index(OUTER)
+
+    @pl.when((place >= groups[0]) & (place <= groups[-1]))
+    def _():
+        products_of(*sources, c_conv_ref, products_ref, padded_ref)
+        diagonal_of(
+            sources[4], columns_ref, cum_rows_ref, step_rows_ref, x_ref, gate_ref, products_ref,
+            gated_ref, scale_ref,
+        )
 
 
 def gate_kernel(
@@ -334,8 +346,9 @@
     )[0:1]
 
 
-def normalize_kernel(features_all, squares_ref, gated_ref, gain_ref, out_ref):
+def normalize_kernel(features_all, squares_ref, gated_ref, gain_ref, out_ref, rows_ref, sems):
     count = squares_ref.shape[0]
+    tokens, features = gated_ref.shape
     total = squares_ref[0]
     for k in range(1, count):
         total = total + squares_ref[k]
@@ -346,10 +359,25 @@
         precision=HIGHEST, preferred_element_type=jnp.float32,
     )
     scale = lax.rsqrt(column / features_all + epsilon)
-    for j in range(gated_ref.shape[1] // LANES):
-        tile = slice(j * LANES, (j + 1) * LANES)
-        gain = gain_ref[j : j + 1, :]
-        out_ref[:, tile] = (gated_ref[:, tile] * scale * gain).astype(jnp.bfloat16)
+    chunks = sems.shape[0]
+    size = tokens // chunks
+    copies = []
+    for i in range(chunks):
+        part = slice(i * size, (i + 1) * size)
+        for j in range(features // LANES):
+            tile = slice(j * LANES, (j + 1) * LANES)
+            rows_ref[part, tile] = (
+                gated_ref[part, tile] * scale[part] * gain_ref[j : j + 1, :]
+            ).astype(jnp.bfloat16)
+        copies.append(
+            pltpu.make_async_copy(
+                rows_ref.at[pl.ds(i * size, size), :], out_ref.at[pl.ds(i * size, size), :],
+                sems.at[i],
+            )
+        )
+        copies[-1].start()
+    for copy in copies:
+        copy.wait()
 
 
 def body(
@@ -368,31 +396,32 @@
     ahead = lambda n, k: [(i, i + k) for i in range(n - k)]
 
     bf16 = jnp.bfloat16
-    tails = call(
-        tails_kernel, out((8, 2 * state), bf16), b_source, c_source,
-        hbm=2, scratch=[pltpu.SemaphoreType.DMA((2,))],
+    small = [doc_lengths[None, :], step_raw.T, step_bias[None, :], decay_rate[None, :]]
+    tails, *small = call(
+        tails_kernel,
+        [out((8, 2 * state), bf16)] + [out(o.shape, o.dtype) for o in small],
+        b_source, c_source, *small,
+        hbm=2 + len(small), scratch=[pltpu.SemaphoreType.DMA((2 + len(small),))],
     )
     halo = lax.ppermute(tails, SEQ, ahead(shards, 1))
     operands = [
-        doc_lengths[None, :], step_raw.T, step_bias[None, :], decay_rate[None, :], inputs,
-        b_source, c_source, conv_weight, conv_bias[None, :],
+        inputs, b_source, c_source, conv_weight, conv_bias[None, :],
         norm_gain.reshape(features // LANES, LANES),
     ]
     results = call(
         prepare_kernel,
-        [out(o.shape, o.dtype) for o in operands[4:]]
+        [out(o.shape, o.dtype) for o in operands]
         + [
             out((tokens, features), bf16), out((heads, tokens)), out((heads, tokens)),
             out((tokens, LANES)), out((1, LANES)), out((tokens, LANES), jnp.int32),
             out((tokens, state)), out((tokens, state)),
         ],
-        *operands,
-        hbm=len(operands), after=(tails,),
+        *operands, *small, tails,
+        hbm=len(operands),
         scratch=[
             pltpu.VMEM((LANES, tokens), jnp.float32),
             pltpu.VMEM((tokens + 8, state), jnp.float32),
             pltpu.SemaphoreType.DMA((len(operands),)),
-            *(pltpu.VMEM(o.shape, o.dtype) for o in operands[:4]),
         ],
     )
     x, b, c, taps, taps_bias, gain = results[0:6]
@@ -404,9 +433,10 @@
         scratch=[pltpu.VMEM((16, state), jnp.float32)],
     )
     pieces = lax.all_to_all(pieces, GROUP, 0, 0)
-    before, factors, total = call(
+    pair = out((rows, features + LANES))
+    before, factors, total_a, total_b = call(
         functools.partial(prefix_kernel, heads),
-        [out((members, rows, features)), out((members, LANES)), out((rows, features + LANES))],
+        [out((members, rows, features)), out((members, LANES)), pair, pair],
         pieces,
         scratch=[
             pltpu.VMEM((members, LANES), jnp.float32),
@@ -414,25 +444,39 @@
         ],
     )
 
-    first = lax.ppermute(total, OUTER, [(0, 1)])
-    second = lax.ppermute(total, OUTER, [(1, 2), (2, 3)])
-    joined = call(functools.partial(join_kernel, heads), out(total.shape), total, first)
+    def diagonal_terms(groups, token, *before, late=()):
+        sources = [
+            c, halo, taps, taps_bias, start, c_early, b_conv, columns, cum_rows, step_rows, x,
+            gate_input,
+        ]
+        count = len(sources)
+        return call(
+            functools.partial(diagonal_kernel, groups),
+            [
+                out(token.shape), out((tokens, state), bf16), out((tokens, features)),
+                out((tokens, features)),
+            ],
+            *sources, token, *before, after=late, flops=20_000_000_000,
+            aliases={count + k: k for k in range(1 + len(before))},
+            scratch=[
+                pltpu.VMEM((tokens, tokens), jnp.float32),
+                pltpu.VMEM((16, state), jnp.float32),
+            ],
+        )
+
+    total_a, *diagonal = diagonal_terms((0,), total_a)
+    first = lax.ppermute(total_a, OUTER, [(0, 1)])
+    total_b, *diagonal = diagonal_terms((1,), total_b, *diagonal)
+    second = lax.ppermute(total_b, OUTER, [(1, 2), (2, 3)])
+    joined = call(functools.partial(join_kernel, heads), pair, total_b, first)
     far_a = lax.ppermute(joined, OUTER, [(1, 3)])
     far_b = lax.ppermute(first, OUTER, [(1, 2)])
-    c_conv, diagonal, scale = call(
-        diagonal_kernel,
-        [out((tokens, state), bf16), out((tokens, features)), out((tokens, features))],
-        c, halo, taps, taps_bias, start, c_early, b_conv, columns, cum_rows, step_rows, x,
-        gate_input, after=(joined,), flops=20_000_000_000,
-        scratch=[
-            pltpu.VMEM((tokens, tokens), jnp.float32),
-            pltpu.VMEM((16, state), jnp.float32),
-        ],
-    )
+    factors, *diagonal = diagonal_terms((2, 3), factors, *diagonal, late=(joined,))
+    c_conv, diagonal, scale = diagonal
     states_in = call(
         functools.partial(states_in_kernel, heads),
         out((members, rows, features), bf16),
-        first, second, far_a, far_b, before, factors, after=(diagonal, scale),
+        first, second, far_a, far_b, before, factors,
         scratch=[pltpu.VMEM((members, features), jnp.float32)],
     )
     states_in = lax.all_to_all(states_in, GROUP, 0, 0)
@@ -446,7 +490,8 @@
     return call(
         functools.partial(normalize_kernel, features * lax.axis_size("tp")),
         jax.ShapeDtypeStruct((tokens, features), bf16),
-        squares, gated, gain,
+        squares, gated, gain, to_hbm=True,
+        scratch=[pltpu.VMEM((tokens, features), bf16), pltpu.SemaphoreType.DMA((4,))],
     )
 
 

time: 75.5 us -> 74.9 us (level)
  starting transfers between devices: 14 us -> 10.3 us
  waiting for transfers between devices: 3.12 us -> 5.1 us
  blocking collectives: 50 us -> 51 us
    ppermute x2, starting transfers between devices: 5.38 us -> 2.65 us  [the longest x1 1.36 us: body(): second = lax.ppermute(total_b, OUTER, [(1, 2), (2, 3)])]
    ppermute x1, starting transfers between devices: 3.96 us -> 2.99 us  [body(): far_a = lax.ppermute(joined, OUTER, [(1, 3)])]
    ppermute x2, waiting for transfers between devices: 0.05 us -> 1.03 us  [the longest x1 1.02 us: body(): first = lax.ppermute(total_a, OUTER, [(0, 1)])]
    all_to_all x1, blocking collectives: 14.9 us -> 15.8 us  [body(): states_in = lax.all_to_all(states_in, GROUP, 0, 0)]
    ppermute x1, waiting for transfers between devices: 0.01 us -> 0.86 us  [body(): far_b = lax.ppermute(first, OUTER, [(1, 2)])]
    pallas_call x9 -> x11, Pallas kernels: 7.91 us -> 7.93 us  [call(): pl.pallas_call(kernel, out_shape=list(outs) if multiple else outs, in_spe...]
  transfers between devices with their start and end apart: 5 -> 5, of which waited for: 2 -> 3; matrix products, arithmetic and copies ran while one was open for 0% -> 0% of each run, Pallas kernels for 6% -> 5%
where the time goes in v5:
time: 74.9 us; the launch traced here: 74.5 us
  blocking collectives  51 us (68%)
  starting transfers between devices  10.3 us (14%)
  Pallas kernels  7.93 us (11%)
  waiting for transfers between devices  5.1 us (7%)
    all_to_all x1, blocking collectives, body(): pieces = lax.all_to_all(pieces, GROUP, 0, 0)  18.1 us
    all_gather x1, blocking collectives, body(): squares = lax.all_gather(squares, 'tp')  17.2 us
    all_to_all x1, blocking collectives, body(): states_in = lax.all_to_all(states_in, GROUP, 0, 0)  15.8 us
    pallas_call x11, Pallas kernels, call(): pl.pallas_call(kernel, out_shape=list(outs) if multiple else outs, in_spe...  7.93 us
    ppermute x1, waiting for transfers between devices, body(): halo = lax.ppermute(tails, SEQ, ahead(shards, 1))  3.22 us
    ppermute x1, starting transfers between devices, body(): halo = lax.ppermute(tails, SEQ, ahead(shards, 1))  3.12 us
    ppermute x1, starting transfers between devices, body(): far_a = lax.ppermute(joined, OUTER, [(1, 3)])  2.99 us
    ppermute x1, starting transfers between devices, body(): far_b = lax.ppermute(first, OUTER, [(1, 2)])  1.56 us
  transfers between devices with their start and end apart: 5, of which 3 were waited for; matrix products, arithmetic and copies ran while one was open for 0% of the time, Pallas kernels for 5%

profile of v5, /device:TPU:65, one launch (start us, length us, event | category | flops | bytes accessed | tf_op | source)
XLA Modules:
  0.0 74.5 jit_solution(8984882999135019411)
XLA Ops:
  0.0 0.8 %shard_map.109 = (bf16[8,256]{1,0:T(8,128)(2,1)S(1)}, s32[1,8]{1,0:T(1,128)S(1)}, f32[20,256]{1,0:T(8,128)S(1)}, f32[1,20]{1,0:T(1,128)S(1)}, f32[1,20]{1,0:T(1,128)S(1)}) custom-call(bf16[256,128]{1,0:T(8,128)(2,1)} %refs_1_.1, bf16[256,128]{1,0:T(8,128)(2,1)} %refs_2_.1, s32[1,8]{1,0:T(1,128)} %bitcast.11, f32[20,256]{1,0:T(8,128)} %bitcast.8, ...), custom_call_target="tpu_custom_call" | custom-call | flops 1000000 | bytes 1000000 | tf_op jit(solution)/shard_map/pallas_call | solution.py:28
  0.8 3.1 %collective-permute-start = (bf16[8,256]{1,0:T(8,128)(2,1)S(1)}, bf16[8,256]{1,0:T(8,128)(2,1)S(1)}, u32[]{:S(2)}, u32[]{:S(2)}) collective-permute-start(bf16[8,256]{1,0:T(8,128)(2,1)S(1)} %get-tuple-element.48.refs_10_), channel_id=1, source_target_pairs={{0,4},{4,8},{8,12},{12,16},{16,20},{20,24},{24,28},{28,32},{32,36}... | collective-permute-start | bytes 12296 | tf_op jit(solution)/shard_map/ppermute | solution.py:406
  4.0 2.2 %shard_map.110 = (bf16[256,1280]{1,0:T(8,128)(2,1)S(1)}, bf16[256,128]{1,0:T(8,128)(2,1)S(1)}, bf16[256,128]{1,0:T(8,128)(2,1)S(1)}, f32[4,256]{1,0:T(4,128)S(1)...) custom-call(bf16[256,1280]{1,0:T(8,128)(2,1)} %refs_0_.1, ...), custom_call_target="tpu_custom_call" | custom-call | flops 1000000 | bytes 1000000 | tf_op jit(solution)/shard_map/pallas_call | solution.py:28
  6.2 3.2 %collective-permute-done.halo_ref.refs_1_ = bf16[8,256]{1,0:T(8,128)(2,1)S(1)} collective-permute-done((bf16[8,256]{1,0:T(8,128)(2,1)S(1)}, bf16[8,256]{1,0:T(8,128)(2,1)S(1)}, u32[]{:S(2)}, u32[]{:S(2)}) %collective-permute-start) | collective-permute-done | bytes 4128 | tf_op jit(solution)/shard_map/ppermute | solution.py:406
  9.4 0.3 shard_map.111
  9.7 0.0 copy-start
  9.8 18.1 %all_to_all.10.pieces_ref = f32[32,4,1408]{2,1,0:T(4,128)S(1)} all-to-all(f32[32,4,1408]{2,1,0:T(4,128)S(1)} %get-tuple-element.63), channel_id=1, replica_groups=mesh['za'=4,'zb'=2,'y'=4,'x'=4,'tp'=4] {'zb','y','x'}, dimensions={0} | all-to-all | bytes 1441792 | tf_op jit(solution)/shard_map/all_to_all | solution.py:435
  27.8 0.3 shard_map.112
  28.2 0.0 copy-done
  28.2 1.3 %collective-permute-start.1 = (f32[4,1408]{1,0:T(4,128)S(1)}, f32[4,1408]{1,0:T(4,128)S(1)}, u32[]{:S(2)}, u32[]{:S(2)}) collective-permute-start(f32[4,1408]{1,0:T(4,128)S(1)} %get-tuple-element.65), channel_id=1, source_target_pairs={{0,128},{1,129},{2,130},{3,131},{4,132},{5,133},{6,134},{7,135},{8... | collective-permute-start | bytes 67592 | tf_op jit(solution)/shard_map/ppermute | solution.py:468
  29.5 1.8 %shard_map.114 = (f32[4,1408]{1,0:T(4,128)S(1)}, bf16[256,128]{1,0:T(8,128)(2,1)S(1)}, f32[256,1280]{1,0:T(8,128)S(1)}, f32[256,1280]{1,0:T(8,128)S(1)}) custom-call(bf16[256,128]{1,0:T(8,128)(2,1)S(1)} %get-tuple-element.49.refs_0_, ...), custom_call_target="tpu_custom_call", output_to_operand_aliasing={{0}: (12, {}), {1}: (13, {}), {2}: (14, {}), {3}: (15, {})} | custom-call | flops 20000000000 | bytes 1000000 | tf_op jit(solution)/shard_map/pallas_call | solution.py:28
  31.3 1.4 %collective-permute-start.2 = (f32[4,1408]{1,0:T(4,128)S(1)}, f32[4,1408]{1,0:T(4,128)S(1)}, u32[]{:S(2)}, u32[]{:S(2)}) collective-permute-start(f32[4,1408]{1,0:T(4,128)S(1)} %get-tuple-element.70.own_ref), channel_id=1, source_target_pairs={{128,256},{256,384},{129,257},{257,385},{130,258},{258,386},{131,2... | collective-permute-start | bytes 67592 | tf_op jit(solution)/shard_map/ppermute | solution.py:470
  32.6 1.0 %collective-permute-done.1.behind_ref.first_ref = f32[4,1408]{1,0:T(4,128)S(1)} collective-permute-done((f32[4,1408]{1,0:T(4,128)S(1)}, f32[4,1408]{1,0:T(4,128)S(1)}, u32[]{:S(2)}, u32[]{:S(2)}) %collective-permute-start.1) | collective-permute-done | bytes 22560 | tf_op jit(solution)/shard_map/ppermute | solution.py:468
  33.7 0.1 shard_map.115.refs_16_
  33.8 3.0 %collective-permute-start.3 = (f32[4,1408]{1,0:T(4,128)S(1)}, f32[4,1408]{1,0:T(4,128)S(1)}, u32[]{:S(2)}, u32[]{:S(2)}) collective-permute-start(f32[4,1408]{1,0:T(4,128)S(1)} %shard_map.115.refs_16_), channel_id=1, source_target_pairs={{128,384},{129,385},{130,386},{131,387},{132,388},{133,389},{134,3... | collective-permute-start | bytes 67592 | tf_op jit(solution)/shard_map/ppermute | solution.py:472
  36.8 1.6 %collective-permute-start.4 = (f32[4,1408]{1,0:T(4,128)S(1)}, f32[4,1408]{1,0:T(4,128)S(1)}, u32[]{:S(2)}, u32[]{:S(2)}) collective-permute-start(f32[4,1408]{1,0:T(4,128)S(1)} %collective-permute-done.1.behind_ref.first_ref), channel_id=1, source_target_pairs={{128,256},{129,257},{130,258},{131,259},{132,260},{133,261},{134,2... | collective-permute-start | bytes 67592 | tf_op jit(solution)/shard_map/ppermute | solution.py:473
  38.4 0.0 collective-permute-done.2.second_ref
  38.4 0.0 collective-permute-done.3.far_a_ref
  38.4 0.9 %collective-permute-done.4.far_b_ref = f32[4,1408]{1,0:T(4,128)S(1)} collective-permute-done((f32[4,1408]{1,0:T(4,128)S(1)}, f32[4,1408]{1,0:T(4,128)S(1)}, u32[]{:S(2)}, u32[]{:S(2)}) %collective-permute-start.4) | collective-permute-done | bytes 22560 | tf_op jit(solution)/shard_map/ppermute | solution.py:473
  39.2 0.4 shard_map.117
  39.7 15.8 %all_to_all.11.state_ref = bf16[32,4,1280]{2,1,0:T(4,128)(2,1)S(1)} all-to-all(bf16[32,4,1280]{2,1,0:T(4,128)(2,1)S(1)} %shard_map.117), channel_id=1, replica_groups=mesh['za'=4,'zb'=2,'y'=4,'x'=4,'tp'=4] {'zb','y','x'}, dimensions={0} | all-to-all | bytes 655360 | tf_op jit(solution)/shard_map/all_to_all | solution.py:482
  55.4 0.7 shard_map.118
  56.1 17.2 %all-gather.1.squares_ref = f32[4,1,256]{2,1,0:T(1,128)S(1)} all-gather(f32[1,1,256]{2,1,0:T(1,128)S(1)} %bitcast.7), channel_id=2, replica_groups=mesh['za'=4,'zb'=2,'y'=4,'x'=4,'tp'=4] {'tp'}, dimensions={0}, use_global_device_ids=true | all-gather | bytes 5120 | tf_op jit(solution)/shard_map/all_gather | solution.py:489
  73.3 1.2 %shard_map.119 = bf16[256,1280]{1,0:T(8,128)(2,1)} custom-call(f32[4,1,256]{2,1,0:T(1,128)S(1)} %all-gather.1.squares_ref, f32[256,1280]{1,0:T(8,128)S(1)} %get-tuple-element.81.gated_ref, f32[10,128]{1,0:T(8,128)S(1)} %get-tuple-element.82.gain_ref), custom_call_target="tpu_custom_call" | custom-call | flops 1000000 | bytes 1000000 | tf_op jit(solution)/shard_map/pallas_call | solution.py:28
  (2 shorter events, 0.0 us)
Async XLA Ops:
  0.8 8.6 %collective-permute-start = (bf16[8,256]{1,0:T(8,128)(2,1)S(1)}, bf16[8,256]{1,0:T(8,128)(2,1)S(1)}, u32[]{:S(2)}, u32[]{:S(2)}) collective-permute-start(bf16[8,256]{1,0:T(8,128)(2,1)S(1)} %get-tuple-element.48.refs_10_), channel_id=1, source_target_pairs={{0,4},{4,8},{8,12},{12,16},{16,20},{20,24},{24,28},{28,32},{32,36}... | collective-permute-start | bytes 12296 | tf_op jit(solution)/shard_map/ppermute | solution.py:406
  9.7 18.4 %copy-start = (bf16[256,1280]{1,0:T(8,128)(2,1)S(1)}, bf16[256,1280]{1,0:T(8,128)(2,1)}, u32[]{:S(2)}) copy-start(bf16[256,1280]{1,0:T(8,128)(2,1)} %refs_11_.5) | copy-start | bytes 1966084
  28.2 5.4 %collective-permute-start.1 = (f32[4,1408]{1,0:T(4,128)S(1)}, f32[4,1408]{1,0:T(4,128)S(1)}, u32[]{:S(2)}, u32[]{:S(2)}) collective-permute-start(f32[4,1408]{1,0:T(4,128)S(1)} %get-tuple-element.65), channel_id=1, source_target_pairs={{0,128},{1,129},{2,130},{3,131},{4,132},{5,133},{6,134},{7,135},{8... | collective-permute-start | bytes 67592 | tf_op jit(solution)/shard_map/ppermute | solution.py:468
  31.3 7.1 %collective-permute-start.2 = (f32[4,1408]{1,0:T(4,128)S(1)}, f32[4,1408]{1,0:T(4,128)S(1)}, u32[]{:S(2)}, u32[]{:S(2)}) collective-permute-start(f32[4,1408]{1,0:T(4,128)S(1)} %get-tuple-element.70.own_ref), channel_id=1, source_target_pairs={{128,256},{256,384},{129,257},{257,385},{130,258},{258,386},{131,2... | collective-permute-start | bytes 67592 | tf_op jit(solution)/shard_map/ppermute | solution.py:470
  33.8 4.6 %collective-permute-start.3 = (f32[4,1408]{1,0:T(4,128)S(1)}, f32[4,1408]{1,0:T(4,128)S(1)}, u32[]{:S(2)}, u32[]{:S(2)}) collective-permute-start(f32[4,1408]{1,0:T(4,128)S(1)} %shard_map.115.refs_16_), channel_id=1, source_target_pairs={{128,384},{129,385},{130,386},{131,387},{132,388},{133,389},{134,3... | collective-permute-start | bytes 67592 | tf_op jit(solution)/shard_map/ppermute | solution.py:472
  36.8 2.5 %collective-permute-start.4 = (f32[4,1408]{1,0:T(4,128)S(1)}, f32[4,1408]{1,0:T(4,128)S(1)}, u32[]{:S(2)}, u32[]{:S(2)}) collective-permute-start(f32[4,1408]{1,0:T(4,128)S(1)} %collective-permute-done.1.behind_ref.first_ref), channel_id=1, source_target_pairs={{128,256},{129,257},{130,258},{131,259},{132,260},{133,261},{134,2... | collective-permute-start | bytes 67592 | tf_op jit(solution)/shard_map/ppermute | solution.py:473

commit v6 on v5

--- a/solution.py
+++ b/solution.py
@@ -227,18 +227,17 @@
     features = own_ref.shape[1] - LANES
     factor = wide_factor(own_ref, features, features // heads)
     joined_ref[:, 0:features] = factor * behind_ref[:, 0:features] + own_ref[:, 0:features]
-    joined_ref[:, features:] = own_ref[:, features:] * behind_ref[:, features:]
+    joined_ref[:, features:] = own_ref[:, features:]
 
 
 def states_in_kernel(
-    heads, first_ref, second_ref, far_a_ref, far_b_ref, before_ref, factors_ref, state_ref, wide_ref
+    heads, first_ref, second_ref, far_ref, before_ref, factors_ref, state_ref, wide_ref
 ):
     members, rows, features = before_ref.shape
     width = features // heads
     factor = wide_factor(second_ref, features, width)
-    far = far_a_ref[:, 0:features] + far_b_ref[:, 0:features]
     near = first_ref[:, 0:features] + second_ref[:, 0:features]
-    entering = factor * far + near
+    entering = factor * far_ref[:, 0:features] + near
     factors = factors_ref[...]
     for j in range(features // LANES):
         wide_ref[:, j * LANES : (j + 1) * LANES] = tile_of_heads(factors, j, width)
@@ -310,12 +309,14 @@
         scale_ref[:, tile] = tile_of_heads(carried, j, width) * gate
 
 
-def diagonal_kernel(groups, *refs):
+def diagonal_kernel(turn, *refs):
     (*sources, columns_ref, cum_rows_ref, step_rows_ref, x_ref, gate_ref) = refs[:12]
     _, c_conv_ref, gated_ref, scale_ref, products_ref, padded_ref = refs[-6:]
     place = lax.axis_index(OUTER)
-
-    @pl.when((place >= groups[0]) & (place <= groups[-1]))
+    early = (place == 0) & (lax.axis_index("tp") < lax.axis_size("tp") // 2)
+    late = place >= 2
+
+    @pl.when((early, jnp.logical_not(early | late), late)[turn])
     def _():
         products_of(*sources, c_conv_ref, products_ref, padded_ref)
         diagonal_of(
@@ -444,14 +445,14 @@
         ],
     )
 
-    def diagonal_terms(groups, token, *before, late=()):
+    def diagonal_terms(turn, token, *before, late=()):
         sources = [
             c, halo, taps, taps_bias, start, c_early, b_conv, columns, cum_rows, step_rows, x,
             gate_input,
         ]
         count = len(sources)
         return call(
-            functools.partial(diagonal_kernel, groups),
+            functools.partial(diagonal_kernel, turn),
             [
                 out(token.shape), out((tokens, state), bf16), out((tokens, features)),
                 out((tokens, features)),
@@ -464,19 +465,18 @@
             ],
         )
 
-    total_a, *diagonal = diagonal_terms((0,), total_a)
+    total_a, *diagonal = diagonal_terms(0, total_a)
     first = lax.ppermute(total_a, OUTER, [(0, 1)])
-    total_b, *diagonal = diagonal_terms((1,), total_b, *diagonal)
-    second = lax.ppermute(total_b, OUTER, [(1, 2), (2, 3)])
+    total_b, *diagonal = diagonal_terms(1, total_b, *diagonal)
     joined = call(functools.partial(join_kernel, heads), pair, total_b, first)
-    far_a = lax.ppermute(joined, OUTER, [(1, 3)])
-    far_b = lax.ppermute(first, OUTER, [(1, 2)])
-    factors, *diagonal = diagonal_terms((2, 3), factors, *diagonal, late=(joined,))
+    far = lax.ppermute(joined, OUTER, [(1, 3)])
+    second = lax.ppermute(joined, OUTER, [(1, 2), (2, 3)])
+    factors, *diagonal = diagonal_terms(2, factors, *diagonal, late=(joined,))
     c_conv, diagonal, scale = diagonal
     states_in = call(
         functools.partial(states_in_kernel, heads),
         out((members, rows, features), bf16),
-        first, second, far_a, far_b, before, factors,
+        first, second, far, before, factors,
         scratch=[pltpu.VMEM((members, features), jnp.float32)],
     )
     states_in = lax.all_to_all(states_in, GROUP, 0, 0)

time: 74.9 us -> 73.1 us (0.976)
  the two profiles are of different devices: /device:TPU:65 before, /device:TPU:385 now
where the time goes in v6:
time: 73.1 us; the launch traced here: 72.8 us
  blocking collectives  50.2 us (69%)
  waiting for transfers between devices  8.18 us (11%)
  Pallas kernels  7.93 us (11%)
  starting transfers between devices  6.37 us (9%)
    all_gather x1, blocking collectives, body(): squares = lax.all_gather(squares, 'tp')  18.3 us
    all_to_all x1, blocking collectives, body(): pieces = lax.all_to_all(pieces, GROUP, 0, 0)  16.6 us
    all_to_all x1, blocking collectives, body(): states_in = lax.all_to_all(states_in, GROUP, 0, 0)  15.3 us
    pallas_call x11, Pallas kernels, call(): pl.pallas_call(kernel, out_shape=list(outs) if multiple else outs, in_spe...  7.93 us
    ppermute x1, waiting for transfers between devices, body(): halo = lax.ppermute(tails, SEQ, ahead(shards, 1))  4.43 us
    ppermute x1, waiting for transfers between devices, body(): second = lax.ppermute(joined, OUTER, [(1, 2), (2, 3)])  3.74 us
    ppermute x1, starting transfers between devices, body(): halo = lax.ppermute(tails, SEQ, ahead(shards, 1))  3.12 us
    ppermute x1, starting transfers between devices, body(): second = lax.ppermute(joined, OUTER, [(1, 2), (2, 3)])  1.92 us
  transfers between devices with their start and end apart: 4, of which 2 were waited for; matrix products, arithmetic and copies ran while one was open for 0% of the time, Pallas kernels for 5%

profile of v6, /device:TPU:385, one launch (start us, length us, event | category | flops | bytes accessed | tf_op | source)
XLA Modules:
  0.0 72.8 jit_solution(9708379719906586433)
XLA Ops:
  0.0 0.8 %shard_map.109 = (bf16[8,256]{1,0:T(8,128)(2,1)S(1)}, s32[1,8]{1,0:T(1,128)S(1)}, f32[20,256]{1,0:T(8,128)S(1)}, f32[1,20]{1,0:T(1,128)S(1)}, f32[1,20]{1,0:T(1,128)S(1)}) custom-call(bf16[256,128]{1,0:T(8,128)(2,1)} %refs_1_.1, bf16[256,128]{1,0:T(8,128)(2,1)} %refs_2_.1, s32[1,8]{1,0:T(1,128)} %bitcast.11, f32[20,256]{1,0:T(8,128)} %bitcast.8, ...), custom_call_target="tpu_custom_call" | custom-call | flops 1000000 | bytes 1000000 | tf_op jit(solution)/shard_map/pallas_call | solution.py:28
  0.8 3.1 %collective-permute-start = (bf16[8,256]{1,0:T(8,128)(2,1)S(1)}, bf16[8,256]{1,0:T(8,128)(2,1)S(1)}, u32[]{:S(2)}, u32[]{:S(2)}) collective-permute-start(bf16[8,256]{1,0:T(8,128)(2,1)S(1)} %get-tuple-element.48.refs_10_), channel_id=1, source_target_pairs={{0,4},{4,8},{8,12},{12,16},{16,20},{20,24},{24,28},{28,32},{32,36}... | collective-permute-start | bytes 12296 | tf_op jit(solution)/shard_map/ppermute | solution.py:407
  4.0 2.2 %shard_map.110 = (bf16[256,1280]{1,0:T(8,128)(2,1)S(1)}, bf16[256,128]{1,0:T(8,128)(2,1)S(1)}, bf16[256,128]{1,0:T(8,128)(2,1)S(1)}, f32[4,256]{1,0:T(4,128)S(1)...) custom-call(bf16[256,1280]{1,0:T(8,128)(2,1)} %refs_0_.1, ...), custom_call_target="tpu_custom_call" | custom-call | flops 1000000 | bytes 1000000 | tf_op jit(solution)/shard_map/pallas_call | solution.py:28
  6.2 4.4 %collective-permute-done.halo_ref.refs_1_ = bf16[8,256]{1,0:T(8,128)(2,1)S(1)} collective-permute-done((bf16[8,256]{1,0:T(8,128)(2,1)S(1)}, bf16[8,256]{1,0:T(8,128)(2,1)S(1)}, u32[]{:S(2)}, u32[]{:S(2)}) %collective-permute-start) | collective-permute-done | bytes 4128 | tf_op jit(solution)/shard_map/ppermute | solution.py:407
  10.6 0.3 shard_map.111
  11.0 0.0 copy-start
  11.0 16.6 %all_to_all.10.pieces_ref = f32[32,4,1408]{2,1,0:T(4,128)S(1)} all-to-all(f32[32,4,1408]{2,1,0:T(4,128)S(1)} %get-tuple-element.63), channel_id=1, replica_groups=mesh['za'=4,'zb'=2,'y'=4,'x'=4,'tp'=4] {'zb','y','x'}, dimensions={0} | all-to-all | bytes 1441792 | tf_op jit(solution)/shard_map/all_to_all | solution.py:436
  27.6 0.3 shard_map.112
  27.9 0.0 copy-done
  27.9 0.7 collective-permute-start.1
  28.6 0.0 collective-permute-done.1.behind_ref.first_ref
  28.7 0.1 shard_map.115.refs_16_
  28.8 0.7 collective-permute-start.3
  29.4 1.9 %collective-permute-start.2 = (f32[4,1408]{1,0:T(4,128)S(1)}, f32[4,1408]{1,0:T(4,128)S(1)}, u32[]{:S(2)}, u32[]{:S(2)}) collective-permute-start(f32[4,1408]{1,0:T(4,128)S(1)} %shard_map.115.refs_16_), channel_id=1, source_target_pairs={{128,256},{256,384},{129,257},{257,385},{130,258},{258,386},{131,2... | collective-permute-start | bytes 67592 | tf_op jit(solution)/shard_map/ppermute | solution.py:473
  31.4 1.8 %shard_map.116 = (f32[32,128]{1,0:T(8,128)S(1)}, bf16[256,128]{1,0:T(8,128)(2,1)S(1)}, f32[256,1280]{1,0:T(8,128)S(1)}, f32[256,1280]{1,0:T(8,128)S(1)}) custom-call(bf16[256,128]{1,0:T(8,128)(2,1)S(1)} %get-tuple-element.49.refs_0_, ...), custom_call_target="tpu_custom_call", output_to_operand_aliasing={{0}: (12, {}), {1}: (13, {}), {2}: (14, {}), {3}: (15, {})} | custom-call | flops 20000000000 | bytes 1000000 | tf_op jit(solution)/shard_map/pallas_call | solution.py:28
  33.1 0.0 collective-permute-done.3.far_ref
  33.1 3.7 %collective-permute-done.2.second_ref = f32[4,1408]{1,0:T(4,128)S(1)} collective-permute-done((f32[4,1408]{1,0:T(4,128)S(1)}, f32[4,1408]{1,0:T(4,128)S(1)}, u32[]{:S(2)}, u32[]{:S(2)}) %collective-permute-start.2) | collective-permute-done | bytes 22560 | tf_op jit(solution)/shard_map/ppermute | solution.py:473
  36.9 0.4 shard_map.117
  37.3 15.3 %all_to_all.11.state_ref = bf16[32,4,1280]{2,1,0:T(4,128)(2,1)S(1)} all-to-all(bf16[32,4,1280]{2,1,0:T(4,128)(2,1)S(1)} %shard_map.117), channel_id=1, replica_groups=mesh['za'=4,'zb'=2,'y'=4,'x'=4,'tp'=4] {'zb','y','x'}, dimensions={0} | all-to-all | bytes 655360 | tf_op jit(solution)/shard_map/all_to_all | solution.py:482
  52.6 0.7 shard_map.118
  53.3 18.3 %all-gather.1.squares_ref = f32[4,1,256]{2,1,0:T(1,128)S(1)} all-gather(f32[1,1,256]{2,1,0:T(1,128)S(1)} %bitcast.7), channel_id=2, replica_groups=mesh['za'=4,'zb'=2,'y'=4,'x'=4,'tp'=4] {'tp'}, dimensions={0}, use_global_device_ids=true | all-gather | bytes 5120 | tf_op jit(solution)/shard_map/all_gather | solution.py:489
  71.6 1.2 %shard_map.119 = bf16[256,1280]{1,0:T(8,128)(2,1)} custom-call(f32[4,1,256]{2,1,0:T(1,128)S(1)} %all-gather.1.squares_ref, f32[256,1280]{1,0:T(8,128)S(1)} %get-tuple-element.81.gated_ref, f32[10,128]{1,0:T(8,128)S(1)} %get-tuple-element.82.gain_ref), custom_call_target="tpu_custom_call" | custom-call | flops 1000000 | bytes 1000000 | tf_op jit(solution)/shard_map/pallas_call | solution.py:28
  (2 shorter events, 0.0 us)
Async XLA Ops:
  0.8 9.8 %collective-permute-start = (bf16[8,256]{1,0:T(8,128)(2,1)S(1)}, bf16[8,256]{1,0:T(8,128)(2,1)S(1)}, u32[]{:S(2)}, u32[]{:S(2)}) collective-permute-start(bf16[8,256]{1,0:T(8,128)(2,1)S(1)} %get-tuple-element.48.refs_10_), channel_id=1, source_target_pairs={{0,4},{4,8},{8,12},{12,16},{16,20},{20,24},{24,28},{28,32},{32,36}... | collective-permute-start | bytes 12296 | tf_op jit(solution)/shard_map/ppermute | solution.py:407
  11.0 17.0 %copy-start = (bf16[256,1280]{1,0:T(8,128)(2,1)S(1)}, bf16[256,1280]{1,0:T(8,128)(2,1)}, u32[]{:S(2)}) copy-start(bf16[256,1280]{1,0:T(8,128)(2,1)} %refs_11_.5) | copy-start | bytes 1966084
  27.9 0.7 collective-permute-start.1
  28.8 4.4 %collective-permute-start.3 = (f32[4,1408]{1,0:T(4,128)S(1)}, f32[4,1408]{1,0:T(4,128)S(1)}, u32[]{:S(2)}, u32[]{:S(2)}) collective-permute-start(f32[4,1408]{1,0:T(4,128)S(1)} %shard_map.115.refs_16_), channel_id=1, source_target_pairs={{128,384},{129,385},{130,386},{131,387},{132,388},{133,389},{134,3... | collective-permute-start | bytes 67592 | tf_op jit(solution)/shard_map/ppermute | solution.py:472
  29.4 7.4 %collective-permute-start.2 = (f32[4,1408]{1,0:T(4,128)S(1)}, f32[4,1408]{1,0:T(4,128)S(1)}, u32[]{:S(2)}, u32[]{:S(2)}) collective-permute-start(f32[4,1408]{1,0:T(4,128)S(1)} %shard_map.115.refs_16_), channel_id=1, source_target_pairs={{128,256},{256,384},{129,257},{257,385},{130,258},{258,386},{131,2... | collective-permute-start | bytes 67592 | tf_op jit(solution)/shard_map/ppermute | solution.py:473

commit v7 on v6

--- a/solution.py
+++ b/solution.py
@@ -103,9 +103,9 @@
     targets = refs[count + 5 : 2 * count + 5]
     (
         weighted_ref, cum_rows_ref, step_rows_ref, columns_ref, factor_ref, start_ref, b_conv_ref,
-        c_conv_ref, stack_ref, padded_ref, sems,
+        stack_ref, padded_ref, sems,
     ) = refs[2 * count + 5 :]
-    x_ref, b_ref, c_ref, taps_ref, taps_bias_ref, _ = targets
+    x_ref, b_ref, _, taps_ref, taps_bias_ref, _ = targets
     copies = [
         pltpu.make_async_copy(source, target, sems.at[k])
         for k, (source, target) in enumerate(zip(sources, targets))
@@ -154,12 +154,11 @@
         weighted_ref[:, tile] = (
             x_ref[:, tile].astype(jnp.float32) * tile_of_heads(columns, j, width, WEIGHTS_AT)
         ).astype(jnp.bfloat16)
+    side = slice(0, state)
     padded_ref[0:8, :] = jnp.zeros((8, state), jnp.float32)
-    for k, (source_ref, target_ref) in enumerate(((b_ref, b_conv_ref), (c_ref, c_conv_ref))):
-        side = slice(k * state, (k + 1) * state)
-        padded_ref[8:, :] = source_ref[...].astype(jnp.float32)
-        result = convolve(padded_ref, taps_ref[:, side], taps_bias_ref[:, side], relative, chosen)
-        target_ref[...] = result.astype(target_ref.dtype)
+    padded_ref[8:, :] = b_ref[...].astype(jnp.float32)
+    b_conv = convolve(padded_ref, taps_ref[:, side], taps_bias_ref[:, side], relative, chosen)
+    b_conv_ref[...] = b_conv.astype(jnp.float32)
 
 
 def first_rows(source_ref, halo, weight, bias, start_ref, padded_ref):
@@ -246,17 +245,16 @@
 
 
 def products_of(
-    c_ref, halo_ref, taps_ref, taps_bias_ref, start_ref, c_early_ref, b_conv_ref, c_conv_ref,
-    products_ref, padded_ref,
+    c_ref, halo_ref, taps_ref, taps_bias_ref, start_ref, b_conv_ref, c_conv_ref, products_ref,
+    padded_ref,
 ):
     tokens, state = c_ref.shape
-    first = first_rows(
-        c_ref, halo_ref[:, state:], taps_ref[:, state:], taps_bias_ref[:, state:], start_ref,
-        padded_ref,
-    )
-    c_conv = jnp.concatenate(
-        [first.astype(jnp.float32), c_early_ref[8:, :]], axis=0
-    ).astype(jnp.bfloat16)
+    padded_ref[0:8, :] = halo_ref[:, state:].astype(jnp.float32)
+    padded_ref[8:, :] = c_ref[...].astype(jnp.float32)
+    relative = lax.broadcasted_iota(jnp.int32, (tokens, LANES), 0)
+    c_conv = convolve(
+        padded_ref, taps_ref[:, state:], taps_bias_ref[:, state:], relative, start_ref[...]
+    )
     c_conv_ref[...] = c_conv
     products = lax.dot_general(
         c_conv, b_conv_ref[...], (((1,), (1,)), ((), ())), preferred_element_type=jnp.float32
@@ -310,7 +308,7 @@
 
 
 def diagonal_kernel(turn, *refs):
-    (*sources, columns_ref, cum_rows_ref, step_rows_ref, x_ref, gate_ref) = refs[:12]
+    (*sources, columns_ref, cum_rows_ref, step_rows_ref, x_ref, gate_ref) = refs[:11]
     _, c_conv_ref, gated_ref, scale_ref, products_ref, padded_ref = refs[-6:]
     place = lax.axis_index(OUTER)
     early = (place == 0) & (lax.axis_index("tp") < lax.axis_size("tp") // 2)
@@ -325,19 +323,14 @@
         )
 
 
-def gate_kernel(
-    state_ref, c_conv_ref, diagonal_ref, scale_ref, gated_ref, squares_ref, rows_ref
-):
+def gate_kernel(state_ref, c_conv_ref, diagonal_ref, scale_ref, gated_ref, squares_ref):
     members, rows, features = state_ref.shape
-    for m in range(members):
-        rows_ref[m * rows : (m + 1) * rows, :] = state_ref[m].astype(jnp.float32)
     c_conv = c_conv_ref[...]
     squares = jnp.zeros((c_conv.shape[0], LANES), jnp.float32)
     for j in range(features // LANES):
         tile = slice(j * LANES, (j + 1) * LANES)
-        carried = jnp.dot(
-            c_conv, rows_ref[:, tile].astype(jnp.bfloat16), preferred_element_type=jnp.float32
-        )
+        state = state_ref[:, :, tile].astype(jnp.float32).reshape(members * rows, LANES)
+        carried = jnp.dot(c_conv, state.astype(jnp.bfloat16), preferred_element_type=jnp.float32)
         gated = diagonal_ref[:, tile] + scale_ref[:, tile] * carried
         gated_ref[:, tile] = gated
         squares = squares + gated * gated
@@ -415,7 +408,7 @@
         + [
             out((tokens, features), bf16), out((heads, tokens)), out((heads, tokens)),
             out((tokens, LANES)), out((1, LANES)), out((tokens, LANES), jnp.int32),
-            out((tokens, state)), out((tokens, state)),
+            out((tokens, state)),
         ],
         *operands, *small, tails,
         hbm=len(operands),
@@ -426,7 +419,7 @@
         ],
     )
     x, b, c, taps, taps_bias, gain = results[0:6]
-    weighted, cum_rows, step_rows, columns, factor, start, b_early, c_early = results[6:]
+    weighted, cum_rows, step_rows, columns, factor, start, b_early = results[6:]
     pieces, b_conv = call(
         states_kernel,
         [out((members, rows, features + LANES)), out((tokens, state), bf16)],
@@ -447,7 +440,7 @@
 
     def diagonal_terms(turn, token, *before, late=()):
         sources = [
-            c, halo, taps, taps_bias, start, c_early, b_conv, columns, cum_rows, step_rows, x,
+            c, halo, taps, taps_bias, start, b_conv, columns, cum_rows, step_rows, x,
             gate_input,
         ]
         count = len(sources)
@@ -461,7 +454,7 @@
             aliases={count + k: k for k in range(1 + len(before))},
             scratch=[
                 pltpu.VMEM((tokens, tokens), jnp.float32),
-                pltpu.VMEM((16, state), jnp.float32),
+                pltpu.VMEM((tokens + 8, state), jnp.float32),
             ],
         )
 
@@ -484,7 +477,6 @@
         gate_kernel,
         [out((tokens, features)), out((1, tokens))],
         states_in, c_conv, diagonal, scale,
-        scratch=[pltpu.VMEM((state, features), jnp.float32)],
     )
     squares = lax.all_gather(squares, "tp")
     return call(

time: 73.1 us -> 72.4 us (level)
  the two profiles are of different devices: /device:TPU:385 before, /device:TPU:65 now
where the time goes in v7:
time: 72.4 us; the launch traced here: 72.1 us
  blocking collectives  48.4 us (67%)
  starting transfers between devices  9.17 us (13%)
  Pallas kernels  7.83 us (11%)
  waiting for transfers between devices  6.55 us (9%)
    all_to_all x1, blocking collectives, body(): pieces = lax.all_to_all(pieces, GROUP, 0, 0)  18 us
    all_gather x1, blocking collectives, body(): squares = lax.all_gather(squares, 'tp')  16.5 us
    all_to_all x1, blocking collectives, body(): states_in = lax.all_to_all(states_in, GROUP, 0, 0)  13.9 us
    pallas_call x11, Pallas kernels, call(): pl.pallas_call(kernel, out_shape=list(outs) if multiple else outs, in_spe...  7.83 us
    ppermute x1, starting transfers between devices, body(): far = lax.ppermute(joined, OUTER, [(1, 3)])  3.47 us
    ppermute x1, waiting for transfers between devices, body(): halo = lax.ppermute(tails, SEQ, ahead(shards, 1))  3.33 us
    ppermute x1, starting transfers between devices, body(): halo = lax.ppermute(tails, SEQ, ahead(shards, 1))  3.12 us
    ppermute x1, waiting for transfers between devices, body(): first = lax.ppermute(total_a, OUTER, [(0, 1)])  2.34 us
  transfers between devices with their start and end apart: 4, of which 3 were waited for; matrix products, arithmetic and copies ran while one was open for 0% of the time, Pallas kernels for 5%

profile of v7, /device:TPU:65, one launch (start us, length us, event | category | flops | bytes accessed | tf_op | source)
XLA Modules:
  0.0 72.1 jit_solution(16456895502549560648)
XLA Ops:
  0.0 0.8 %shard_map.109 = (bf16[8,256]{1,0:T(8,128)(2,1)S(1)}, s32[1,8]{1,0:T(1,128)S(1)}, f32[20,256]{1,0:T(8,128)S(1)}, f32[1,20]{1,0:T(1,128)S(1)}, f32[1,20]{1,0:T(1,128)S(1)}) custom-call(bf16[256,128]{1,0:T(8,128)(2,1)} %refs_1_.1, bf16[256,128]{1,0:T(8,128)(2,1)} %refs_2_.1, s32[1,8]{1,0:T(1,128)} %bitcast.11, f32[20,256]{1,0:T(8,128)} %bitcast.8, ...), custom_call_target="tpu_custom_call" | custom-call | flops 1000000 | bytes 1000000 | tf_op jit(solution)/shard_map/pallas_call | solution.py:28
  0.8 3.1 %collective-permute-start = (bf16[8,256]{1,0:T(8,128)(2,1)S(1)}, bf16[8,256]{1,0:T(8,128)(2,1)S(1)}, u32[]{:S(2)}, u32[]{:S(2)}) collective-permute-start(bf16[8,256]{1,0:T(8,128)(2,1)S(1)} %get-tuple-element.47.refs_10_), channel_id=1, source_target_pairs={{0,4},{4,8},{8,12},{12,16},{16,20},{20,24},{24,28},{28,32},{32,36}... | collective-permute-start | bytes 12296 | tf_op jit(solution)/shard_map/ppermute | solution.py:400
  4.0 2.1 %shard_map.110 = (bf16[256,1280]{1,0:T(8,128)(2,1)S(1)}, bf16[256,128]{1,0:T(8,128)(2,1)S(1)}, bf16[256,128]{1,0:T(8,128)(2,1)S(1)}, f32[4,256]{1,0:T(4,128)S(1)...) custom-call(bf16[256,1280]{1,0:T(8,128)(2,1)} %refs_0_.1, ...), custom_call_target="tpu_custom_call" | custom-call | flops 1000000 | bytes 1000000 | tf_op jit(solution)/shard_map/pallas_call | solution.py:28
  6.1 3.3 %collective-permute-done.halo_ref.refs_1_ = bf16[8,256]{1,0:T(8,128)(2,1)S(1)} collective-permute-done((bf16[8,256]{1,0:T(8,128)(2,1)S(1)}, bf16[8,256]{1,0:T(8,128)(2,1)S(1)}, u32[]{:S(2)}, u32[]{:S(2)}) %collective-permute-start) | collective-permute-done | bytes 4128 | tf_op jit(solution)/shard_map/ppermute | solution.py:400
  9.4 0.3 shard_map.111
  9.7 0.0 copy-start
  9.8 18.0 %all_to_all.10.pieces_ref = f32[32,4,1408]{2,1,0:T(4,128)S(1)} all-to-all(f32[32,4,1408]{2,1,0:T(4,128)S(1)} %get-tuple-element.61), channel_id=1, replica_groups=mesh['za'=4,'zb'=2,'y'=4,'x'=4,'tp'=4] {'zb','y','x'}, dimensions={0} | all-to-all | bytes 1441792 | tf_op jit(solution)/shard_map/all_to_all | solution.py:429
  27.7 0.3 shard_map.112
  28.1 0.0 copy-done
  28.1 1.3 %collective-permute-start.1 = (f32[4,1408]{1,0:T(4,128)S(1)}, f32[4,1408]{1,0:T(4,128)S(1)}, u32[]{:S(2)}, u32[]{:S(2)}) collective-permute-start(f32[4,1408]{1,0:T(4,128)S(1)} %get-tuple-element.63), channel_id=1, source_target_pairs={{0,128},{1,129},{2,130},{3,131},{4,132},{5,133},{6,134},{7,135},{8... | collective-permute-start | bytes 67592 | tf_op jit(solution)/shard_map/ppermute | solution.py:462
  29.4 1.8 %shard_map.114 = (f32[4,1408]{1,0:T(4,128)S(1)}, bf16[256,128]{1,0:T(8,128)(2,1)S(1)}, f32[256,1280]{1,0:T(8,128)S(1)}, f32[256,1280]{1,0:T(8,128)S(1)}) custom-call(bf16[256,128]{1,0:T(8,128)(2,1)S(1)} %get-tuple-element.48.refs_0_, ...), custom_call_target="tpu_custom_call", output_to_operand_aliasing={{0}: (11, {}), {1}: (12, {}), {2}: (13, {}), {3}: (14, {})} | custom-call | flops 20000000000 | bytes 1000000 | tf_op jit(solution)/shard_map/pallas_call | solution.py:28
  31.2 2.3 %collective-permute-done.1.behind_ref.first_ref = f32[4,1408]{1,0:T(4,128)S(1)} collective-permute-done((f32[4,1408]{1,0:T(4,128)S(1)}, f32[4,1408]{1,0:T(4,128)S(1)}, u32[]{:S(2)}, u32[]{:S(2)}) %collective-permute-start.1) | collective-permute-done | bytes 22560 | tf_op jit(solution)/shard_map/ppermute | solution.py:462
  33.6 0.1 shard_map.115.refs_15_
  33.7 3.5 %collective-permute-start.3 = (f32[4,1408]{1,0:T(4,128)S(1)}, f32[4,1408]{1,0:T(4,128)S(1)}, u32[]{:S(2)}, u32[]{:S(2)}) collective-permute-start(f32[4,1408]{1,0:T(4,128)S(1)} %shard_map.115.refs_15_), channel_id=1, source_target_pairs={{128,384},{129,385},{130,386},{131,387},{132,388},{133,389},{134,3... | collective-permute-start | bytes 67592 | tf_op jit(solution)/shard_map/ppermute | solution.py:465
  37.1 1.3 %collective-permute-start.2 = (f32[4,1408]{1,0:T(4,128)S(1)}, f32[4,1408]{1,0:T(4,128)S(1)}, u32[]{:S(2)}, u32[]{:S(2)}) collective-permute-start(f32[4,1408]{1,0:T(4,128)S(1)} %shard_map.115.refs_15_), channel_id=1, source_target_pairs={{128,256},{256,384},{129,257},{257,385},{130,258},{258,386},{131,2... | collective-permute-start | bytes 67592 | tf_op jit(solution)/shard_map/ppermute | solution.py:466
  38.5 0.0 collective-permute-done.3.far_ref
  38.5 0.9 %collective-permute-done.2.second_ref = f32[4,1408]{1,0:T(4,128)S(1)} collective-permute-done((f32[4,1408]{1,0:T(4,128)S(1)}, f32[4,1408]{1,0:T(4,128)S(1)}, u32[]{:S(2)}, u32[]{:S(2)}) %collective-permute-start.2) | collective-permute-done | bytes 22560 | tf_op jit(solution)/shard_map/ppermute | solution.py:466
  39.3 0.4 shard_map.117
  39.7 13.9 %all_to_all.11.state_ref = bf16[32,4,1280]{2,1,0:T(4,128)(2,1)S(1)} all-to-all(bf16[32,4,1280]{2,1,0:T(4,128)(2,1)S(1)} %shard_map.117), channel_id=1, replica_groups=mesh['za'=4,'zb'=2,'y'=4,'x'=4,'tp'=4] {'zb','y','x'}, dimensions={0} | all-to-all | bytes 655360 | tf_op jit(solution)/shard_map/all_to_all | solution.py:475
  53.6 0.7 shard_map.118
  54.3 16.5 %all-gather.1.squares_ref = f32[4,1,256]{2,1,0:T(1,128)S(1)} all-gather(f32[1,1,256]{2,1,0:T(1,128)S(1)} %bitcast.7), channel_id=2, replica_groups=mesh['za'=4,'zb'=2,'y'=4,'x'=4,'tp'=4] {'tp'}, dimensions={0}, use_global_device_ids=true | all-gather | bytes 5120 | tf_op jit(solution)/shard_map/all_gather | solution.py:481
  70.9 1.2 %shard_map.119 = bf16[256,1280]{1,0:T(8,128)(2,1)} custom-call(f32[4,1,256]{2,1,0:T(1,128)S(1)} %all-gather.1.squares_ref, f32[256,1280]{1,0:T(8,128)S(1)} %get-tuple-element.79.gated_ref, f32[10,128]{1,0:T(8,128)S(1)} %get-tuple-element.80.gain_ref), custom_call_target="tpu_custom_call" | custom-call | flops 1000000 | bytes 1000000 | tf_op jit(solution)/shard_map/pallas_call | solution.py:28
  (2 shorter events, 0.0 us)
Async XLA Ops:
  0.8 8.6 %collective-permute-start = (bf16[8,256]{1,0:T(8,128)(2,1)S(1)}, bf16[8,256]{1,0:T(8,128)(2,1)S(1)}, u32[]{:S(2)}, u32[]{:S(2)}) collective-permute-start(bf16[8,256]{1,0:T(8,128)(2,1)S(1)} %get-tuple-element.47.refs_10_), channel_id=1, source_target_pairs={{0,4},{4,8},{8,12},{12,16},{16,20},{20,24},{24,28},{28,32},{32,36}... | collective-permute-start | bytes 12296 | tf_op jit(solution)/shard_map/ppermute | solution.py:400
  9.7 18.3 %copy-start = (bf16[256,1280]{1,0:T(8,128)(2,1)S(1)}, bf16[256,1280]{1,0:T(8,128)(2,1)}, u32[]{:S(2)}) copy-start(bf16[256,1280]{1,0:T(8,128)(2,1)} %refs_10_.5) | copy-start | bytes 1966084
  28.1 5.4 %collective-permute-start.1 = (f32[4,1408]{1,0:T(4,128)S(1)}, f32[4,1408]{1,0:T(4,128)S(1)}, u32[]{:S(2)}, u32[]{:S(2)}) collective-permute-start(f32[4,1408]{1,0:T(4,128)S(1)} %get-tuple-element.63), channel_id=1, source_target_pairs={{0,128},{1,129},{2,130},{3,131},{4,132},{5,133},{6,134},{7,135},{8... | collective-permute-start | bytes 67592 | tf_op jit(solution)/shard_map/ppermute | solution.py:462
  33.7 4.8 %collective-permute-start.3 = (f32[4,1408]{1,0:T(4,128)S(1)}, f32[4,1408]{1,0:T(4,128)S(1)}, u32[]{:S(2)}, u32[]{:S(2)}) collective-permute-start(f32[4,1408]{1,0:T(4,128)S(1)} %shard_map.115.refs_15_), channel_id=1, source_target_pairs={{128,384},{129,385},{130,386},{131,387},{132,388},{133,389},{134,3... | collective-permute-start | bytes 67592 | tf_op jit(solution)/shard_map/ppermute | solution.py:465
  37.1 2.2 %collective-permute-start.2 = (f32[4,1408]{1,0:T(4,128)S(1)}, f32[4,1408]{1,0:T(4,128)S(1)}, u32[]{:S(2)}, u32[]{:S(2)}) collective-permute-start(f32[4,1408]{1,0:T(4,128)S(1)} %shard_map.115.refs_15_), channel_id=1, source_target_pairs={{128,256},{256,384},{129,257},{257,385},{130,258},{258,386},{131,2... | collective-permute-start | bytes 67592 | tf_op jit(solution)/shard_map/ppermute | solution.py:466

commit v8 on v7

--- a/solution.py
+++ b/solution.py
@@ -41,10 +41,10 @@
     return pltpu.VMEM(shape, dtype)
 
 
-def tile_of_heads(columns, tile, width, first=0):
+def tile_of_heads(columns, tile, width):
     per, rows = LANES // width, columns.shape[0]
     lane = lax.broadcasted_iota(jnp.int32, (rows, LANES), 1)
-    h = first + tile * per
+    h = tile * per
     spread = jnp.broadcast_to(columns[:, h : h + 1], (rows, LANES))
     for k in range(1, per):
         other = jnp.broadcast_to(columns[:, h + k : h + k + 1], (rows, LANES))
@@ -79,6 +79,37 @@
         term = weight[k : k + 1, :] * padded_ref[8 - back : 8 - back + tokens, :]
         summed = summed + jnp.where(relative - back >= start, term, 0.0)
     return (summed * jax.nn.sigmoid(summed)).astype(jnp.bfloat16)
+
+
+def bf16_parts(value):
+    parts = []
+    for _ in range(3):
+        part = value.astype(jnp.bfloat16)
+        parts.append(part)
+        value = value - part.astype(jnp.float32)
+    return parts
+
+
+def spread_matrix(first, last, width, at):
+    row = lax.broadcasted_iota(jnp.int32, (LANES, last - first), 0)
+    head = (first + lax.broadcasted_iota(jnp.int32, (LANES, last - first), 1)) // width
+    inside = (row >= at) if at else (row < 32)
+    return jnp.where(inside & ((row & 31) == head), 1.0, 0.0).astype(jnp.bfloat16)
+
+
+def spread_rows(values, features, heads, wide_ref):
+    count = values.shape[0]
+    parts = jnp.concatenate(bf16_parts(jnp.where(
+        lax.broadcasted_iota(jnp.int32, values.shape, 1) < heads, values, 0.0
+    )), axis=0)
+    for j in range(0, features, 256):
+        wide = jnp.dot(
+            parts, spread_matrix(j, j + 256, features // heads, 0),
+            preferred_element_type=jnp.float32,
+        )
+        wide_ref[:, j : j + 256] = (
+            wide[2 * count :] + wide[count : 2 * count]
+        ) + wide[0:count]
 
 
 def sequence_index():
@@ -131,9 +162,10 @@
     log_decay = -step * to_column(rate_ref[...])
     rows = lax.broadcasted_iota(jnp.int32, (tokens, tokens), 0)
     cols = lax.broadcasted_iota(jnp.int32, (tokens, tokens), 1)
-    cum = jnp.dot(
-        log_decay, jnp.where(rows <= cols, 1.0, 0.0), precision=HIGHEST,
-        preferred_element_type=jnp.float32,
+    upper = jnp.where(rows <= cols, 1.0, 0.0).astype(jnp.bfloat16)
+    cum = sum(
+        jnp.dot(part, upper, preferred_element_type=jnp.float32)
+        for part in reversed(bf16_parts(log_decay))
     )
     cum_rows_ref[...] = cum
     step_rows_ref[...] = step
@@ -143,17 +175,22 @@
     )
     stack_ref[...] = jnp.zeros_like(stack_ref)
     stack_ref[0:heads, :] = cum
-    stack_ref[WEIGHTS_AT : WEIGHTS_AT + heads, :] = weighting
+    for k, part in enumerate(bf16_parts(weighting)):
+        at = WEIGHTS_AT * (k + 1)
+        stack_ref[at : at + heads, :] = part.astype(jnp.float32)
     columns = stack_ref[...].T
     columns_ref[...] = columns
     factor_ref[...] = jnp.where(end_start < 0, jnp.exp(columns[tokens - 1 : tokens, :]), 0.0)
     for copy in copies:
         copy.wait()
-    for j in range(x_ref.shape[1] // LANES):
-        tile = slice(j * LANES, (j + 1) * LANES)
-        weighted_ref[:, tile] = (
-            x_ref[:, tile].astype(jnp.float32) * tile_of_heads(columns, j, width, WEIGHTS_AT)
-        ).astype(jnp.bfloat16)
+    weights = columns.astype(jnp.bfloat16)
+    for j in range(0, x_ref.shape[1], 256):
+        tile = slice(j, j + 256)
+        spread = jnp.dot(
+            weights, spread_matrix(j, j + 256, width, WEIGHTS_AT),
+            preferred_element_type=jnp.float32,
+        )
+        weighted_ref[:, tile] = (x_ref[:, tile].astype(jnp.float32) * spread).astype(jnp.bfloat16)
     side = slice(0, state)
     padded_ref[0:8, :] = jnp.zeros((8, state), jnp.float32)
     padded_ref[8:, :] = b_ref[...].astype(jnp.float32)
@@ -196,12 +233,9 @@
 ):
     members, rows, padded = pieces_ref.shape
     features = padded - LANES
-    width = features // heads
     for m in range(members):
         single_ref[m : m + 1, :] = pieces_ref[m, 0:1, features:]
-    single = single_ref[...]
-    for j in range(features // LANES):
-        wide_ref[:, j * LANES : (j + 1) * LANES] = tile_of_heads(single, j, width)
+    spread_rows(single_ref[...], features, heads, wide_ref)
     product = jnp.ones((1, LANES), jnp.float32)
     for m in range(members):
         factors_ref[m : m + 1, :] = product
@@ -230,16 +264,13 @@
 
 
 def states_in_kernel(
-    heads, first_ref, second_ref, far_ref, before_ref, factors_ref, state_ref, wide_ref
+    heads, first_ref, second_ref, far_ref, before_ref, wide_ref, state_ref
 ):
     members, rows, features = before_ref.shape
     width = features // heads
     factor = wide_factor(second_ref, features, width)
     near = first_ref[:, 0:features] + second_ref[:, 0:features]
     entering = factor * far_ref[:, 0:features] + near
-    factors = factors_ref[...]
-    for j in range(features // LANES):
-        wide_ref[:, j * LANES : (j + 1) * LANES] = tile_of_heads(factors, j, width)
     for m in range(members):
         state_ref[m] = (wide_ref[m : m + 1, :] * entering + before_ref[m]).astype(jnp.bfloat16)
 
@@ -308,14 +339,15 @@
 
 
 def diagonal_kernel(turn, *refs):
-    (*sources, columns_ref, cum_rows_ref, step_rows_ref, x_ref, gate_ref) = refs[:11]
-    _, c_conv_ref, gated_ref, scale_ref, products_ref, padded_ref = refs[-6:]
+    (*sources, columns_ref, cum_rows_ref, step_rows_ref, x_ref, gate_ref, factors_ref) = refs[:12]
+    wide_ref, c_conv_ref, gated_ref, scale_ref, products_ref, padded_ref = refs[-6:]
     place = lax.axis_index(OUTER)
     early = (place == 0) & (lax.axis_index("tp") < lax.axis_size("tp") // 2)
     late = place >= 2
 
     @pl.when((early, jnp.logical_not(early | late), late)[turn])
     def _():
+        spread_rows(factors_ref[...], x_ref.shape[1], cum_rows_ref.shape[0], wide_ref)
         products_of(*sources, c_conv_ref, products_ref, padded_ref)
         diagonal_of(
             sources[4], columns_ref, cum_rows_ref, step_rows_ref, x_ref, gate_ref, products_ref,
@@ -334,9 +366,10 @@
         gated = diagonal_ref[:, tile] + scale_ref[:, tile] * carried
         gated_ref[:, tile] = gated
         squares = squares + gated * gated
-    squares_ref[...] = lax.dot_general(
-        jnp.ones((8, LANES), jnp.float32), squares, (((1,), (1,)), ((), ())),
-        precision=HIGHEST, preferred_element_type=jnp.float32,
+    ones = jnp.ones((8, LANES), jnp.bfloat16)
+    squares_ref[...] = sum(
+        lax.dot_general(ones, part, (((1,), (1,)), ((), ())), preferred_element_type=jnp.float32)
+        for part in reversed(bf16_parts(squares))
     )[0:1]
 
 
@@ -346,13 +379,8 @@
     total = squares_ref[0]
     for k in range(1, count):
         total = total + squares_ref[k]
-    first = lax.broadcasted_iota(jnp.int32, (8, total.shape[1]), 0) == 0
-    column = lax.dot_general(
-        jnp.where(first, jnp.broadcast_to(total, first.shape), 0.0),
-        jnp.ones((8, LANES), jnp.float32), (((0,), (0,)), ((), ())),
-        precision=HIGHEST, preferred_element_type=jnp.float32,
-    )
-    scale = lax.rsqrt(column / features_all + epsilon)
+    scale = lax.rsqrt(total / features_all + epsilon)
+    scale = jnp.broadcast_to(scale, (LANES, tokens)).T
     chunks = sems.shape[0]
     size = tokens // chunks
     copies = []
@@ -440,23 +468,25 @@
 
     def diagonal_terms(turn, token, *before, late=()):
         sources = [
-            c, halo, taps, taps_bias, start, b_conv, columns, cum_rows, step_rows, x,
-            gate_input,
+            c, halo, taps, taps_bias, start, b_conv, columns, cum_rows, step_rows, x, gate_input,
+            factors,
         ]
+        token = [] if token is None else [token]
         count = len(sources)
-        return call(
+        results = call(
             functools.partial(diagonal_kernel, turn),
-            [
-                out(token.shape), out((tokens, state), bf16), out((tokens, features)),
+            [out(t.shape) for t in token] + [
+                out((members, features)), out((tokens, state), bf16), out((tokens, features)),
                 out((tokens, features)),
             ],
-            *sources, token, *before, after=late, flops=20_000_000_000,
-            aliases={count + k: k for k in range(1 + len(before))},
+            *sources, *token, *before, after=late, flops=20_000_000_000,
+            aliases={count + k: k for k in range(len(token) + len(before))},
             scratch=[
                 pltpu.VMEM((tokens, tokens), jnp.float32),
                 pltpu.VMEM((tokens + 8, state), jnp.float32),
             ],
         )
+        return results
 
     total_a, *diagonal = diagonal_terms(0, total_a)
     first = lax.ppermute(total_a, OUTER, [(0, 1)])
@@ -464,13 +494,11 @@
     joined = call(functools.partial(join_kernel, heads), pair, total_b, first)
     far = lax.ppermute(joined, OUTER, [(1, 3)])
     second = lax.ppermute(joined, OUTER, [(1, 2), (2, 3)])
-    factors, *diagonal = diagonal_terms(2, factors, *diagonal, late=(joined,))
-    c_conv, diagonal, scale = diagonal
+    wide, c_conv, diagonal, scale = diagonal_terms(2, None, *diagonal, late=(joined,))
     states_in = call(
         functools.partial(states_in_kernel, heads),
         out((members, rows, features), bf16),
-        first, second, far, before, factors,
-        scratch=[pltpu.VMEM((members, features), jnp.float32)],
+        first, second, far, before, wide,
     )
     states_in = lax.all_to_all(states_in, GROUP, 0, 0)
     gated, squares = call(

time: 72.4 us -> 72.1 us (level)
  no operation moved by 1% of the time
where the time goes in v8:
time: 72.1 us; the launch traced here: 71.6 us
  blocking collectives  48.1 us (67%)
  starting transfers between devices  9.36 us (13%)
  Pallas kernels  7.13 us (10%)
  waiting for transfers between devices  6.89 us (10%)
    all_to_all x1, blocking collectives, body(): pieces = lax.all_to_all(pieces, GROUP, 0, 0)  17.6 us
    all_gather x1, blocking collectives, body(): squares = lax.all_gather(squares, 'tp')  17.2 us
    all_to_all x1, blocking collectives, body(): states_in = lax.all_to_all(states_in, GROUP, 0, 0)  13.3 us
    pallas_call x11, Pallas kernels, call(): pl.pallas_call(kernel, out_shape=list(outs) if multiple else outs, in_spe...  7.13 us
    ppermute x1, waiting for transfers between devices, body(): halo = lax.ppermute(tails, SEQ, ahead(shards, 1))  3.7 us
    ppermute x1, starting transfers between devices, body(): far = lax.ppermute(joined, OUTER, [(1, 3)])  3.66 us
    ppermute x1, starting transfers between devices, body(): halo = lax.ppermute(tails, SEQ, ahead(shards, 1))  3.12 us
    ppermute x1, waiting for transfers between devices, body(): first = lax.ppermute(total_a, OUTER, [(0, 1)])  2.32 us
  transfers between devices with their start and end apart: 4, of which 3 were waited for; matrix products, arithmetic and copies ran while one was open for 0% of the time, Pallas kernels for 5%

profile of v8, /device:TPU:65, one launch (start us, length us, event | category | flops | bytes accessed | tf_op | source)
XLA Modules:
  0.0 71.6 jit_solution(1759513919141920273)
XLA Ops:
  0.0 0.8 %shard_map.109 = (bf16[8,256]{1,0:T(8,128)(2,1)S(1)}, s32[1,8]{1,0:T(1,128)S(1)}, f32[20,256]{1,0:T(8,128)S(1)}, f32[1,20]{1,0:T(1,128)S(1)}, f32[1,20]{1,0:T(1,128)S(1)}) custom-call(bf16[256,128]{1,0:T(8,128)(2,1)} %refs_1_.1, bf16[256,128]{1,0:T(8,128)(2,1)} %refs_2_.1, s32[1,8]{1,0:T(1,128)} %bitcast.11, f32[20,256]{1,0:T(8,128)} %bitcast.8, ...), custom_call_target="tpu_custom_call" | custom-call | flops 1000000 | bytes 1000000 | tf_op jit(solution)/shard_map/pallas_call | solution.py:28
  0.8 3.1 %collective-permute-start = (bf16[8,256]{1,0:T(8,128)(2,1)S(1)}, bf16[8,256]{1,0:T(8,128)(2,1)S(1)}, u32[]{:S(2)}, u32[]{:S(2)}) collective-permute-start(bf16[8,256]{1,0:T(8,128)(2,1)S(1)} %get-tuple-element.49.refs_10_), channel_id=1, source_target_pairs={{0,4},{4,8},{8,12},{12,16},{16,20},{20,24},{24,28},{28,32},{32,36}... | collective-permute-start | bytes 12296 | tf_op jit(solution)/shard_map/ppermute | solution.py:428
  4.0 1.7 %shard_map.110 = (bf16[256,1280]{1,0:T(8,128)(2,1)S(1)}, bf16[256,128]{1,0:T(8,128)(2,1)S(1)}, bf16[256,128]{1,0:T(8,128)(2,1)S(1)}, f32[4,256]{1,0:T(4,128)S(1)...) custom-call(bf16[256,1280]{1,0:T(8,128)(2,1)} %refs_0_.1, ...), custom_call_target="tpu_custom_call" | custom-call | flops 1000000 | bytes 1000000 | tf_op jit(solution)/shard_map/pallas_call | solution.py:28
  5.7 3.7 %collective-permute-done.halo_ref.refs_1_ = bf16[8,256]{1,0:T(8,128)(2,1)S(1)} collective-permute-done((bf16[8,256]{1,0:T(8,128)(2,1)S(1)}, bf16[8,256]{1,0:T(8,128)(2,1)S(1)}, u32[]{:S(2)}, u32[]{:S(2)}) %collective-permute-start) | collective-permute-done | bytes 4128 | tf_op jit(solution)/shard_map/ppermute | solution.py:428
  9.4 0.3 shard_map.111
  9.7 0.0 copy-start
  9.8 17.6 %all_to_all.10.pieces_ref = f32[32,4,1408]{2,1,0:T(4,128)S(1)} all-to-all(f32[32,4,1408]{2,1,0:T(4,128)S(1)} %get-tuple-element.63), channel_id=1, replica_groups=mesh['za'=4,'zb'=2,'y'=4,'x'=4,'tp'=4] {'zb','y','x'}, dimensions={0} | all-to-all | bytes 1441792 | tf_op jit(solution)/shard_map/all_to_all | solution.py:457
  27.4 0.4 shard_map.112
  27.8 0.0 copy-done
  27.8 1.3 %collective-permute-start.1 = (f32[4,1408]{1,0:T(4,128)S(1)}, f32[4,1408]{1,0:T(4,128)S(1)}, u32[]{:S(2)}, u32[]{:S(2)}) collective-permute-start(f32[4,1408]{1,0:T(4,128)S(1)} %get-tuple-element.66), channel_id=1, source_target_pairs={{0,128},{1,129},{2,130},{3,131},{4,132},{5,133},{6,134},{7,135},{8... | collective-permute-start | bytes 67592 | tf_op jit(solution)/shard_map/ppermute | solution.py:492
  29.1 1.8 %shard_map.114 = (f32[4,1408]{1,0:T(4,128)S(1)}, f32[32,1280]{1,0:T(8,128)S(1)}, bf16[256,128]{1,0:T(8,128)(2,1)S(1)}, f32[256,1280]{1,0:T(8,128)S(1)}, f32[256,1280]{1,0:T(8,128)S(1)}) custom-call(bf16[256,128]{1,0:T(8,128)(2,1)S(1)} %get-tuple-element.50.refs_0_, ...), custom_call_target="tpu_custom_call", output_to_operand_aliasing={{0}: (12, {}), {1}: (13, {}), {2}: (14, {}), {3}: (15, {}),... | custom-call | flops 20000000000 | bytes 1000000 | tf_op jit(solution)/shard_map/pallas_call | solution.py:28
  30.9 2.3 %collective-permute-done.1.behind_ref.first_ref = f32[4,1408]{1,0:T(4,128)S(1)} collective-permute-done((f32[4,1408]{1,0:T(4,128)S(1)}, f32[4,1408]{1,0:T(4,128)S(1)}, u32[]{:S(2)}, u32[]{:S(2)}) %collective-permute-start.1) | collective-permute-done | bytes 22560 | tf_op jit(solution)/shard_map/ppermute | solution.py:492
  33.2 0.1 shard_map.115.refs_16_
  33.4 3.7 %collective-permute-start.3 = (f32[4,1408]{1,0:T(4,128)S(1)}, f32[4,1408]{1,0:T(4,128)S(1)}, u32[]{:S(2)}, u32[]{:S(2)}) collective-permute-start(f32[4,1408]{1,0:T(4,128)S(1)} %shard_map.115.refs_16_), channel_id=1, source_target_pairs={{128,384},{129,385},{130,386},{131,387},{132,388},{133,389},{134,3... | collective-permute-start | bytes 67592 | tf_op jit(solution)/shard_map/ppermute | solution.py:495
  37.0 1.3 %collective-permute-start.2 = (f32[4,1408]{1,0:T(4,128)S(1)}, f32[4,1408]{1,0:T(4,128)S(1)}, u32[]{:S(2)}, u32[]{:S(2)}) collective-permute-start(f32[4,1408]{1,0:T(4,128)S(1)} %shard_map.115.refs_16_), channel_id=1, source_target_pairs={{128,256},{256,384},{129,257},{257,385},{130,258},{258,386},{131,2... | collective-permute-start | bytes 67592 | tf_op jit(solution)/shard_map/ppermute | solution.py:496
  38.3 0.0 collective-permute-done.3.far_ref
  38.4 0.9 %collective-permute-done.2.second_ref = f32[4,1408]{1,0:T(4,128)S(1)} collective-permute-done((f32[4,1408]{1,0:T(4,128)S(1)}, f32[4,1408]{1,0:T(4,128)S(1)}, u32[]{:S(2)}, u32[]{:S(2)}) %collective-permute-start.2) | collective-permute-done | bytes 22560 | tf_op jit(solution)/shard_map/ppermute | solution.py:496
  39.2 0.3 shard_map.117
  39.5 13.3 %all_to_all.11.state_ref = bf16[32,4,1280]{2,1,0:T(4,128)(2,1)S(1)} all-to-all(bf16[32,4,1280]{2,1,0:T(4,128)(2,1)S(1)} %shard_map.117), channel_id=1, replica_groups=mesh['za'=4,'zb'=2,'y'=4,'x'=4,'tp'=4] {'zb','y','x'}, dimensions={0} | all-to-all | bytes 655360 | tf_op jit(solution)/shard_map/all_to_all | solution.py:503
  52.9 0.6 shard_map.118
  53.4 17.2 %all-gather.1.squares_ref = f32[4,1,256]{2,1,0:T(1,128)S(1)} all-gather(f32[1,1,256]{2,1,0:T(1,128)S(1)} %bitcast.7), channel_id=2, replica_groups=mesh['za'=4,'zb'=2,'y'=4,'x'=4,'tp'=4] {'tp'}, dimensions={0}, use_global_device_ids=true | all-gather | bytes 5120 | tf_op jit(solution)/shard_map/all_gather | solution.py:509
  70.6 1.0 %shard_map.119 = bf16[256,1280]{1,0:T(8,128)(2,1)} custom-call(f32[4,1,256]{2,1,0:T(1,128)S(1)} %all-gather.1.squares_ref, f32[256,1280]{1,0:T(8,128)S(1)} %get-tuple-element.83.gated_ref, f32[10,128]{1,0:T(8,128)S(1)} %get-tuple-element.84.gain_ref), custom_call_target="tpu_custom_call" | custom-call | flops 1000000 | bytes 1000000 | tf_op jit(solution)/shard_map/pallas_call | solution.py:28
  (2 shorter events, 0.0 us)
Async XLA Ops:
  0.8 8.6 %collective-permute-start = (bf16[8,256]{1,0:T(8,128)(2,1)S(1)}, bf16[8,256]{1,0:T(8,128)(2,1)S(1)}, u32[]{:S(2)}, u32[]{:S(2)}) collective-permute-start(bf16[8,256]{1,0:T(8,128)(2,1)S(1)} %get-tuple-element.49.refs_10_), channel_id=1, source_target_pairs={{0,4},{4,8},{8,12},{12,16},{16,20},{20,24},{24,28},{28,32},{32,36}... | collective-permute-start | bytes 12296 | tf_op jit(solution)/shard_map/ppermute | solution.py:428
  9.7 18.0 %copy-start = (bf16[256,1280]{1,0:T(8,128)(2,1)S(1)}, bf16[256,1280]{1,0:T(8,128)(2,1)}, u32[]{:S(2)}) copy-start(bf16[256,1280]{1,0:T(8,128)(2,1)} %refs_10_.5) | copy-start | bytes 1966084
  27.8 5.4 %collective-permute-start.1 = (f32[4,1408]{1,0:T(4,128)S(1)}, f32[4,1408]{1,0:T(4,128)S(1)}, u32[]{:S(2)}, u32[]{:S(2)}) collective-permute-start(f32[4,1408]{1,0:T(4,128)S(1)} %get-tuple-element.66), channel_id=1, source_target_pairs={{0,128},{1,129},{2,130},{3,131},{4,132},{5,133},{6,134},{7,135},{8... | collective-permute-start | bytes 67592 | tf_op jit(solution)/shard_map/ppermute | solution.py:492
  33.4 5.0 %collective-permute-start.3 = (f32[4,1408]{1,0:T(4,128)S(1)}, f32[4,1408]{1,0:T(4,128)S(1)}, u32[]{:S(2)}, u32[]{:S(2)}) collective-permute-start(f32[4,1408]{1,0:T(4,128)S(1)} %shard_map.115.refs_16_), channel_id=1, source_target_pairs={{128,384},{129,385},{130,386},{131,387},{132,388},{133,389},{134,3... | collective-permute-start | bytes 67592 | tf_op jit(solution)/shard_map/ppermute | solution.py:495
  37.0 2.2 %collective-permute-start.2 = (f32[4,1408]{1,0:T(4,128)S(1)}, f32[4,1408]{1,0:T(4,128)S(1)}, u32[]{:S(2)}, u32[]{:S(2)}) collective-permute-start(f32[4,1408]{1,0:T(4,128)S(1)} %shard_map.115.refs_16_), channel_id=1, source_target_pairs={{128,256},{256,384},{129,257},{257,385},{130,258},{258,386},{131,2... | collective-permute-start | bytes 67592 | tf_op jit(solution)/shard_map/ppermute | solution.py:496

commit v9 on v8

--- a/solution.py
+++ b/solution.py
@@ -13,7 +13,6 @@
 OUTER = "za"
 LANES = 128
 epsilon = 1e-05
-HIGHEST = lax.Precision.HIGHEST
 VMEM = pl.BlockSpec(memory_space=pltpu.VMEM)
 HBM = pl.BlockSpec(memory_space=pltpu.HBM)
 
@@ -229,7 +228,8 @@
 
 
 def prefix_kernel(
-    heads, pieces_ref, before_ref, factors_ref, total_a_ref, total_b_ref, single_ref, wide_ref
+    heads, pieces_ref, before_ref, factors_ref, total_a_ref, total_b_ref, total_c_ref, single_ref,
+    wide_ref,
 ):
     members, rows, padded = pieces_ref.shape
     features = padded - LANES
@@ -244,7 +244,7 @@
     for m in range(members):
         before_ref[m] = total
         total = wide_ref[m : m + 1, :] * total + pieces_ref[m, :, 0:features]
-    for total_ref in (total_a_ref, total_b_ref):
+    for total_ref in (total_a_ref, total_b_ref, total_c_ref):
         total_ref[:, 0:features] = total
         total_ref[:, features:] = jnp.broadcast_to(product, (rows, LANES))
 
@@ -256,21 +256,12 @@
     )
 
 
-def join_kernel(heads, own_ref, behind_ref, joined_ref):
-    features = own_ref.shape[1] - LANES
-    factor = wide_factor(own_ref, features, features // heads)
-    joined_ref[:, 0:features] = factor * behind_ref[:, 0:features] + own_ref[:, 0:features]
-    joined_ref[:, features:] = own_ref[:, features:]
-
-
-def states_in_kernel(
-    heads, first_ref, second_ref, far_ref, before_ref, wide_ref, state_ref
-):
-    members, rows, features = before_ref.shape
-    width = features // heads
-    factor = wide_factor(second_ref, features, width)
-    near = first_ref[:, 0:features] + second_ref[:, 0:features]
-    entering = factor * far_ref[:, 0:features] + near
+def states_in_kernel(heads, *refs):
+    *near_refs, far_ref, before_ref, wide_ref, state_ref, near_ref = refs
+    members, _, features = before_ref.shape
+    near_ref[...] = sum(ref[...] for ref in near_refs)
+    factor = wide_factor(near_ref, features, features // heads)
+    entering = factor * far_ref[:, 0:features] + near_ref[:, 0:features]
     for m in range(members):
         state_ref[m] = (wide_ref[m : m + 1, :] * entering + before_ref[m]).astype(jnp.bfloat16)
 
@@ -456,9 +447,9 @@
     )
     pieces = lax.all_to_all(pieces, GROUP, 0, 0)
     pair = out((rows, features + LANES))
-    before, factors, total_a, total_b = call(
+    before, factors, total_a, total_b, total_c = call(
         functools.partial(prefix_kernel, heads),
-        [out((members, rows, features)), out((members, LANES)), pair, pair],
+        [out((members, rows, features)), out((members, LANES)), pair, pair, pair],
         pieces,
         scratch=[
             pltpu.VMEM((members, LANES), jnp.float32),
@@ -466,39 +457,42 @@
         ],
     )
 
-    def diagonal_terms(turn, token, *before, late=()):
+    def diagonal_terms(turn, token, *before):
         sources = [
             c, halo, taps, taps_bias, start, b_conv, columns, cum_rows, step_rows, x, gate_input,
             factors,
         ]
         token = [] if token is None else [token]
         count = len(sources)
-        results = call(
+        return call(
             functools.partial(diagonal_kernel, turn),
             [out(t.shape) for t in token] + [
                 out((members, features)), out((tokens, state), bf16), out((tokens, features)),
                 out((tokens, features)),
             ],
-            *sources, *token, *before, after=late, flops=20_000_000_000,
+            *sources, *token, *before, flops=20_000_000_000,
             aliases={count + k: k for k in range(len(token) + len(before))},
             scratch=[
                 pltpu.VMEM((tokens, tokens), jnp.float32),
                 pltpu.VMEM((tokens + 8, state), jnp.float32),
             ],
         )
-        return results
+
+    def send(total, *pairs):
+        return lax.ppermute(total, OUTER, pairs)
 
     total_a, *diagonal = diagonal_terms(0, total_a)
-    first = lax.ppermute(total_a, OUTER, [(0, 1)])
-    total_b, *diagonal = diagonal_terms(1, total_b, *diagonal)
-    joined = call(functools.partial(join_kernel, heads), pair, total_b, first)
-    far = lax.ppermute(joined, OUTER, [(1, 3)])
-    second = lax.ppermute(joined, OUTER, [(1, 2), (2, 3)])
-    wide, c_conv, diagonal, scale = diagonal_terms(2, None, *diagonal, late=(joined,))
+    near_a = send(total_a, (0, 1))
+    near_b = send(total_b, (1, 2))
+    total_c, *diagonal = diagonal_terms(1, total_c, *diagonal)
+    far = send(total_c, (0, 2), (1, 3))
+    near_d = send(total_c, (2, 3))
+    wide, c_conv, diagonal, scale = diagonal_terms(2, None, *diagonal)
     states_in = call(
         functools.partial(states_in_kernel, heads),
         out((members, rows, features), bf16),
-        first, second, far, before, wide,
+        near_a, near_b, near_d, far, before, wide,
+        scratch=[pltpu.VMEM(pair.shape, jnp.float32)],
     )
     states_in = lax.all_to_all(states_in, GROUP, 0, 0)
     gated, squares = call(

time: 72.1 us -> 78.4 us (1.087)
  the two profiles are of different devices: /device:TPU:65 before, /device:TPU:1 now
where the time goes in v9:
time: 78.4 us; the launch traced here: 78.1 us
  blocking collectives  50.7 us (65%)
  starting transfers between devices  19.3 us (25%)
  Pallas kernels  7.05 us (9%)
  waiting for transfers between devices  0.88 us (1%)
    all_to_all x1, blocking collectives, body(): pieces = lax.all_to_all(pieces, GROUP, 0, 0)  18.8 us
    all_gather x1, blocking collectives, body(): squares = lax.all_gather(squares, 'tp')  18.6 us
    ppermute x4, starting transfers between devices, send(): return lax.ppermute(total, OUTER, pairs)  15.4 us
    all_to_all x1, blocking collectives, body(): states_in = lax.all_to_all(states_in, GROUP, 0, 0)  13.2 us
    pallas_call x10, Pallas kernels, call(): pl.pallas_call(kernel, out_shape=list(outs) if multiple else outs, in_spe...  7.05 us
    ppermute x1, starting transfers between devices, body(): halo = lax.ppermute(tails, SEQ, ahead(shards, 1))  3.93 us
  transfers between devices with their start and end apart: 5, of which 1 were waited for; matrix products, arithmetic and copies ran while one was open for 0% of the time, Pallas kernels for 2%

profile of v9, /device:TPU:1, one launch (start us, length us, event | category | flops | bytes accessed | tf_op | source)
XLA Modules:
  0.0 78.1 jit_solution(13552779746145481178)
XLA Ops:
  0.0 0.8 %shard_map.109 = (bf16[8,256]{1,0:T(8,128)(2,1)S(1)}, s32[1,8]{1,0:T(1,128)S(1)}, f32[20,256]{1,0:T(8,128)S(1)}, f32[1,20]{1,0:T(1,128)S(1)}, f32[1,20]{1,0:T(1,128)S(1)}) custom-call(bf16[256,128]{1,0:T(8,128)(2,1)} %refs_1_.1, bf16[256,128]{1,0:T(8,128)(2,1)} %refs_2_.1, s32[1,8]{1,0:T(1,128)} %bitcast.11, f32[20,256]{1,0:T(8,128)} %bitcast.8, ...), custom_call_target="tpu_custom_call" | custom-call | flops 1000000 | bytes 1000000 | tf_op jit(solution)/shard_map/pallas_call | solution.py:27
  0.8 3.9 %collective-permute-start = (bf16[8,256]{1,0:T(8,128)(2,1)S(1)}, bf16[8,256]{1,0:T(8,128)(2,1)S(1)}, u32[]{:S(2)}, u32[]{:S(2)}) collective-permute-start(bf16[8,256]{1,0:T(8,128)(2,1)S(1)} %get-tuple-element.50.refs_10_), channel_id=1, source_target_pairs={{0,4},{4,8},{8,12},{12,16},{16,20},{20,24},{24,28},{28,32},{32,36}... | collective-permute-start | bytes 12296 | tf_op jit(solution)/shard_map/ppermute | solution.py:419
  4.8 1.7 %shard_map.110 = (bf16[256,1280]{1,0:T(8,128)(2,1)S(1)}, bf16[256,128]{1,0:T(8,128)(2,1)S(1)}, bf16[256,128]{1,0:T(8,128)(2,1)S(1)}, f32[4,256]{1,0:T(4,128)S(1)...) custom-call(bf16[256,1280]{1,0:T(8,128)(2,1)} %refs_0_.1, ...), custom_call_target="tpu_custom_call" | custom-call | flops 1000000 | bytes 1000000 | tf_op jit(solution)/shard_map/pallas_call | solution.py:27
  6.5 0.0 collective-permute-done.halo_ref.refs_1_
  6.5 0.3 shard_map.111
  6.9 0.0 copy-start
  6.9 18.8 %all_to_all.10.pieces_ref = f32[32,4,1408]{2,1,0:T(4,128)S(1)} all-to-all(f32[32,4,1408]{2,1,0:T(4,128)S(1)} %get-tuple-element.64), channel_id=1, replica_groups=mesh['za'=4,'zb'=2,'y'=4,'x'=4,'tp'=4] {'zb','y','x'}, dimensions={0} | all-to-all | bytes 1441792 | tf_op jit(solution)/shard_map/all_to_all | solution.py:448
  25.7 0.4 shard_map.112
  26.1 0.0 copy-done
  26.1 1.8 %shard_map.113 = (f32[4,1408]{1,0:T(4,128)S(1)}, f32[32,1280]{1,0:T(8,128)S(1)}, bf16[256,128]{1,0:T(8,128)(2,1)S(1)}, f32[256,1280]{1,0:T(8,128)S(1)}, f32[256,1280]{1,0:T(8,128)S(1)}) custom-call(bf16[256,128]{1,0:T(8,128)(2,1)S(1)} %get-tuple-element.51.refs_0_, ...), custom_call_target="tpu_custom_call", output_to_operand_aliasing={{0}: (12, {})} | custom-call | flops 20000000000 | bytes 1000000 | tf_op jit(solution)/shard_map/pallas_call | solution.py:27
  28.0 7.0 %collective-permute-start.4 = (f32[4,1408]{1,0:T(4,128)S(1)}, f32[4,1408]{1,0:T(4,128)S(1)}, u32[]{:S(2)}, u32[]{:S(2)}) collective-permute-start(f32[4,1408]{1,0:T(4,128)S(1)} %get-tuple-element.74), channel_id=1, source_target_pairs={{0,256},{128,384},{1,257},{129,385},{2,258},{130,386},{3,259},{131... | collective-permute-start | bytes 67592 | tf_op jit(solution)/shard_map/ppermute | solution.py:482
  35.0 0.7 collective-permute-start.3
  35.7 0.7 collective-permute-start.2
  36.4 7.0 %collective-permute-start.1 = (f32[4,1408]{1,0:T(4,128)S(1)}, f32[4,1408]{1,0:T(4,128)S(1)}, u32[]{:S(2)}, u32[]{:S(2)}) collective-permute-start(f32[4,1408]{1,0:T(4,128)S(1)} %get-tuple-element.67), channel_id=1, source_target_pairs={{0,128},{1,129},{2,130},{3,131},{4,132},{5,133},{6,134},{7,135},{8... | collective-permute-start | bytes 67592 | tf_op jit(solution)/shard_map/ppermute | solution.py:482
  43.4 0.0 collective-permute-done.2.refs_1_
  43.4 0.9 %collective-permute-done.1.refs_0_ = f32[4,1408]{1,0:T(4,128)S(1)} collective-permute-done((f32[4,1408]{1,0:T(4,128)S(1)}, f32[4,1408]{1,0:T(4,128)S(1)}, u32[]{:S(2)}, u32[]{:S(2)}) %collective-permute-start.1) | collective-permute-done | bytes 22560 | tf_op jit(solution)/shard_map/ppermute | solution.py:482
  44.3 0.0 collective-permute-done.4.refs_3_
  44.3 0.0 collective-permute-done.3.refs_2_
  44.3 0.3 shard_map.116
  44.6 13.2 %all_to_all.11.state_ref = bf16[32,4,1280]{2,1,0:T(4,128)(2,1)S(1)} all-to-all(bf16[32,4,1280]{2,1,0:T(4,128)(2,1)S(1)} %shard_map.116), channel_id=1, replica_groups=mesh['za'=4,'zb'=2,'y'=4,'x'=4,'tp'=4] {'zb','y','x'}, dimensions={0} | all-to-all | bytes 655360 | tf_op jit(solution)/shard_map/all_to_all | solution.py:497
  57.9 0.6 shard_map.117
  58.4 18.6 %all-gather.1.squares_ref = f32[4,1,256]{2,1,0:T(1,128)S(1)} all-gather(f32[1,1,256]{2,1,0:T(1,128)S(1)} %bitcast.7), channel_id=2, replica_groups=mesh['za'=4,'zb'=2,'y'=4,'x'=4,'tp'=4] {'tp'}, dimensions={0}, use_global_device_ids=true | all-gather | bytes 5120 | tf_op jit(solution)/shard_map/all_gather | solution.py:503
  77.1 1.0 %shard_map.118 = bf16[256,1280]{1,0:T(8,128)(2,1)} custom-call(f32[4,1,256]{2,1,0:T(1,128)S(1)} %all-gather.1.squares_ref, f32[256,1280]{1,0:T(8,128)S(1)} %get-tuple-element.85.gated_ref, f32[10,128]{1,0:T(8,128)S(1)} %get-tuple-element.86.gain_ref), custom_call_target="tpu_custom_call" | custom-call | flops 1000000 | bytes 1000000 | tf_op jit(solution)/shard_map/pallas_call | solution.py:27
  (2 shorter events, 0.0 us)
Async XLA Ops:
  0.8 5.7 %collective-permute-start = (bf16[8,256]{1,0:T(8,128)(2,1)S(1)}, bf16[8,256]{1,0:T(8,128)(2,1)S(1)}, u32[]{:S(2)}, u32[]{:S(2)}) collective-permute-start(bf16[8,256]{1,0:T(8,128)(2,1)S(1)} %get-tuple-element.50.refs_10_), channel_id=1, source_target_pairs={{0,4},{4,8},{8,12},{12,16},{16,20},{20,24},{24,28},{28,32},{32,36}... | collective-permute-start | bytes 12296 | tf_op jit(solution)/shard_map/ppermute | solution.py:419
  6.9 19.2 %copy-start = (bf16[256,1280]{1,0:T(8,128)(2,1)S(1)}, bf16[256,1280]{1,0:T(8,128)(2,1)}, u32[]{:S(2)}) copy-start(bf16[256,1280]{1,0:T(8,128)(2,1)} %refs_10_.5) | copy-start | bytes 1966084
  28.0 16.3 %collective-permute-start.4 = (f32[4,1408]{1,0:T(4,128)S(1)}, f32[4,1408]{1,0:T(4,128)S(1)}, u32[]{:S(2)}, u32[]{:S(2)}) collective-permute-start(f32[4,1408]{1,0:T(4,128)S(1)} %get-tuple-element.74), channel_id=1, source_target_pairs={{0,256},{128,384},{1,257},{129,385},{2,258},{130,386},{3,259},{131... | collective-permute-start | bytes 67592 | tf_op jit(solution)/shard_map/ppermute | solution.py:482
  35.0 9.3 %collective-permute-start.3 = (f32[4,1408]{1,0:T(4,128)S(1)}, f32[4,1408]{1,0:T(4,128)S(1)}, u32[]{:S(2)}, u32[]{:S(2)}) collective-permute-start(f32[4,1408]{1,0:T(4,128)S(1)} %get-tuple-element.74), channel_id=1, source_target_pairs={{256,384},{257,385},{258,386},{259,387},{260,388},{261,389},{262,3... | collective-permute-start | bytes 67592 | tf_op jit(solution)/shard_map/ppermute | solution.py:482
  35.7 7.7 %collective-permute-start.2 = (f32[4,1408]{1,0:T(4,128)S(1)}, f32[4,1408]{1,0:T(4,128)S(1)}, u32[]{:S(2)}, u32[]{:S(2)}) collective-permute-start(f32[4,1408]{1,0:T(4,128)S(1)} %get-tuple-element.68), channel_id=1, source_target_pairs={{128,256},{129,257},{130,258},{131,259},{132,260},{133,261},{134,2... | collective-permute-start | bytes 67592 | tf_op jit(solution)/shard_map/ppermute | solution.py:482
  36.4 7.9 %collective-permute-start.1 = (f32[4,1408]{1,0:T(4,128)S(1)}, f32[4,1408]{1,0:T(4,128)S(1)}, u32[]{:S(2)}, u32[]{:S(2)}) collective-permute-start(f32[4,1408]{1,0:T(4,128)S(1)} %get-tuple-element.67), channel_id=1, source_target_pairs={{0,128},{1,129},{2,130},{3,131},{4,132},{5,133},{6,134},{7,135},{8... | collective-permute-start | bytes 67592 | tf_op jit(solution)/shard_map/ppermute | solution.py:482

commit v10 on v9

--- a/solution.py
+++ b/solution.py
@@ -334,9 +334,8 @@
     wide_ref, c_conv_ref, gated_ref, scale_ref, products_ref, padded_ref = refs[-6:]
     place = lax.axis_index(OUTER)
     early = (place == 0) & (lax.axis_index("tp") < lax.axis_size("tp") // 2)
-    late = place >= 2
-
-    @pl.when((early, jnp.logical_not(early | late), late)[turn])
+
+    @pl.when((early, jnp.logical_not(early))[turn])
     def _():
         spread_rows(factors_ref[...], x_ref.shape[1], cum_rows_ref.shape[0], wide_ref)
         products_of(*sources, c_conv_ref, products_ref, padded_ref)
@@ -483,15 +482,13 @@
 
     total_a, *diagonal = diagonal_terms(0, total_a)
     near_a = send(total_a, (0, 1))
-    near_b = send(total_b, (1, 2))
-    total_c, *diagonal = diagonal_terms(1, total_c, *diagonal)
-    far = send(total_c, (0, 2), (1, 3))
-    near_d = send(total_c, (2, 3))
-    wide, c_conv, diagonal, scale = diagonal_terms(2, None, *diagonal)
+    far = send(total_b, (0, 2), (1, 3))
+    near_b = send(total_c, (1, 2), (2, 3))
+    wide, c_conv, diagonal, scale = diagonal_terms(1, None, *diagonal)
     states_in = call(
         functools.partial(states_in_kernel, heads),
         out((members, rows, features), bf16),
-        near_a, near_b, near_d, far, before, wide,
+        near_a, near_b, far, before, wide,
         scratch=[pltpu.VMEM(pair.shape, jnp.float32)],
     )
     states_in = lax.all_to_all(states_in, GROUP, 0, 0)

time: 78.4 us -> 77.7 us (level)
    ppermute x4 -> x3, starting transfers between devices: 15.4 us -> 15 us  [send(): return lax.ppermute(total, OUTER, pairs)]
    pallas_call x10 -> x9, Pallas kernels: 7.05 us -> 7.03 us  [call(): pl.pallas_call(kernel, out_shape=list(outs) if multiple else outs, in_spe...]
  transfers between devices with their start and end apart: 5 -> 4, of which waited for: 1 -> 1; matrix products, arithmetic and copies ran while one was open for 0% -> 0% of each run, Pallas kernels for 2% -> 5%
where the time goes in v10:
time: 77.7 us; the launch traced here: 77.4 us
  blocking collectives  50.4 us (65%)
  starting transfers between devices  18.9 us (24%)
  Pallas kernels  7.03 us (9%)
  waiting for transfers between devices  0.87 us (1%)
    all_to_all x1, blocking collectives, body(): pieces = lax.all_to_all(pieces, GROUP, 0, 0)  18.8 us
    all_gather x1, blocking collectives, body(): squares = lax.all_gather(squares, 'tp')  18.4 us
    ppermute x3, starting transfers between devices, send(): return lax.ppermute(total, OUTER, pairs)  15 us
    all_to_all x1, blocking collectives, body(): states_in = lax.all_to_all(states_in, GROUP, 0, 0)  13.2 us
    pallas_call x9, Pallas kernels, call(): pl.pallas_call(kernel, out_shape=list(outs) if multiple else outs, in_spe...  7.03 us
    ppermute x1, starting transfers between devices, body(): halo = lax.ppermute(tails, SEQ, ahead(shards, 1))  3.93 us
  transfers between devices with their start and end apart: 4, of which 1 were waited for; matrix products, arithmetic and copies ran while one was open for 0% of the time, Pallas kernels for 5%

profile of v10, /device:TPU:1, one launch (start us, length us, event | category | flops | bytes accessed | tf_op | source)
XLA Modules:
  0.0 77.4 jit_solution(10207225847570758557)
XLA Ops:
  0.0 0.8 %shard_map.109 = (bf16[8,256]{1,0:T(8,128)(2,1)S(1)}, s32[1,8]{1,0:T(1,128)S(1)}, f32[20,256]{1,0:T(8,128)S(1)}, f32[1,20]{1,0:T(1,128)S(1)}, f32[1,20]{1,0:T(1,128)S(1)}) custom-call(bf16[256,128]{1,0:T(8,128)(2,1)} %refs_1_.1, bf16[256,128]{1,0:T(8,128)(2,1)} %refs_2_.1, s32[1,8]{1,0:T(1,128)} %bitcast.11, f32[20,256]{1,0:T(8,128)} %bitcast.8, ...), custom_call_target="tpu_custom_call" | custom-call | flops 1000000 | bytes 1000000 | tf_op jit(solution)/shard_map/pallas_call | solution.py:27
  0.8 3.9 %collective-permute-start = (bf16[8,256]{1,0:T(8,128)(2,1)S(1)}, bf16[8,256]{1,0:T(8,128)(2,1)S(1)}, u32[]{:S(2)}, u32[]{:S(2)}) collective-permute-start(bf16[8,256]{1,0:T(8,128)(2,1)S(1)} %get-tuple-element.45.refs_10_), channel_id=1, source_target_pairs={{0,4},{4,8},{8,12},{12,16},{16,20},{20,24},{24,28},{28,32},{32,36}... | collective-permute-start | bytes 12296 | tf_op jit(solution)/shard_map/ppermute | solution.py:418
  4.8 1.7 %shard_map.110 = (bf16[256,1280]{1,0:T(8,128)(2,1)S(1)}, bf16[256,128]{1,0:T(8,128)(2,1)S(1)}, bf16[256,128]{1,0:T(8,128)(2,1)S(1)}, f32[4,256]{1,0:T(4,128)S(1)...) custom-call(bf16[256,1280]{1,0:T(8,128)(2,1)} %refs_0_.1, ...), custom_call_target="tpu_custom_call" | custom-call | flops 1000000 | bytes 1000000 | tf_op jit(solution)/shard_map/pallas_call | solution.py:27
  6.5 0.0 collective-permute-done.halo_ref.refs_1_
  6.5 0.3 shard_map.111
  6.9 0.0 copy-start
  6.9 18.8 %all_to_all.10.pieces_ref = f32[32,4,1408]{2,1,0:T(4,128)S(1)} all-to-all(f32[32,4,1408]{2,1,0:T(4,128)S(1)} %get-tuple-element.59), channel_id=1, replica_groups=mesh['za'=4,'zb'=2,'y'=4,'x'=4,'tp'=4] {'zb','y','x'}, dimensions={0} | all-to-all | bytes 1441792 | tf_op jit(solution)/shard_map/all_to_all | solution.py:447
  25.7 0.4 shard_map.112
  26.1 0.7 collective-permute-start.2
  26.8 13.1 %collective-permute-start.3 = (f32[4,1408]{1,0:T(4,128)S(1)}, f32[4,1408]{1,0:T(4,128)S(1)}, u32[]{:S(2)}, u32[]{:S(2)}) collective-permute-start(f32[4,1408]{1,0:T(4,128)S(1)} %get-tuple-element.64), channel_id=1, source_target_pairs={{0,256},{128,384},{1,257},{129,385},{2,258},{130,386},{3,259},{131... | collective-permute-start | bytes 67592 | tf_op jit(solution)/shard_map/ppermute | solution.py:481
  39.8 0.0 copy-done
  39.8 1.8 %shard_map.113 = (f32[4,1408]{1,0:T(4,128)S(1)}, f32[32,1280]{1,0:T(8,128)S(1)}, bf16[256,128]{1,0:T(8,128)(2,1)S(1)}, f32[256,1280]{1,0:T(8,128)S(1)}, f32[256,1280]{1,0:T(8,128)S(1)}) custom-call(bf16[256,128]{1,0:T(8,128)(2,1)S(1)} %get-tuple-element.46.refs_0_, ...), custom_call_target="tpu_custom_call", output_to_operand_aliasing={{0}: (12, {})} | custom-call | flops 20000000000 | bytes 1000000 | tf_op jit(solution)/shard_map/pallas_call | solution.py:27
  41.7 1.3 %collective-permute-start.1 = (f32[4,1408]{1,0:T(4,128)S(1)}, f32[4,1408]{1,0:T(4,128)S(1)}, u32[]{:S(2)}, u32[]{:S(2)}) collective-permute-start(f32[4,1408]{1,0:T(4,128)S(1)} %get-tuple-element.62), channel_id=1, source_target_pairs={{0,128},{1,129},{2,130},{3,131},{4,132},{5,133},{6,134},{7,135},{8... | collective-permute-start | bytes 67592 | tf_op jit(solution)/shard_map/ppermute | solution.py:481
  43.0 0.0 collective-permute-done.2.refs_1_
  43.0 0.0 collective-permute-done.3.refs_2_
  43.0 0.9 %collective-permute-done.1.refs_0_ = f32[4,1408]{1,0:T(4,128)S(1)} collective-permute-done((f32[4,1408]{1,0:T(4,128)S(1)}, f32[4,1408]{1,0:T(4,128)S(1)}, u32[]{:S(2)}, u32[]{:S(2)}) %collective-permute-start.1) | collective-permute-done | bytes 22560 | tf_op jit(solution)/shard_map/ppermute | solution.py:481
  43.9 0.3 shard_map.115
  44.2 13.2 %all_to_all.11.state_ref = bf16[32,4,1280]{2,1,0:T(4,128)(2,1)S(1)} all-to-all(bf16[32,4,1280]{2,1,0:T(4,128)(2,1)S(1)} %shard_map.115), channel_id=1, replica_groups=mesh['za'=4,'zb'=2,'y'=4,'x'=4,'tp'=4] {'zb','y','x'}, dimensions={0} | all-to-all | bytes 655360 | tf_op jit(solution)/shard_map/all_to_all | solution.py:494
  57.4 0.6 shard_map.116
  58.0 18.4 %all-gather.1.squares_ref = f32[4,1,256]{2,1,0:T(1,128)S(1)} all-gather(f32[1,1,256]{2,1,0:T(1,128)S(1)} %bitcast.7), channel_id=2, replica_groups=mesh['za'=4,'zb'=2,'y'=4,'x'=4,'tp'=4] {'tp'}, dimensions={0}, use_global_device_ids=true | all-gather | bytes 5120 | tf_op jit(solution)/shard_map/all_gather | solution.py:500
  76.3 1.0 %shard_map.117 = bf16[256,1280]{1,0:T(8,128)(2,1)} custom-call(f32[4,1,256]{2,1,0:T(1,128)S(1)} %all-gather.1.squares_ref, f32[256,1280]{1,0:T(8,128)S(1)} %get-tuple-element.75.gated_ref, f32[10,128]{1,0:T(8,128)S(1)} %get-tuple-element.76.gain_ref), custom_call_target="tpu_custom_call" | custom-call | flops 1000000 | bytes 1000000 | tf_op jit(solution)/shard_map/pallas_call | solution.py:27
  (1 shorter events, 0.0 us)
Async XLA Ops:
  0.8 5.7 %collective-permute-start = (bf16[8,256]{1,0:T(8,128)(2,1)S(1)}, bf16[8,256]{1,0:T(8,128)(2,1)S(1)}, u32[]{:S(2)}, u32[]{:S(2)}) collective-permute-start(bf16[8,256]{1,0:T(8,128)(2,1)S(1)} %get-tuple-element.45.refs_10_), channel_id=1, source_target_pairs={{0,4},{4,8},{8,12},{12,16},{16,20},{20,24},{24,28},{28,32},{32,36}... | collective-permute-start | bytes 12296 | tf_op jit(solution)/shard_map/ppermute | solution.py:418
  6.9 33.0 %copy-start = (bf16[256,1280]{1,0:T(8,128)(2,1)S(1)}, bf16[256,1280]{1,0:T(8,128)(2,1)}, u32[]{:S(2)}) copy-start(bf16[256,1280]{1,0:T(8,128)(2,1)} %refs_10_.3) | copy-start | bytes 1966084
  26.1 16.9 %collective-permute-start.2 = (f32[4,1408]{1,0:T(4,128)S(1)}, f32[4,1408]{1,0:T(4,128)S(1)}, u32[]{:S(2)}, u32[]{:S(2)}) collective-permute-start(f32[4,1408]{1,0:T(4,128)S(1)} %get-tuple-element.63), channel_id=1, source_target_pairs={{128,256},{256,384},{129,257},{257,385},{130,258},{258,386},{131,2... | collective-permute-start | bytes 67592 | tf_op jit(solution)/shard_map/ppermute | solution.py:481
  26.8 16.2 %collective-permute-start.3 = (f32[4,1408]{1,0:T(4,128)S(1)}, f32[4,1408]{1,0:T(4,128)S(1)}, u32[]{:S(2)}, u32[]{:S(2)}) collective-permute-start(f32[4,1408]{1,0:T(4,128)S(1)} %get-tuple-element.64), channel_id=1, source_target_pairs={{0,256},{128,384},{1,257},{129,385},{2,258},{130,386},{3,259},{131... | collective-permute-start | bytes 67592 | tf_op jit(solution)/shard_map/ppermute | solution.py:481
  41.7 2.2 %collective-permute-start.1 = (f32[4,1408]{1,0:T(4,128)S(1)}, f32[4,1408]{1,0:T(4,128)S(1)}, u32[]{:S(2)}, u32[]{:S(2)}) collective-permute-start(f32[4,1408]{1,0:T(4,128)S(1)} %get-tuple-element.62), channel_id=1, source_target_pairs={{0,128},{1,129},{2,130},{3,131},{4,132},{5,133},{6,134},{7,135},{8... | collective-permute-start | bytes 67592 | tf_op jit(solution)/shard_map/ppermute | solution.py:481

commit v11 on v10

--- a/solution.py
+++ b/solution.py
@@ -333,9 +333,8 @@
     (*sources, columns_ref, cum_rows_ref, step_rows_ref, x_ref, gate_ref, factors_ref) = refs[:12]
     wide_ref, c_conv_ref, gated_ref, scale_ref, products_ref, padded_ref = refs[-6:]
     place = lax.axis_index(OUTER)
-    early = (place == 0) & (lax.axis_index("tp") < lax.axis_size("tp") // 2)
-
-    @pl.when((early, jnp.logical_not(early))[turn])
+
+    @pl.when((place == 0, place == 1, place >= 2)[turn])
     def _():
         spread_rows(factors_ref[...], x_ref.shape[1], cum_rows_ref.shape[0], wide_ref)
         products_of(*sources, c_conv_ref, products_ref, padded_ref)
@@ -482,9 +481,10 @@
 
     total_a, *diagonal = diagonal_terms(0, total_a)
     near_a = send(total_a, (0, 1))
+    total_b, *diagonal = diagonal_terms(1, total_b, *diagonal)
     far = send(total_b, (0, 2), (1, 3))
     near_b = send(total_c, (1, 2), (2, 3))
-    wide, c_conv, diagonal, scale = diagonal_terms(1, None, *diagonal)
+    wide, c_conv, diagonal, scale = diagonal_terms(2, None, *diagonal)
     states_in = call(
         functools.partial(states_in_kernel, heads),
         out((members, rows, features), bf16),

time: 77.7 us -> 75.3 us (0.969)
  starting transfers between devices: 18.9 us -> 16.5 us
    ppermute x3, starting transfers between devices: 15 us -> 12.6 us  [send(): return lax.ppermute(total, OUTER, pairs)]
    pallas_call x9 -> x10, Pallas kernels: 7.03 us -> 7.05 us  [call(): pl.pallas_call(kernel, out_shape=list(outs) if multiple else outs, in_spe...]
where the time goes in v11:
time: 75.3 us; the launch traced here: 75 us
  blocking collectives  50.4 us (67%)
  starting transfers between devices  16.5 us (22%)
  Pallas kernels  7.05 us (9%)
  waiting for transfers between devices  0.87 us (1%)
    all_to_all x1, blocking collectives, body(): pieces = lax.all_to_all(pieces, GROUP, 0, 0)  18.8 us
    all_gather x1, blocking collectives, body(): squares = lax.all_gather(squares, 'tp')  18.4 us
    all_to_all x1, blocking collectives, body(): states_in = lax.all_to_all(states_in, GROUP, 0, 0)  13.2 us
    ppermute x3, starting transfers between devices, send(): return lax.ppermute(total, OUTER, pairs)  12.6 us
    pallas_call x10, Pallas kernels, call(): pl.pallas_call(kernel, out_shape=list(outs) if multiple else outs, in_spe...  7.05 us
    ppermute x1, starting transfers between devices, body(): halo = lax.ppermute(tails, SEQ, ahead(shards, 1))  3.93 us
  transfers between devices with their start and end apart: 4, of which 1 were waited for; matrix products, arithmetic and copies ran while one was open for 0% of the time, Pallas kernels for 5%

profile of v11, /device:TPU:1, one launch (start us, length us, event | category | flops | bytes accessed | tf_op | source)
XLA Modules:
  0.0 75.0 jit_solution(7831740725554900227)
XLA Ops:
  0.0 0.8 %shard_map.109 = (bf16[8,256]{1,0:T(8,128)(2,1)S(1)}, s32[1,8]{1,0:T(1,128)S(1)}, f32[20,256]{1,0:T(8,128)S(1)}, f32[1,20]{1,0:T(1,128)S(1)}, f32[1,20]{1,0:T(1,128)S(1)}) custom-call(bf16[256,128]{1,0:T(8,128)(2,1)} %refs_1_.1, bf16[256,128]{1,0:T(8,128)(2,1)} %refs_2_.1, s32[1,8]{1,0:T(1,128)} %bitcast.11, f32[20,256]{1,0:T(8,128)} %bitcast.8, ...), custom_call_target="tpu_custom_call" | custom-call | flops 1000000 | bytes 1000000 | tf_op jit(solution)/shard_map/pallas_call | solution.py:27
  0.8 3.9 %collective-permute-start = (bf16[8,256]{1,0:T(8,128)(2,1)S(1)}, bf16[8,256]{1,0:T(8,128)(2,1)S(1)}, u32[]{:S(2)}, u32[]{:S(2)}) collective-permute-start(bf16[8,256]{1,0:T(8,128)(2,1)S(1)} %get-tuple-element.50.refs_10_), channel_id=1, source_target_pairs={{0,4},{4,8},{8,12},{12,16},{16,20},{20,24},{24,28},{28,32},{32,36}... | collective-permute-start | bytes 12296 | tf_op jit(solution)/shard_map/ppermute | solution.py:417
  4.8 1.7 %shard_map.110 = (bf16[256,1280]{1,0:T(8,128)(2,1)S(1)}, bf16[256,128]{1,0:T(8,128)(2,1)S(1)}, bf16[256,128]{1,0:T(8,128)(2,1)S(1)}, f32[4,256]{1,0:T(4,128)S(1)...) custom-call(bf16[256,1280]{1,0:T(8,128)(2,1)} %refs_0_.1, ...), custom_call_target="tpu_custom_call" | custom-call | flops 1000000 | bytes 1000000 | tf_op jit(solution)/shard_map/pallas_call | solution.py:27
  6.5 0.0 collective-permute-done.halo_ref.refs_1_
  6.5 0.3 shard_map.111
  6.9 0.0 copy-start
  6.9 18.8 %all_to_all.10.pieces_ref = f32[32,4,1408]{2,1,0:T(4,128)S(1)} all-to-all(f32[32,4,1408]{2,1,0:T(4,128)S(1)} %get-tuple-element.64), channel_id=1, replica_groups=mesh['za'=4,'zb'=2,'y'=4,'x'=4,'tp'=4] {'zb','y','x'}, dimensions={0} | all-to-all | bytes 1441792 | tf_op jit(solution)/shard_map/all_to_all | solution.py:446
  25.7 0.4 shard_map.112
  26.1 0.7 collective-permute-start.2
  26.8 0.0 copy-done
  26.8 1.8 %shard_map.113 = (f32[4,1408]{1,0:T(4,128)S(1)}, f32[32,1280]{1,0:T(8,128)S(1)}, bf16[256,128]{1,0:T(8,128)(2,1)S(1)}, f32[256,1280]{1,0:T(8,128)S(1)}, f32[256,1280]{1,0:T(8,128)S(1)}) custom-call(bf16[256,128]{1,0:T(8,128)(2,1)S(1)} %get-tuple-element.51.refs_0_, ...), custom_call_target="tpu_custom_call", output_to_operand_aliasing={{0}: (12, {})} | custom-call | flops 20000000000 | bytes 1000000 | tf_op jit(solution)/shard_map/pallas_call | solution.py:27
  28.6 8.6 %collective-permute-start.1 = (f32[4,1408]{1,0:T(4,128)S(1)}, f32[4,1408]{1,0:T(4,128)S(1)}, u32[]{:S(2)}, u32[]{:S(2)}) collective-permute-start(f32[4,1408]{1,0:T(4,128)S(1)} %get-tuple-element.67), channel_id=1, source_target_pairs={{0,128},{1,129},{2,130},{3,131},{4,132},{5,133},{6,134},{7,135},{8... | collective-permute-start | bytes 67592 | tf_op jit(solution)/shard_map/ppermute | solution.py:480
  37.2 3.4 %collective-permute-start.3 = (f32[4,1408]{1,0:T(4,128)S(1)}, f32[4,1408]{1,0:T(4,128)S(1)}, u32[]{:S(2)}, u32[]{:S(2)}) collective-permute-start(f32[4,1408]{1,0:T(4,128)S(1)} %get-tuple-element.74), channel_id=1, source_target_pairs={{0,256},{128,384},{1,257},{129,385},{2,258},{130,386},{3,259},{131... | collective-permute-start | bytes 67592 | tf_op jit(solution)/shard_map/ppermute | solution.py:480
  40.6 0.0 collective-permute-done.2.refs_1_
  40.6 0.0 collective-permute-done.1.refs_0_
  40.6 0.9 %collective-permute-done.3.refs_2_ = f32[4,1408]{1,0:T(4,128)S(1)} collective-permute-done((f32[4,1408]{1,0:T(4,128)S(1)}, f32[4,1408]{1,0:T(4,128)S(1)}, u32[]{:S(2)}, u32[]{:S(2)}) %collective-permute-start.3) | collective-permute-done | bytes 22560 | tf_op jit(solution)/shard_map/ppermute | solution.py:480
  41.5 0.3 shard_map.116
  41.8 13.2 %all_to_all.11.state_ref = bf16[32,4,1280]{2,1,0:T(4,128)(2,1)S(1)} all-to-all(bf16[32,4,1280]{2,1,0:T(4,128)(2,1)S(1)} %shard_map.116), channel_id=1, replica_groups=mesh['za'=4,'zb'=2,'y'=4,'x'=4,'tp'=4] {'zb','y','x'}, dimensions={0} | all-to-all | bytes 655360 | tf_op jit(solution)/shard_map/all_to_all | solution.py:494
  55.0 0.6 shard_map.117
  55.6 18.4 %all-gather.1.squares_ref = f32[4,1,256]{2,1,0:T(1,128)S(1)} all-gather(f32[1,1,256]{2,1,0:T(1,128)S(1)} %bitcast.7), channel_id=2, replica_groups=mesh['za'=4,'zb'=2,'y'=4,'x'=4,'tp'=4] {'tp'}, dimensions={0}, use_global_device_ids=true | all-gather | bytes 5120 | tf_op jit(solution)/shard_map/all_gather | solution.py:500
  73.9 1.0 %shard_map.118 = bf16[256,1280]{1,0:T(8,128)(2,1)} custom-call(f32[4,1,256]{2,1,0:T(1,128)S(1)} %all-gather.1.squares_ref, f32[256,1280]{1,0:T(8,128)S(1)} %get-tuple-element.85.gated_ref, f32[10,128]{1,0:T(8,128)S(1)} %get-tuple-element.86.gain_ref), custom_call_target="tpu_custom_call" | custom-call | flops 1000000 | bytes 1000000 | tf_op jit(solution)/shard_map/pallas_call | solution.py:27
  (2 shorter events, 0.0 us)
Async XLA Ops:
  0.8 5.7 %collective-permute-start = (bf16[8,256]{1,0:T(8,128)(2,1)S(1)}, bf16[8,256]{1,0:T(8,128)(2,1)S(1)}, u32[]{:S(2)}, u32[]{:S(2)}) collective-permute-start(bf16[8,256]{1,0:T(8,128)(2,1)S(1)} %get-tuple-element.50.refs_10_), channel_id=1, source_target_pairs={{0,4},{4,8},{8,12},{12,16},{16,20},{20,24},{24,28},{28,32},{32,36}... | collective-permute-start | bytes 12296 | tf_op jit(solution)/shard_map/ppermute | solution.py:417
  6.9 19.9 %copy-start = (bf16[256,1280]{1,0:T(8,128)(2,1)S(1)}, bf16[256,1280]{1,0:T(8,128)(2,1)}, u32[]{:S(2)}) copy-start(bf16[256,1280]{1,0:T(8,128)(2,1)} %refs_10_.5) | copy-start | bytes 1966084
  26.1 14.5 %collective-permute-start.2 = (f32[4,1408]{1,0:T(4,128)S(1)}, f32[4,1408]{1,0:T(4,128)S(1)}, u32[]{:S(2)}, u32[]{:S(2)}) collective-permute-start(f32[4,1408]{1,0:T(4,128)S(1)} %get-tuple-element.68), channel_id=1, source_target_pairs={{128,256},{256,384},{129,257},{257,385},{130,258},{258,386},{131,2... | collective-permute-start | bytes 67592 | tf_op jit(solution)/shard_map/ppermute | solution.py:480
  28.6 12.0 %collective-permute-start.1 = (f32[4,1408]{1,0:T(4,128)S(1)}, f32[4,1408]{1,0:T(4,128)S(1)}, u32[]{:S(2)}, u32[]{:S(2)}) collective-permute-start(f32[4,1408]{1,0:T(4,128)S(1)} %get-tuple-element.67), channel_id=1, source_target_pairs={{0,128},{1,129},{2,130},{3,131},{4,132},{5,133},{6,134},{7,135},{8... | collective-permute-start | bytes 67592 | tf_op jit(solution)/shard_map/ppermute | solution.py:480
  37.2 4.3 %collective-permute-start.3 = (f32[4,1408]{1,0:T(4,128)S(1)}, f32[4,1408]{1,0:T(4,128)S(1)}, u32[]{:S(2)}, u32[]{:S(2)}) collective-permute-start(f32[4,1408]{1,0:T(4,128)S(1)} %get-tuple-element.74), channel_id=1, source_target_pairs={{0,256},{128,384},{1,257},{129,385},{2,258},{130,386},{3,259},{131... | collective-permute-start | bytes 67592 | tf_op jit(solution)/shard_map/ppermute | solution.py:480

commit v12 on v11

--- a/solution.py
+++ b/solution.py
@@ -51,9 +51,7 @@
     return spread
 
 
-def tails_kernel(b_ref, c_ref, *refs):
-    count = (len(refs) - 2) // 2
-    sources, tails_ref, targets, sems = refs[:count], refs[count], refs[count + 1 : -1], refs[-1]
+def tails_kernel(b_ref, c_ref, tails_ref, sems):
     tokens, state = b_ref.shape
     copies = [
         pltpu.make_async_copy(
@@ -61,8 +59,6 @@
         )
         for k, r in enumerate((b_ref, c_ref))
     ]
-    for k, (source, target) in enumerate(zip(sources, targets)):
-        copies.append(pltpu.make_async_copy(source, target, sems.at[k + 2]))
     for copy in copies:
         copy.start()
     for copy in copies:
@@ -128,20 +124,23 @@
 
 
 def prepare_kernel(*refs):
-    count = 6
-    sources, (docs_ref, raw_ref, bias_ref, rate_ref, _) = refs[:count], refs[count : count + 5]
-    targets = refs[count + 5 : 2 * count + 5]
+    count, held = 10, 4
+    sources, kept = refs[:count], refs[count + 1 : 2 * count + 1 - held]
     (
         weighted_ref, cum_rows_ref, step_rows_ref, columns_ref, factor_ref, start_ref, b_conv_ref,
-        stack_ref, padded_ref, sems,
-    ) = refs[2 * count + 5 :]
-    x_ref, b_ref, _, taps_ref, taps_bias_ref, _ = targets
+        stack_ref, padded_ref, sems, docs_ref, raw_ref, bias_ref, rate_ref,
+    ) = refs[2 * count + 1 - held :]
+    b_ref, taps_ref, taps_bias_ref, x_ref, _, _ = kept
     copies = [
         pltpu.make_async_copy(source, target, sems.at[k])
-        for k, (source, target) in enumerate(zip(sources, targets))
+        for k, (source, target) in enumerate(
+            zip(sources, (docs_ref, raw_ref, bias_ref, rate_ref, *kept))
+        )
     ]
     for copy in copies:
         copy.start()
+    for copy in copies[:4]:
+        copy.wait()
     heads, tokens = raw_ref.shape
     state = b_ref.shape[1]
     width = x_ref.shape[1] // heads
@@ -180,7 +179,14 @@
     columns = stack_ref[...].T
     columns_ref[...] = columns
     factor_ref[...] = jnp.where(end_start < 0, jnp.exp(columns[tokens - 1 : tokens, :]), 0.0)
-    for copy in copies:
+    for copy in copies[4:7]:
+        copy.wait()
+    side = slice(0, state)
+    padded_ref[0:8, :] = jnp.zeros((8, state), jnp.float32)
+    padded_ref[8:, :] = b_ref[...].astype(jnp.float32)
+    b_conv = convolve(padded_ref, taps_ref[:, side], taps_bias_ref[:, side], relative, chosen)
+    b_conv_ref[...] = b_conv.astype(jnp.float32)
+    for copy in copies[7:]:
         copy.wait()
     weights = columns.astype(jnp.bfloat16)
     for j in range(0, x_ref.shape[1], 256):
@@ -190,11 +196,6 @@
             preferred_element_type=jnp.float32,
         )
         weighted_ref[:, tile] = (x_ref[:, tile].astype(jnp.float32) * spread).astype(jnp.bfloat16)
-    side = slice(0, state)
-    padded_ref[0:8, :] = jnp.zeros((8, state), jnp.float32)
-    padded_ref[8:, :] = b_ref[...].astype(jnp.float32)
-    b_conv = convolve(padded_ref, taps_ref[:, side], taps_bias_ref[:, side], relative, chosen)
-    b_conv_ref[...] = b_conv.astype(jnp.float32)
 
 
 def first_rows(source_ref, halo, weight, bias, start_ref, padded_ref):
@@ -257,11 +258,12 @@
 
 
 def states_in_kernel(heads, *refs):
-    *near_refs, far_ref, before_ref, wide_ref, state_ref, near_ref = refs
+    *near_refs, far_a_ref, far_b_ref, before_ref, wide_ref, state_ref, near_ref = refs
     members, _, features = before_ref.shape
     near_ref[...] = sum(ref[...] for ref in near_refs)
     factor = wide_factor(near_ref, features, features // heads)
-    entering = factor * far_ref[:, 0:features] + near_ref[:, 0:features]
+    far = far_a_ref[:, 0:features] + far_b_ref[:, 0:features]
+    entering = factor * far + near_ref[:, 0:features]
     for m in range(members):
         state_ref[m] = (wide_ref[m : m + 1, :] * entering + before_ref[m]).astype(jnp.bfloat16)
 
@@ -407,35 +409,34 @@
     ahead = lambda n, k: [(i, i + k) for i in range(n - k)]
 
     bf16 = jnp.bfloat16
-    small = [doc_lengths[None, :], step_raw.T, step_bias[None, :], decay_rate[None, :]]
-    tails, *small = call(
-        tails_kernel,
-        [out((8, 2 * state), bf16)] + [out(o.shape, o.dtype) for o in small],
-        b_source, c_source, *small,
-        hbm=2 + len(small), scratch=[pltpu.SemaphoreType.DMA((2 + len(small),))],
+    tails = call(
+        tails_kernel, out((8, 2 * state), bf16), b_source, c_source,
+        hbm=2, scratch=[pltpu.SemaphoreType.DMA((2,))],
     )
     halo = lax.ppermute(tails, SEQ, ahead(shards, 1))
     operands = [
-        inputs, b_source, c_source, conv_weight, conv_bias[None, :],
+        doc_lengths[None, :], step_raw.T, step_bias[None, :], decay_rate[None, :], b_source,
+        conv_weight, conv_bias[None, :], inputs, c_source,
         norm_gain.reshape(features // LANES, LANES),
     ]
     results = call(
         prepare_kernel,
-        [out(o.shape, o.dtype) for o in operands]
+        [out(o.shape, o.dtype) for o in operands[4:]]
         + [
             out((tokens, features), bf16), out((heads, tokens)), out((heads, tokens)),
             out((tokens, LANES)), out((1, LANES)), out((tokens, LANES), jnp.int32),
             out((tokens, state)),
         ],
-        *operands, *small, tails,
+        *operands, tails,
         hbm=len(operands),
         scratch=[
             pltpu.VMEM((LANES, tokens), jnp.float32),
             pltpu.VMEM((tokens + 8, state), jnp.float32),
             pltpu.SemaphoreType.DMA((len(operands),)),
+            *(pltpu.VMEM(o.shape, o.dtype) for o in operands[:4]),
         ],
     )
-    x, b, c, taps, taps_bias, gain = results[0:6]
+    b, taps, taps_bias, x, c, gain = results[0:6]
     weighted, cum_rows, step_rows, columns, factor, start, b_early = results[6:]
     pieces, b_conv = call(
         states_kernel,
@@ -482,13 +483,14 @@
     total_a, *diagonal = diagonal_terms(0, total_a)
     near_a = send(total_a, (0, 1))
     total_b, *diagonal = diagonal_terms(1, total_b, *diagonal)
-    far = send(total_b, (0, 2), (1, 3))
+    far_a = send(total_b, (0, 2))
     near_b = send(total_c, (1, 2), (2, 3))
+    far_b = send(total_b, (1, 3))
     wide, c_conv, diagonal, scale = diagonal_terms(2, None, *diagonal)
     states_in = call(
         functools.partial(states_in_kernel, heads),
         out((members, rows, features), bf16),
-        near_a, near_b, far, before, wide,
+        near_a, near_b, far_a, far_b, before, wide,
         scratch=[pltpu.VMEM(pair.shape, jnp.float32)],
     )
     states_in = lax.all_to_all(states_in, GROUP, 0, 0)

time: 75.3 us -> 76.7 us (1.019)
  starting transfers between devices: 16.5 us -> 17.8 us
    ppermute x3 -> x4, starting transfers between devices: 12.6 us -> 13.9 us  [send(): return lax.ppermute(total, OUTER, pairs)]
  transfers between devices with their start and end apart: 4 -> 5, of which waited for: 1 -> 1; matrix products, arithmetic and copies ran while one was open for 0% -> 0% of each run, Pallas kernels for 5% -> 3%
where the time goes in v12:
time: 76.7 us; the launch traced here: 76.4 us
  blocking collectives  50.4 us (66%)
  starting transfers between devices  17.8 us (23%)
  Pallas kernels  7.19 us (9%)
  waiting for transfers between devices  0.88 us (1%)
    all_to_all x1, blocking collectives, body(): pieces = lax.all_to_all(pieces, GROUP, 0, 0)  19.2 us
    all_gather x1, blocking collectives, body(): squares = lax.all_gather(squares, 'tp')  17.9 us
    ppermute x4, starting transfers between devices, send(): return lax.ppermute(total, OUTER, pairs)  13.9 us
    all_to_all x1, blocking collectives, body(): states_in = lax.all_to_all(states_in, GROUP, 0, 0)  13.3 us
    pallas_call x10, Pallas kernels, call(): pl.pallas_call(kernel, out_shape=list(outs) if multiple else outs, in_spe...  7.19 us
    ppermute x1, starting transfers between devices, body(): halo = lax.ppermute(tails, SEQ, ahead(shards, 1))  3.93 us
  transfers between devices with their start and end apart: 5, of which 1 were waited for; matrix products, arithmetic and copies ran while one was open for 0% of the time, Pallas kernels for 3%

profile of v12, /device:TPU:1, one launch (start us, length us, event | category | flops | bytes accessed | tf_op | source)
XLA Modules:
  0.0 76.4 jit_solution(5407649929363882675)
XLA Ops:
  0.0 0.7 shard_map.109.refs_10_
  0.7 3.9 %collective-permute-start = (bf16[8,256]{1,0:T(8,128)(2,1)S(1)}, bf16[8,256]{1,0:T(8,128)(2,1)S(1)}, u32[]{:S(2)}, u32[]{:S(2)}) collective-permute-start(bf16[8,256]{1,0:T(8,128)(2,1)S(1)} %shard_map.109.refs_10_), channel_id=1, source_target_pairs={{0,4},{4,8},{8,12},{12,16},{16,20},{20,24},{24,28},{28,32},{32,36}... | collective-permute-start | bytes 12296 | tf_op jit(solution)/shard_map/ppermute | solution.py:416
  4.7 2.0 %shard_map.110 = (bf16[256,128]{1,0:T(8,128)(2,1)S(1)}, f32[4,256]{1,0:T(4,128)S(1)}, f32[1,256]{1,0:T(1,128)S(1)}, bf16[256,1280]{1,0:T(8,128)(2,1)S(1)}, bf16[...) custom-call(s32[1,8]{1,0:T(1,128)} %bitcast.11, ...), custom_call_target="tpu_custom_call" | custom-call | flops 1000000 | bytes 1000000 | tf_op jit(solution)/shard_map/pallas_call | solution.py:27
  6.7 0.0 collective-permute-done.halo_ref.refs_1_
  6.7 0.3 shard_map.111
  7.0 0.0 copy-start
  7.0 19.2 %all_to_all.10.pieces_ref = f32[32,4,1408]{2,1,0:T(4,128)S(1)} all-to-all(f32[32,4,1408]{2,1,0:T(4,128)S(1)} %get-tuple-element.54), channel_id=1, replica_groups=mesh['za'=4,'zb'=2,'y'=4,'x'=4,'tp'=4] {'zb','y','x'}, dimensions={0} | all-to-all | bytes 1441792 | tf_op jit(solution)/shard_map/all_to_all | solution.py:447
  26.2 0.4 shard_map.112
  26.6 0.0 copy-done
  26.6 1.8 %shard_map.113 = (f32[4,1408]{1,0:T(4,128)S(1)}, f32[32,1280]{1,0:T(8,128)S(1)}, bf16[256,128]{1,0:T(8,128)(2,1)S(1)}, f32[256,1280]{1,0:T(8,128)S(1)}, f32[256,1280]{1,0:T(8,128)S(1)}) custom-call(bf16[256,128]{1,0:T(8,128)(2,1)S(1)} %get-tuple-element.41.refs_0_, ...), custom_call_target="tpu_custom_call", output_to_operand_aliasing={{0}: (12, {})} | custom-call | flops 20000000000 | bytes 1000000 | tf_op jit(solution)/shard_map/pallas_call | solution.py:27
  28.5 0.7 collective-permute-start.4
  29.1 7.0 %collective-permute-start.3 = (f32[4,1408]{1,0:T(4,128)S(1)}, f32[4,1408]{1,0:T(4,128)S(1)}, u32[]{:S(2)}, u32[]{:S(2)}) collective-permute-start(f32[4,1408]{1,0:T(4,128)S(1)} %get-tuple-element.64), channel_id=1, source_target_pairs={{0,256},{1,257},{2,258},{3,259},{4,260},{5,261},{6,262},{7,263},{8... | collective-permute-start | bytes 67592 | tf_op jit(solution)/shard_map/ppermute | solution.py:481
  36.1 0.7 collective-permute-start.2
  36.8 5.5 %collective-permute-start.1 = (f32[4,1408]{1,0:T(4,128)S(1)}, f32[4,1408]{1,0:T(4,128)S(1)}, u32[]{:S(2)}, u32[]{:S(2)}) collective-permute-start(f32[4,1408]{1,0:T(4,128)S(1)} %get-tuple-element.57), channel_id=1, source_target_pairs={{0,128},{1,129},{2,130},{3,131},{4,132},{5,133},{6,134},{7,135},{8... | collective-permute-start | bytes 67592 | tf_op jit(solution)/shard_map/ppermute | solution.py:481
  42.4 0.0 collective-permute-done.2.refs_1_
  42.4 0.9 %collective-permute-done.1.refs_0_ = f32[4,1408]{1,0:T(4,128)S(1)} collective-permute-done((f32[4,1408]{1,0:T(4,128)S(1)}, f32[4,1408]{1,0:T(4,128)S(1)}, u32[]{:S(2)}, u32[]{:S(2)}) %collective-permute-start.1) | collective-permute-done | bytes 22560 | tf_op jit(solution)/shard_map/ppermute | solution.py:481
  43.3 0.0 collective-permute-done.4.refs_3_
  43.3 0.0 collective-permute-done.3.refs_2_
  43.3 0.3 shard_map.116
  43.6 13.3 %all_to_all.11.state_ref = bf16[32,4,1280]{2,1,0:T(4,128)(2,1)S(1)} all-to-all(bf16[32,4,1280]{2,1,0:T(4,128)(2,1)S(1)} %shard_map.116), channel_id=1, replica_groups=mesh['za'=4,'zb'=2,'y'=4,'x'=4,'tp'=4] {'zb','y','x'}, dimensions={0} | all-to-all | bytes 655360 | tf_op jit(solution)/shard_map/all_to_all | solution.py:496
  56.9 0.6 shard_map.117
  57.5 17.9 %all-gather.1.squares_ref = f32[4,1,256]{2,1,0:T(1,128)S(1)} all-gather(f32[1,1,256]{2,1,0:T(1,128)S(1)} %bitcast.7), channel_id=2, replica_groups=mesh['za'=4,'zb'=2,'y'=4,'x'=4,'tp'=4] {'tp'}, dimensions={0}, use_global_device_ids=true | all-gather | bytes 5120 | tf_op jit(solution)/shard_map/all_gather | solution.py:502
  75.4 1.0 %shard_map.118 = bf16[256,1280]{1,0:T(8,128)(2,1)} custom-call(f32[4,1,256]{2,1,0:T(1,128)S(1)} %all-gather.1.squares_ref, f32[256,1280]{1,0:T(8,128)S(1)} %get-tuple-element.75.gated_ref, f32[10,128]{1,0:T(8,128)S(1)} %get-tuple-element.76.gain_ref), custom_call_target="tpu_custom_call" | custom-call | flops 1000000 | bytes 1000000 | tf_op jit(solution)/shard_map/pallas_call | solution.py:27
  (2 shorter events, 0.0 us)
Async XLA Ops:
  0.7 5.9 %collective-permute-start = (bf16[8,256]{1,0:T(8,128)(2,1)S(1)}, bf16[8,256]{1,0:T(8,128)(2,1)S(1)}, u32[]{:S(2)}, u32[]{:S(2)}) collective-permute-start(bf16[8,256]{1,0:T(8,128)(2,1)S(1)} %shard_map.109.refs_10_), channel_id=1, source_target_pairs={{0,4},{4,8},{8,12},{12,16},{16,20},{20,24},{24,28},{28,32},{32,36}... | collective-permute-start | bytes 12296 | tf_op jit(solution)/shard_map/ppermute | solution.py:416
  7.0 19.6 %copy-start = (bf16[256,1280]{1,0:T(8,128)(2,1)S(1)}, bf16[256,1280]{1,0:T(8,128)(2,1)}, u32[]{:S(2)}) copy-start(bf16[256,1280]{1,0:T(8,128)(2,1)} %refs_10_.5) | copy-start | bytes 1966084
  28.5 14.8 %collective-permute-start.4 = (f32[4,1408]{1,0:T(4,128)S(1)}, f32[4,1408]{1,0:T(4,128)S(1)}, u32[]{:S(2)}, u32[]{:S(2)}) collective-permute-start(f32[4,1408]{1,0:T(4,128)S(1)} %get-tuple-element.64), channel_id=1, source_target_pairs={{128,384},{129,385},{130,386},{131,387},{132,388},{133,389},{134,3... | collective-permute-start | bytes 67592 | tf_op jit(solution)/shard_map/ppermute | solution.py:481
  29.1 14.1 %collective-permute-start.3 = (f32[4,1408]{1,0:T(4,128)S(1)}, f32[4,1408]{1,0:T(4,128)S(1)}, u32[]{:S(2)}, u32[]{:S(2)}) collective-permute-start(f32[4,1408]{1,0:T(4,128)S(1)} %get-tuple-element.64), channel_id=1, source_target_pairs={{0,256},{1,257},{2,258},{3,259},{4,260},{5,261},{6,262},{7,263},{8... | collective-permute-start | bytes 67592 | tf_op jit(solution)/shard_map/ppermute | solution.py:481
  36.1 6.2 %collective-permute-start.2 = (f32[4,1408]{1,0:T(4,128)S(1)}, f32[4,1408]{1,0:T(4,128)S(1)}, u32[]{:S(2)}, u32[]{:S(2)}) collective-permute-start(f32[4,1408]{1,0:T(4,128)S(1)} %get-tuple-element.58), channel_id=1, source_target_pairs={{128,256},{256,384},{129,257},{257,385},{130,258},{258,386},{131,2... | collective-permute-start | bytes 67592 | tf_op jit(solution)/shard_map/ppermute | solution.py:481
  36.8 6.4 %collective-permute-start.1 = (f32[4,1408]{1,0:T(4,128)S(1)}, f32[4,1408]{1,0:T(4,128)S(1)}, u32[]{:S(2)}, u32[]{:S(2)}) collective-permute-start(f32[4,1408]{1,0:T(4,128)S(1)} %get-tuple-element.57), channel_id=1, source_target_pairs={{0,128},{1,129},{2,130},{3,131},{4,132},{5,133},{6,134},{7,135},{8... | collective-permute-start | bytes 67592 | tf_op jit(solution)/shard_map/ppermute | solution.py:481

commit v13 on v12

--- a/solution.py
+++ b/solution.py
@@ -124,13 +124,14 @@
 
 
 def prepare_kernel(*refs):
-    count, held = 10, 4
-    sources, kept = refs[:count], refs[count + 1 : 2 * count + 1 - held]
+    count, held = 9, 4
+    sources, x_ref = refs[:count], refs[count]
+    kept = refs[count + 2 : 2 * count + 2 - held]
     (
         weighted_ref, cum_rows_ref, step_rows_ref, columns_ref, factor_ref, start_ref, b_conv_ref,
         stack_ref, padded_ref, sems, docs_ref, raw_ref, bias_ref, rate_ref,
-    ) = refs[2 * count + 1 - held :]
-    b_ref, taps_ref, taps_bias_ref, x_ref, _, _ = kept
+    ) = refs[2 * count + 2 - held :]
+    b_ref, taps_ref, taps_bias_ref, _, _ = kept
     copies = [
         pltpu.make_async_copy(source, target, sems.at[k])
         for k, (source, target) in enumerate(
@@ -179,15 +180,13 @@
     columns = stack_ref[...].T
     columns_ref[...] = columns
     factor_ref[...] = jnp.where(end_start < 0, jnp.exp(columns[tokens - 1 : tokens, :]), 0.0)
-    for copy in copies[4:7]:
+    for copy in copies[4:]:
         copy.wait()
     side = slice(0, state)
     padded_ref[0:8, :] = jnp.zeros((8, state), jnp.float32)
     padded_ref[8:, :] = b_ref[...].astype(jnp.float32)
     b_conv = convolve(padded_ref, taps_ref[:, side], taps_bias_ref[:, side], relative, chosen)
     b_conv_ref[...] = b_conv.astype(jnp.float32)
-    for copy in copies[7:]:
-        copy.wait()
     weights = columns.astype(jnp.bfloat16)
     for j in range(0, x_ref.shape[1], 256):
         tile = slice(j, j + 256)
@@ -258,12 +257,11 @@
 
 
 def states_in_kernel(heads, *refs):
-    *near_refs, far_a_ref, far_b_ref, before_ref, wide_ref, state_ref, near_ref = refs
+    *near_refs, far_ref, before_ref, wide_ref, state_ref, near_ref = refs
     members, _, features = before_ref.shape
     near_ref[...] = sum(ref[...] for ref in near_refs)
     factor = wide_factor(near_ref, features, features // heads)
-    far = far_a_ref[:, 0:features] + far_b_ref[:, 0:features]
-    entering = factor * far + near_ref[:, 0:features]
+    entering = factor * far_ref[:, 0:features] + near_ref[:, 0:features]
     for m in range(members):
         state_ref[m] = (wide_ref[m : m + 1, :] * entering + before_ref[m]).astype(jnp.bfloat16)
 
@@ -411,13 +409,12 @@
     bf16 = jnp.bfloat16
     tails = call(
         tails_kernel, out((8, 2 * state), bf16), b_source, c_source,
-        hbm=2, scratch=[pltpu.SemaphoreType.DMA((2,))],
+        hbm=2, scratch=[pltpu.SemaphoreType.DMA((2,))], flops=20_000_000_000,
     )
     halo = lax.ppermute(tails, SEQ, ahead(shards, 1))
     operands = [
         doc_lengths[None, :], step_raw.T, step_bias[None, :], decay_rate[None, :], b_source,
-        conv_weight, conv_bias[None, :], inputs, c_source,
-        norm_gain.reshape(features // LANES, LANES),
+        conv_weight, conv_bias[None, :], c_source, norm_gain.reshape(features // LANES, LANES),
     ]
     results = call(
         prepare_kernel,
@@ -427,7 +424,7 @@
             out((tokens, LANES)), out((1, LANES)), out((tokens, LANES), jnp.int32),
             out((tokens, state)),
         ],
-        *operands, tails,
+        *operands, inputs, tails,
         hbm=len(operands),
         scratch=[
             pltpu.VMEM((LANES, tokens), jnp.float32),
@@ -436,8 +433,8 @@
             *(pltpu.VMEM(o.shape, o.dtype) for o in operands[:4]),
         ],
     )
-    b, taps, taps_bias, x, c, gain = results[0:6]
-    weighted, cum_rows, step_rows, columns, factor, start, b_early = results[6:]
+    b, taps, taps_bias, c, gain = results[0:5]
+    weighted, cum_rows, step_rows, columns, factor, start, b_early = results[5:]
     pieces, b_conv = call(
         states_kernel,
         [out((members, rows, features + LANES)), out((tokens, state), bf16)],
@@ -458,7 +455,7 @@
 
     def diagonal_terms(turn, token, *before):
         sources = [
-            c, halo, taps, taps_bias, start, b_conv, columns, cum_rows, step_rows, x, gate_input,
+            c, halo, taps, taps_bias, start, b_conv, columns, cum_rows, step_rows, inputs, gate_input,
             factors,
         ]
         token = [] if token is None else [token]
@@ -483,14 +480,13 @@
     total_a, *diagonal = diagonal_terms(0, total_a)
     near_a = send(total_a, (0, 1))
     total_b, *diagonal = diagonal_terms(1, total_b, *diagonal)
-    far_a = send(total_b, (0, 2))
+    far = send(total_b, (0, 2), (1, 3))
     near_b = send(total_c, (1, 2), (2, 3))
-    far_b = send(total_b, (1, 3))
     wide, c_conv, diagonal, scale = diagonal_terms(2, None, *diagonal)
     states_in = call(
         functools.partial(states_in_kernel, heads),
         out((members, rows, features), bf16),
-        near_a, near_b, far_a, far_b, before, wide,
+        near_a, near_b, far, before, wide,
         scratch=[pltpu.VMEM(pair.shape, jnp.float32)],
     )
     states_in = lax.all_to_all(states_in, GROUP, 0, 0)

time: 76.7 us -> 75.4 us (0.983)
  starting transfers between devices: 17.8 us -> 16.5 us
    ppermute x4 -> x3, starting transfers between devices: 13.9 us -> 12.6 us  [send(): return lax.ppermute(total, OUTER, pairs)]
  transfers between devices with their start and end apart: 5 -> 4, of which waited for: 1 -> 1; matrix products, arithmetic and copies ran while one was open for 0% -> 0% of each run, Pallas kernels for 3% -> 5%
where the time goes in v13:
time: 75.4 us; the launch traced here: 75.1 us
  blocking collectives  50.4 us (67%)
  starting transfers between devices  16.5 us (22%)
  Pallas kernels  7.13 us (9%)
  waiting for transfers between devices  0.87 us (1%)
    all_to_all x1, blocking collectives, body(): pieces = lax.all_to_all(pieces, GROUP, 0, 0)  19.1 us
    all_gather x1, blocking collectives, body(): squares = lax.all_gather(squares, 'tp')  18.4 us
    all_to_all x1, blocking collectives, body(): states_in = lax.all_to_all(states_in, GROUP, 0, 0)  13 us
    ppermute x3, starting transfers between devices, send(): return lax.ppermute(total, OUTER, pairs)  12.6 us
    pallas_call x10, Pallas kernels, call(): pl.pallas_call(kernel, out_shape=list(outs) if multiple else outs, in_spe...  7.13 us
    ppermute x1, starting transfers between devices, body(): halo = lax.ppermute(tails, SEQ, ahead(shards, 1))  3.93 us
  transfers between devices with their start and end apart: 4, of which 1 were waited for; matrix products, arithmetic and copies ran while one was open for 0% of the time, Pallas kernels for 5%

profile of v13, /device:TPU:1, one launch (start us, length us, event | category | flops | bytes accessed | tf_op | source)
XLA Modules:
  0.0 75.1 jit_solution(1706202275706797828)
XLA Ops:
  0.0 0.0 copy-start
  0.0 0.8 %shard_map.109.refs_10_ = bf16[8,256]{1,0:T(8,128)(2,1)S(1)} custom-call(bf16[256,128]{1,0:T(8,128)(2,1)} %refs_4_.1, bf16[256,128]{1,0:T(8,128)(2,1)} %refs_7_.1), custom_call_target="tpu_custom_call" | custom-call | flops 20000000000 | bytes 1000000 | tf_op jit(solution)/shard_map/pallas_call | solution.py:27
  0.8 3.9 %collective-permute-start = (bf16[8,256]{1,0:T(8,128)(2,1)S(1)}, bf16[8,256]{1,0:T(8,128)(2,1)S(1)}, u32[]{:S(2)}, u32[]{:S(2)}) collective-permute-start(bf16[8,256]{1,0:T(8,128)(2,1)S(1)} %shard_map.109.refs_10_), channel_id=1, source_target_pairs={{0,4},{4,8},{8,12},{12,16},{16,20},{20,24},{24,28},{28,32},{32,36}... | collective-permute-start | bytes 12296 | tf_op jit(solution)/shard_map/ppermute | solution.py:414
  4.7 0.0 copy-done
  4.7 1.9 %shard_map.110 = (bf16[256,128]{1,0:T(8,128)(2,1)S(1)}, f32[4,256]{1,0:T(4,128)S(1)}, f32[1,256]{1,0:T(1,128)S(1)}, bf16[256,128]{1,0:T(8,128)(2,1)S(1)}, f32[10...) custom-call(s32[1,8]{1,0:T(1,128)} %bitcast.11, ...), custom_call_target="tpu_custom_call" | custom-call | flops 1000000 | bytes 1000000 | tf_op jit(solution)/shard_map/pallas_call | solution.py:27
  6.6 0.0 collective-permute-done.halo_ref.refs_1_
  6.6 0.3 shard_map.111
  7.0 0.0 copy-start.1
  7.0 19.1 %all_to_all.10.pieces_ref = f32[32,4,1408]{2,1,0:T(4,128)S(1)} all-to-all(f32[32,4,1408]{2,1,0:T(4,128)S(1)} %get-tuple-element.52), channel_id=1, replica_groups=mesh['za'=4,'zb'=2,'y'=4,'x'=4,'tp'=4] {'zb','y','x'}, dimensions={0} | all-to-all | bytes 1441792 | tf_op jit(solution)/shard_map/all_to_all | solution.py:444
  26.1 0.4 shard_map.112
  26.5 0.7 collective-permute-start.2
  27.1 0.0 copy-done.1
  27.2 1.8 %shard_map.113 = (f32[4,1408]{1,0:T(4,128)S(1)}, f32[32,1280]{1,0:T(8,128)S(1)}, bf16[256,128]{1,0:T(8,128)(2,1)S(1)}, f32[256,1280]{1,0:T(8,128)S(1)}, f32[256,1280]{1,0:T(8,128)S(1)}) custom-call(bf16[256,128]{1,0:T(8,128)(2,1)S(1)} %get-tuple-element.40.refs_0_, ...), custom_call_target="tpu_custom_call", output_to_operand_aliasing={{0}: (12, {})} | custom-call | flops 20000000000 | bytes 1000000 | tf_op jit(solution)/shard_map/pallas_call | solution.py:27
  29.0 8.6 %collective-permute-start.1 = (f32[4,1408]{1,0:T(4,128)S(1)}, f32[4,1408]{1,0:T(4,128)S(1)}, u32[]{:S(2)}, u32[]{:S(2)}) collective-permute-start(f32[4,1408]{1,0:T(4,128)S(1)} %get-tuple-element.55), channel_id=1, source_target_pairs={{0,128},{1,129},{2,130},{3,131},{4,132},{5,133},{6,134},{7,135},{8... | collective-permute-start | bytes 67592 | tf_op jit(solution)/shard_map/ppermute | solution.py:478
  37.6 3.4 %collective-permute-start.3 = (f32[4,1408]{1,0:T(4,128)S(1)}, f32[4,1408]{1,0:T(4,128)S(1)}, u32[]{:S(2)}, u32[]{:S(2)}) collective-permute-start(f32[4,1408]{1,0:T(4,128)S(1)} %get-tuple-element.62), channel_id=1, source_target_pairs={{0,256},{128,384},{1,257},{129,385},{2,258},{130,386},{3,259},{131... | collective-permute-start | bytes 67592 | tf_op jit(solution)/shard_map/ppermute | solution.py:478
  41.0 0.0 collective-permute-done.2.refs_1_
  41.0 0.0 collective-permute-done.1.refs_0_
  41.0 0.9 %collective-permute-done.3.refs_2_ = f32[4,1408]{1,0:T(4,128)S(1)} collective-permute-done((f32[4,1408]{1,0:T(4,128)S(1)}, f32[4,1408]{1,0:T(4,128)S(1)}, u32[]{:S(2)}, u32[]{:S(2)}) %collective-permute-start.3) | collective-permute-done | bytes 22560 | tf_op jit(solution)/shard_map/ppermute | solution.py:478
  41.9 0.3 shard_map.116
  42.2 13.0 %all_to_all.11.state_ref = bf16[32,4,1280]{2,1,0:T(4,128)(2,1)S(1)} all-to-all(bf16[32,4,1280]{2,1,0:T(4,128)(2,1)S(1)} %shard_map.116), channel_id=1, replica_groups=mesh['za'=4,'zb'=2,'y'=4,'x'=4,'tp'=4] {'zb','y','x'}, dimensions={0} | all-to-all | bytes 655360 | tf_op jit(solution)/shard_map/all_to_all | solution.py:492
  55.1 0.6 shard_map.117
  55.7 18.4 %all-gather.1.squares_ref = f32[4,1,256]{2,1,0:T(1,128)S(1)} all-gather(f32[1,1,256]{2,1,0:T(1,128)S(1)} %bitcast.7), channel_id=2, replica_groups=mesh['za'=4,'zb'=2,'y'=4,'x'=4,'tp'=4] {'tp'}, dimensions={0}, use_global_device_ids=true | all-gather | bytes 5120 | tf_op jit(solution)/shard_map/all_gather | solution.py:498
  74.0 1.0 %shard_map.118 = bf16[256,1280]{1,0:T(8,128)(2,1)} custom-call(f32[4,1,256]{2,1,0:T(1,128)S(1)} %all-gather.1.squares_ref, f32[256,1280]{1,0:T(8,128)S(1)} %get-tuple-element.73.gated_ref, f32[10,128]{1,0:T(8,128)S(1)} %get-tuple-element.74.gain_ref), custom_call_target="tpu_custom_call" | custom-call | flops 1000000 | bytes 1000000 | tf_op jit(solution)/shard_map/pallas_call | solution.py:27
  (2 shorter events, 0.0 us)
Async XLA Ops:
  0.0 4.7 %copy-start = (bf16[256,1280]{1,0:T(8,128)(2,1)S(1)}, bf16[256,1280]{1,0:T(8,128)(2,1)}, u32[]{:S(2)}) copy-start(bf16[256,1280]{1,0:T(8,128)(2,1)} %refs_9_.7) | copy-start | bytes 1966084
  0.8 5.8 %collective-permute-start = (bf16[8,256]{1,0:T(8,128)(2,1)S(1)}, bf16[8,256]{1,0:T(8,128)(2,1)S(1)}, u32[]{:S(2)}, u32[]{:S(2)}) collective-permute-start(bf16[8,256]{1,0:T(8,128)(2,1)S(1)} %shard_map.109.refs_10_), channel_id=1, source_target_pairs={{0,4},{4,8},{8,12},{12,16},{16,20},{20,24},{24,28},{28,32},{32,36}... | collective-permute-start | bytes 12296 | tf_op jit(solution)/shard_map/ppermute | solution.py:414
  7.0 20.2 %copy-start.1 = (bf16[256,1280]{1,0:T(8,128)(2,1)S(1)}, bf16[256,1280]{1,0:T(8,128)(2,1)}, u32[]{:S(2)}) copy-start(bf16[256,1280]{1,0:T(8,128)(2,1)} %refs_10_.5) | copy-start | bytes 1966084
  26.5 14.5 %collective-permute-start.2 = (f32[4,1408]{1,0:T(4,128)S(1)}, f32[4,1408]{1,0:T(4,128)S(1)}, u32[]{:S(2)}, u32[]{:S(2)}) collective-permute-start(f32[4,1408]{1,0:T(4,128)S(1)} %get-tuple-element.56), channel_id=1, source_target_pairs={{128,256},{256,384},{129,257},{257,385},{130,258},{258,386},{131,2... | collective-permute-start | bytes 67592 | tf_op jit(solution)/shard_map/ppermute | solution.py:478
  29.0 12.0 %collective-permute-start.1 = (f32[4,1408]{1,0:T(4,128)S(1)}, f32[4,1408]{1,0:T(4,128)S(1)}, u32[]{:S(2)}, u32[]{:S(2)}) collective-permute-start(f32[4,1408]{1,0:T(4,128)S(1)} %get-tuple-element.55), channel_id=1, source_target_pairs={{0,128},{1,129},{2,130},{3,131},{4,132},{5,133},{6,134},{7,135},{8... | collective-permute-start | bytes 67592 | tf_op jit(solution)/shard_map/ppermute | solution.py:478
  37.6 4.3 %collective-permute-start.3 = (f32[4,1408]{1,0:T(4,128)S(1)}, f32[4,1408]{1,0:T(4,128)S(1)}, u32[]{:S(2)}, u32[]{:S(2)}) collective-permute-start(f32[4,1408]{1,0:T(4,128)S(1)} %get-tuple-element.62), channel_id=1, source_target_pairs={{0,256},{128,384},{1,257},{129,385},{2,258},{130,386},{3,259},{131... | collective-permute-start | bytes 67592 | tf_op jit(solution)/shard_map/ppermute | solution.py:478

commit v14 on v11

--- a/solution.py
+++ b/solution.py
@@ -63,8 +63,8 @@
     ]
     for k, (source, target) in enumerate(zip(sources, targets)):
         copies.append(pltpu.make_async_copy(source, target, sems.at[k + 2]))
-    for copy in copies:
-        copy.start()
+    for k, copy in enumerate(copies):
+        copy.start(priority=1 if k < 2 else 0)
     for copy in copies:
         copy.wait()
 
@@ -128,14 +128,14 @@
 
 
 def prepare_kernel(*refs):
-    count = 6
-    sources, (docs_ref, raw_ref, bias_ref, rate_ref, _) = refs[:count], refs[count : count + 5]
-    targets = refs[count + 5 : 2 * count + 5]
+    count, given = 5, 6
+    sources, targets = refs[:count], refs[count + given : 2 * count + given]
+    x_ref, docs_ref, raw_ref, bias_ref, rate_ref, _ = refs[count : count + given]
+    b_ref, taps_ref, taps_bias_ref, _, _ = targets
     (
         weighted_ref, cum_rows_ref, step_rows_ref, columns_ref, factor_ref, start_ref, b_conv_ref,
         stack_ref, padded_ref, sems,
-    ) = refs[2 * count + 5 :]
-    x_ref, b_ref, _, taps_ref, taps_bias_ref, _ = targets
+    ) = refs[2 * count + given :]
     copies = [
         pltpu.make_async_copy(source, target, sems.at[k])
         for k, (source, target) in enumerate(zip(sources, targets))
@@ -180,8 +180,6 @@
     columns = stack_ref[...].T
     columns_ref[...] = columns
     factor_ref[...] = jnp.where(end_start < 0, jnp.exp(columns[tokens - 1 : tokens, :]), 0.0)
-    for copy in copies:
-        copy.wait()
     weights = columns.astype(jnp.bfloat16)
     for j in range(0, x_ref.shape[1], 256):
         tile = slice(j, j + 256)
@@ -190,6 +188,8 @@
             preferred_element_type=jnp.float32,
         )
         weighted_ref[:, tile] = (x_ref[:, tile].astype(jnp.float32) * spread).astype(jnp.bfloat16)
+    for copy in copies:
+        copy.wait()
     side = slice(0, state)
     padded_ref[0:8, :] = jnp.zeros((8, state), jnp.float32)
     padded_ref[8:, :] = b_ref[...].astype(jnp.float32)
@@ -413,10 +413,11 @@
         [out((8, 2 * state), bf16)] + [out(o.shape, o.dtype) for o in small],
         b_source, c_source, *small,
         hbm=2 + len(small), scratch=[pltpu.SemaphoreType.DMA((2 + len(small),))],
+        flops=20_000_000_000,
     )
     halo = lax.ppermute(tails, SEQ, ahead(shards, 1))
     operands = [
-        inputs, b_source, c_source, conv_weight, conv_bias[None, :],
+        b_source, conv_weight, conv_bias[None, :], c_source,
         norm_gain.reshape(features // LANES, LANES),
     ]
     results = call(
@@ -427,7 +428,7 @@
             out((tokens, LANES)), out((1, LANES)), out((tokens, LANES), jnp.int32),
             out((tokens, state)),
         ],
-        *operands, *small, tails,
+        *operands, inputs, *small, tails,
         hbm=len(operands),
         scratch=[
             pltpu.VMEM((LANES, tokens), jnp.float32),
@@ -435,8 +436,8 @@
             pltpu.SemaphoreType.DMA((len(operands),)),
         ],
     )
-    x, b, c, taps, taps_bias, gain = results[0:6]
-    weighted, cum_rows, step_rows, columns, factor, start, b_early = results[6:]
+    b, taps, taps_bias, c, gain = results[0:5]
+    weighted, cum_rows, step_rows, columns, factor, start, b_early = results[5:]
     pieces, b_conv = call(
         states_kernel,
         [out((members, rows, features + LANES)), out((tokens, state), bf16)],
@@ -457,7 +458,7 @@
 
     def diagonal_terms(turn, token, *before):
         sources = [
-            c, halo, taps, taps_bias, start, b_conv, columns, cum_rows, step_rows, x, gate_input,
+            c, halo, taps, taps_bias, start, b_conv, columns, cum_rows, step_rows, inputs, gate_input,
             factors,
         ]
         token = [] if token is None else [token]

time: 75.3 us -> 75.1 us (level)
  transfers between devices with their start and end apart: 4 -> 4, of which waited for: 1 -> 1; matrix products, arithmetic and copies ran while one was open for 0% -> 0% of each run, Pallas kernels for 5% -> 4%
where the time goes in v14:
time: 75.1 us; the launch traced here: 74.8 us
  blocking collectives  50.6 us (67%)
  starting transfers between devices  16.5 us (22%)
  Pallas kernels  6.59 us (9%)
  waiting for transfers between devices  0.87 us (1%)
    all_to_all x1, blocking collectives, body(): pieces = lax.all_to_all(pieces, GROUP, 0, 0)  18.7 us
    all_gather x1, blocking collectives, body(): squares = lax.all_gather(squares, 'tp')  18.4 us
    all_to_all x1, blocking collectives, body(): states_in = lax.all_to_all(states_in, GROUP, 0, 0)  13.6 us
    ppermute x3, starting transfers between devices, send(): return lax.ppermute(total, OUTER, pairs)  12.6 us
    pallas_call x10, Pallas kernels, call(): pl.pallas_call(kernel, out_shape=list(outs) if multiple else outs, in_spe...  6.59 us
    ppermute x1, starting transfers between devices, body(): halo = lax.ppermute(tails, SEQ, ahead(shards, 1))  3.93 us
  transfers between devices with their start and end apart: 4, of which 1 were waited for; matrix products, arithmetic and copies ran while one was open for 0% of the time, Pallas kernels for 4%

profile of v14, /device:TPU:1, one launch (start us, length us, event | category | flops | bytes accessed | tf_op | source)
XLA Modules:
  0.0 74.8 jit_solution(1446845943371643278)
XLA Ops:
  0.0 0.0 copy-start
  0.0 0.9 %shard_map.109 = (bf16[8,256]{1,0:T(8,128)(2,1)S(1)}, s32[1,8]{1,0:T(1,128)S(1)}, f32[20,256]{1,0:T(8,128)S(1)}, f32[1,20]{1,0:T(1,128)S(1)}, f32[1,20]{1,0:T(1,128)S(1)}) custom-call(bf16[256,128]{1,0:T(8,128)(2,1)} %refs_0_.1, bf16[256,128]{1,0:T(8,128)(2,1)} %refs_3_.1, s32[1,8]{1,0:T(1,128)} %bitcast.11, f32[20,256]{1,0:T(8,128)} %bitcast.10, ...), custom_call_target="tpu_custom_call" | custom-call | flops 20000000000 | bytes 1000000 | tf_op jit(solution)/shard_map/pallas_call | solution.py:27
  0.9 3.9 %collective-permute-start = (bf16[8,256]{1,0:T(8,128)(2,1)S(1)}, bf16[8,256]{1,0:T(8,128)(2,1)S(1)}, u32[]{:S(2)}, u32[]{:S(2)}) collective-permute-start(bf16[8,256]{1,0:T(8,128)(2,1)S(1)} %get-tuple-element.49.refs_10_), channel_id=1, source_target_pairs={{0,4},{4,8},{8,12},{12,16},{16,20},{20,24},{24,28},{28,32},{32,36}... | collective-permute-start | bytes 12296 | tf_op jit(solution)/shard_map/ppermute | solution.py:418
  4.8 0.0 copy-done
  4.8 1.2 %shard_map.110 = (bf16[256,128]{1,0:T(8,128)(2,1)S(1)}, f32[4,256]{1,0:T(4,128)S(1)}, f32[1,256]{1,0:T(1,128)S(1)}, bf16[256,128]{1,0:T(8,128)(2,1)S(1)}, f32[10...) custom-call(bf16[256,128]{1,0:T(8,128)(2,1)} %refs_0_.1, ...), custom_call_target="tpu_custom_call" | custom-call | flops 1000000 | bytes 1000000 | tf_op jit(solution)/shard_map/pallas_call | solution.py:27
  6.1 0.0 collective-permute-done.halo_ref.refs_1_
  6.1 0.3 shard_map.111
  6.4 0.0 copy-start.1
  6.4 18.7 %all_to_all.10.pieces_ref = f32[32,4,1408]{2,1,0:T(4,128)S(1)} all-to-all(f32[32,4,1408]{2,1,0:T(4,128)S(1)} %get-tuple-element.62), channel_id=1, replica_groups=mesh['za'=4,'zb'=2,'y'=4,'x'=4,'tp'=4] {'zb','y','x'}, dimensions={0} | all-to-all | bytes 1441792 | tf_op jit(solution)/shard_map/all_to_all | solution.py:447
  25.2 0.4 shard_map.112
  25.6 0.7 collective-permute-start.2
  26.2 0.0 copy-done.1
  26.2 1.8 %shard_map.113 = (f32[4,1408]{1,0:T(4,128)S(1)}, f32[32,1280]{1,0:T(8,128)S(1)}, bf16[256,128]{1,0:T(8,128)(2,1)S(1)}, f32[256,1280]{1,0:T(8,128)S(1)}, f32[256,1280]{1,0:T(8,128)S(1)}) custom-call(bf16[256,128]{1,0:T(8,128)(2,1)S(1)} %get-tuple-element.50.refs_0_, ...), custom_call_target="tpu_custom_call", output_to_operand_aliasing={{0}: (12, {})} | custom-call | flops 20000000000 | bytes 1000000 | tf_op jit(solution)/shard_map/pallas_call | solution.py:27
  28.1 9.2 %collective-permute-start.1 = (f32[4,1408]{1,0:T(4,128)S(1)}, f32[4,1408]{1,0:T(4,128)S(1)}, u32[]{:S(2)}, u32[]{:S(2)}) collective-permute-start(f32[4,1408]{1,0:T(4,128)S(1)} %get-tuple-element.65), channel_id=1, source_target_pairs={{0,128},{1,129},{2,130},{3,131},{4,132},{5,133},{6,134},{7,135},{8... | collective-permute-start | bytes 67592 | tf_op jit(solution)/shard_map/ppermute | solution.py:481
  37.3 2.7 %collective-permute-start.3 = (f32[4,1408]{1,0:T(4,128)S(1)}, f32[4,1408]{1,0:T(4,128)S(1)}, u32[]{:S(2)}, u32[]{:S(2)}) collective-permute-start(f32[4,1408]{1,0:T(4,128)S(1)} %get-tuple-element.72), channel_id=1, source_target_pairs={{0,256},{128,384},{1,257},{129,385},{2,258},{130,386},{3,259},{131... | collective-permute-start | bytes 67592 | tf_op jit(solution)/shard_map/ppermute | solution.py:481
  40.1 0.0 collective-permute-done.2.refs_1_
  40.1 0.0 collective-permute-done.1.refs_0_
  40.1 0.9 %collective-permute-done.3.refs_2_ = f32[4,1408]{1,0:T(4,128)S(1)} collective-permute-done((f32[4,1408]{1,0:T(4,128)S(1)}, f32[4,1408]{1,0:T(4,128)S(1)}, u32[]{:S(2)}, u32[]{:S(2)}) %collective-permute-start.3) | collective-permute-done | bytes 22560 | tf_op jit(solution)/shard_map/ppermute | solution.py:481
  40.9 0.3 shard_map.116
  41.2 13.6 %all_to_all.11.state_ref = bf16[32,4,1280]{2,1,0:T(4,128)(2,1)S(1)} all-to-all(bf16[32,4,1280]{2,1,0:T(4,128)(2,1)S(1)} %shard_map.116), channel_id=1, replica_groups=mesh['za'=4,'zb'=2,'y'=4,'x'=4,'tp'=4] {'zb','y','x'}, dimensions={0} | all-to-all | bytes 655360 | tf_op jit(solution)/shard_map/all_to_all | solution.py:495
  54.8 0.6 shard_map.117
  55.4 18.4 %all-gather.1.squares_ref = f32[4,1,256]{2,1,0:T(1,128)S(1)} all-gather(f32[1,1,256]{2,1,0:T(1,128)S(1)} %bitcast.7), channel_id=2, replica_groups=mesh['za'=4,'zb'=2,'y'=4,'x'=4,'tp'=4] {'tp'}, dimensions={0}, use_global_device_ids=true | all-gather | bytes 5120 | tf_op jit(solution)/shard_map/all_gather | solution.py:501
  73.8 1.0 %shard_map.118 = bf16[256,1280]{1,0:T(8,128)(2,1)} custom-call(f32[4,1,256]{2,1,0:T(1,128)S(1)} %all-gather.1.squares_ref, f32[256,1280]{1,0:T(8,128)S(1)} %get-tuple-element.83.gated_ref, f32[10,128]{1,0:T(8,128)S(1)} %get-tuple-element.84.gain_ref), custom_call_target="tpu_custom_call" | custom-call | flops 1000000 | bytes 1000000 | tf_op jit(solution)/shard_map/pallas_call | solution.py:27
  (2 shorter events, 0.0 us)
Async XLA Ops:
  0.0 4.8 %copy-start = (bf16[256,1280]{1,0:T(8,128)(2,1)S(1)}, bf16[256,1280]{1,0:T(8,128)(2,1)}, u32[]{:S(2)}) copy-start(bf16[256,1280]{1,0:T(8,128)(2,1)} %refs_9_.5) | copy-start | bytes 1966084
  0.9 5.2 %collective-permute-start = (bf16[8,256]{1,0:T(8,128)(2,1)S(1)}, bf16[8,256]{1,0:T(8,128)(2,1)S(1)}, u32[]{:S(2)}, u32[]{:S(2)}) collective-permute-start(bf16[8,256]{1,0:T(8,128)(2,1)S(1)} %get-tuple-element.49.refs_10_), channel_id=1, source_target_pairs={{0,4},{4,8},{8,12},{12,16},{16,20},{20,24},{24,28},{28,32},{32,36}... | collective-permute-start | bytes 12296 | tf_op jit(solution)/shard_map/ppermute | solution.py:418
  6.4 19.8 %copy-start.1 = (bf16[256,1280]{1,0:T(8,128)(2,1)S(1)}, bf16[256,1280]{1,0:T(8,128)(2,1)}, u32[]{:S(2)}) copy-start(bf16[256,1280]{1,0:T(8,128)(2,1)} %refs_10_.5) | copy-start | bytes 1966084
  25.6 14.5 %collective-permute-start.2 = (f32[4,1408]{1,0:T(4,128)S(1)}, f32[4,1408]{1,0:T(4,128)S(1)}, u32[]{:S(2)}, u32[]{:S(2)}) collective-permute-start(f32[4,1408]{1,0:T(4,128)S(1)} %get-tuple-element.66), channel_id=1, source_target_pairs={{128,256},{256,384},{129,257},{257,385},{130,258},{258,386},{131,2... | collective-permute-start | bytes 67592 | tf_op jit(solution)/shard_map/ppermute | solution.py:481
  28.1 12.0 %collective-permute-start.1 = (f32[4,1408]{1,0:T(4,128)S(1)}, f32[4,1408]{1,0:T(4,128)S(1)}, u32[]{:S(2)}, u32[]{:S(2)}) collective-permute-start(f32[4,1408]{1,0:T(4,128)S(1)} %get-tuple-element.65), channel_id=1, source_target_pairs={{0,128},{1,129},{2,130},{3,131},{4,132},{5,133},{6,134},{7,135},{8... | collective-permute-start | bytes 67592 | tf_op jit(solution)/shard_map/ppermute | solution.py:481
  37.3 3.6 %collective-permute-start.3 = (f32[4,1408]{1,0:T(4,128)S(1)}, f32[4,1408]{1,0:T(4,128)S(1)}, u32[]{:S(2)}, u32[]{:S(2)}) collective-permute-start(f32[4,1408]{1,0:T(4,128)S(1)} %get-tuple-element.72), channel_id=1, source_target_pairs={{0,256},{128,384},{1,257},{129,385},{2,258},{130,386},{3,259},{131... | collective-permute-start | bytes 67592 | tf_op jit(solution)/shard_map/ppermute | solution.py:481
